TPU v7x, 256 devices: a 2x2x32 block of a 4x8x32 slice. The times are simulated.
256 devices in a mesh: groups: 4 (over y, x), seq: 32 (over z), batch: 2 (over core).
Axes of the slice: x: 2, y: 2, z: 32, core: 2. Of those that a mesh axis runs over, the one named last changes fastest.
The devices are a block of a 4x8x32 slice.
Arguments:
- prompt_cache: bfloat16 [32, 1024, 8, 256], P(('groups', 'batch'), 'seq'), parts along dimension 0, may hold values from -6 to 6
- prompt_states: float32 [32, 32, 16, 16384], P(('groups', 'batch'), 'seq'), parts along dimension 0, may hold values from -6 to 6
- block_steps: float32 [32, 32, 16384], P(('groups', 'batch'), 'seq'), parts along dimension 0, may hold values from 0.005 to 0.1
- prompt_lengths: int32 [32], P('groups'), parts along dimension 0, may hold values from 170 to 1023
- target_slots: int32 [32], P('groups'), parts along dimension 0, may hold values from 0 to 15, as said below
- cache_lengths: int32 [64], P(('groups', 'batch')), parts along dimension 0, may hold values from 170 to 1023
- resident_cache: bfloat16 [64, 32, 32, 8, 256], P(('groups', 'batch'), None, 'seq'), parts along dimension 0, may hold values from -6 to 6
- token_cache: bfloat16 [64, 8, 256], P(('groups', 'batch')), parts along dimension 0, may hold values from -6 to 6
- queries: bfloat16 [64, 64, 128], P(('groups', 'batch')), parts along dimension 0, may hold values from -6 to 6
- resident_states: float32 [64, 16, 16384], P(('groups', 'batch'), None, 'seq'), parts along dimension 0, may hold values from -6 to 6
- decay_rates: float32 [16, 16384], replicated, may hold values from 0.05 to 10
- step_sizes: float32 [64, 16384], P(('groups', 'batch'), 'seq'), parts along dimension 0, may hold values from 0.01 to 1
- inner_input: bfloat16 [64, 16384], P(('groups', 'batch'), 'seq'), parts along dimension 0, may hold values from -6 to 6
- inner_gate: bfloat16 [64, 16384], P(('groups', 'batch'), 'seq'), parts along dimension 0, may hold values from -6 to 6
- state_input: float32 [64, 16], P(('groups', 'batch')), parts along dimension 0, may hold values from -6 to 6
- state_readout: float32 [64, 16], P(('groups', 'batch')), parts along dimension 0, may hold values from -6 to 6
- skip_gain: float32 [16384], P('seq'), may hold values from 0.5 to 1.5
Outputs:
- merged_cache: bfloat16 [64, 32, 32, 8, 256], P(('groups', 'batch'), None, 'seq'), parts along dimension 0
- attention: bfloat16 [64, 64, 128], P(('groups', 'batch'), 'seq'), parts along dimension 0
- next_states: float32 [64, 16, 16384], P(('groups', 'batch'), None, 'seq'), parts along dimension 0
- mamba_output: bfloat16 [64, 16384], P(('groups', 'batch'), 'seq'), parts along dimension 0
There are 4 independent parts, one for each index of `groups`. A program takes and returns all parts, laid end to end along the dimension named above; an argument that names none is the same for every part. Nothing has to cross between parts.
Inputs may be any that keep to these rules, and one draw needn't show every extreme that they name: `target_slots`: 8 distinct slots.
All inputs are finite; a program needn't handle non-finite values.
Results may differ from a plain program's by a relative error of at most 0.0019.
Values may be sent and summed in bfloat16 or wider, within the bound.
No kernel may reach another device: no remote copies, remote signals or barrier semaphores. Data moves between devices by JAX's collectives and lax.ppermute only.
A program may use at most 320 MiB of HBM per device.

v0:
```python
import math

import jax
import jax.numpy as jnp
from jax import lax
from jax.sharding import PartitionSpec as P


def carried_in(shard, axis, combine, identity):
    count, position = (lax.axis_size(axis), lax.axis_index(axis))
    everything = lax.all_gather(shard, axis)
    start = jnp.broadcast_to(jnp.asarray(identity, shard.dtype), shard.shape)

    def step(k, before):
        at = count - 1 - k
        reached = at > position
        new = combine(before, everything[at])
        return jnp.where(reached, new, before)

    return lax.fori_loop(0, count, step, start)


def sent_to_all(shard, axis):
    count = lax.axis_size(axis)
    return lax.all_to_all(
        jnp.broadcast_to(shard[None], (count, *shard.shape)), axis, 0, 0, tiled=True
    )


def joined_along(pieces, dim):
    pieces = jnp.moveaxis(pieces, 0, dim)
    lengths = pieces.shape
    return pieces.reshape(*lengths[:dim], lengths[dim] * lengths[dim + 1], *lengths[dim + 2 :])


def gather_directly(shard, axis, dim):
    pieces = sent_to_all(shard, axis)
    return joined_along(pieces, dim)


def add_terms(earlier, latter):
    return earlier + latter


def to_cyclic(blocks, seq_count):
    count, length, heads, width = blocks.shape
    return blocks.reshape(count, length // seq_count, seq_count, heads, width)


def block_usable(lengths, seq_index, block_len):
    return (seq_index * block_len < lengths).astype(jnp.float32)


def decay_term(states, behind, usable, rates):
    return usable[:, None, None] * jnp.exp(-rates[None] * behind[:, None, :]) * states


def local(
    prompt_cache,
    prompt_states,
    block_steps,
    prompt_lengths,
    target_slots,
    cache_lengths,
    resident_cache,
    token_cache,
    queries,
    resident_states,
    decay_rates,
    step_sizes,
    inner_input,
    inner_gate,
    state_input,
    state_readout,
    skip_gain,
):
    seq_count = lax.axis_size("seq")
    seq_index = lax.axis_index("seq")
    batch_index = lax.axis_index("batch")
    local_prompts, block_len, kv_heads, kv_width = prompt_cache.shape
    head_dim = kv_width // 2
    requests = resident_cache.shape[0]
    channels = decay_rates.shape[1]
    local_channels = channels // seq_count
    own_lengths = lax.dynamic_slice_in_dim(
        prompt_lengths, batch_index * local_prompts, local_prompts
    )
    usable = block_usable(own_lengths, seq_index, block_len)
    moved = lax.all_to_all(
        to_cyclic(prompt_cache, seq_count), "seq", split_axis=2, concat_axis=1, tiled=True
    )
    step_terms = block_steps[:, 0, :] * usable[:, None]
    behind = carried_in(step_terms, "seq", add_terms, jnp.zeros_like(step_terms))
    handed_share = lax.psum_scatter(
        decay_term(prompt_states[:, 0], behind, usable, decay_rates),
        "seq",
        scatter_dimension=2,
        tiled=True,
    )
    arrived = lax.all_gather(moved[:, :, 0], "batch", axis=0, tiled=True)
    handed = gather_directly(handed_share, "batch", 0)
    prompt_count = arrived.shape[0]
    slot_ids = batch_index * requests + jnp.arange(requests, dtype=jnp.int32)
    matches = target_slots[None, :] == slot_ids[:, None]
    fresh = jnp.any(matches, axis=1)
    chosen_len = jnp.sum(jnp.where(matches, prompt_lengths[None, :], 0), axis=1)
    lengths = jnp.where(fresh, chosen_len, cache_lengths)
    picked = jnp.dot(
        matches.astype(jnp.bfloat16),
        arrived.reshape(prompt_count, -1),
        preferred_element_type=jnp.float32,
    )
    picked = picked.astype(jnp.bfloat16).reshape(requests, block_len, kv_heads, kv_width)
    position = jnp.arange(block_len, dtype=jnp.int32) * seq_count + seq_index
    merged = jnp.where(fresh[:, None, None, None], picked, resident_cache[:, :, 0])
    merged = jnp.where(
        (position[None, :] < lengths[:, None])[:, :, None, None],
        merged,
        jnp.zeros((), jnp.bfloat16),
    )
    merged = jnp.where(
        (position[None, :] == lengths[:, None])[:, :, None, None], token_cache[:, None], merged
    )
    heads = queries.shape[1]
    group = heads // kv_heads
    grouped = queries.reshape(requests, kv_heads, group, head_dim)
    scores = jnp.einsum(
        "rgqd,rtgd->rgqt", grouped, merged[..., :head_dim], preferred_element_type=jnp.float32
    ) * (1.0 / math.sqrt(head_dim))
    seen = (position[None, :] <= lengths[:, None])[:, None, None, :]
    masked = jnp.where(seen, scores, -1e30)
    highest = jnp.max(masked, axis=3)
    weights = jnp.where(seen, jnp.exp(masked - highest[..., None]), 0.0)
    denominator = jnp.sum(weights, axis=3)
    summed = jnp.einsum(
        "rgqt,rtgd->rgqd",
        weights.astype(jnp.bfloat16),
        merged[..., head_dim:],
        preferred_element_type=jnp.float32,
    )
    highest = highest.reshape(requests, heads)
    denominator = denominator.reshape(requests, heads)
    summed = summed.reshape(requests, heads, head_dim)
    peer_top, peer_total, peer_sum = (
        lax.all_to_all(highest[:, None], "seq", split_axis=2, concat_axis=1, tiled=True),
        lax.all_to_all(denominator[:, None], "seq", split_axis=2, concat_axis=1, tiled=True),
        lax.all_to_all(summed[:, None], "seq", split_axis=2, concat_axis=1, tiled=True),
    )
    common_top = jnp.max(peer_top, axis=1)
    factor = jnp.exp(peer_top - common_top[:, None])
    owner_total = jnp.sum(peer_total * factor, axis=1)
    owner_sum = jnp.sum(peer_sum * factor[..., None], axis=1)
    attention = (owner_sum / owner_total[..., None]).astype(jnp.bfloat16)
    rates_here = lax.dynamic_slice_in_dim(
        decay_rates, seq_index * local_channels, local_channels, 1
    )
    chosen_state = jnp.einsum(
        "rp,pnc->rnc", matches.astype(jnp.float32), handed, precision=lax.Precision.HIGHEST
    )
    start = jnp.where(fresh[:, None, None], chosen_state, resident_states)
    inner = inner_input.astype(jnp.float32)
    next_states = (
        jnp.exp(-rates_here[None] * step_sizes[:, None, :]) * start
        + (step_sizes * inner)[:, None, :] * state_input[:, :, None]
    )
    readout = jnp.sum(state_readout[:, :, None] * next_states, axis=1) + skip_gain[None, :] * inner
    mamba_output = (readout * jax.nn.silu(inner_gate.astype(jnp.float32))).astype(jnp.bfloat16)
    return (merged[:, :, None], attention, next_states, mamba_output)


def solution(mesh):
    return jax.shard_map(
        local,
        mesh=mesh,
        in_specs=(
            P(("groups", "batch"), "seq", None, None),
            P(("groups", "batch"), "seq", None, None),
            P(("groups", "batch"), "seq", None),
            P("groups"),
            P("groups"),
            P(("groups", "batch")),
            P(("groups", "batch"), None, "seq", None, None),
            P(("groups", "batch"), None, None),
            P(("groups", "batch"), None, None),
            P(("groups", "batch"), None, "seq"),
            P(),
            P(("groups", "batch"), "seq"),
            P(("groups", "batch"), "seq"),
            P(("groups", "batch"), "seq"),
            P(("groups", "batch"), None),
            P(("groups", "batch"), None),
            P("seq"),
        ),
        out_specs=(
            P(("groups", "batch"), None, "seq", None, None),
            P(("groups", "batch"), "seq", None),
            P(("groups", "batch"), None, "seq"),
            P(("groups", "batch"), "seq"),
        ),
        check_vma=False,
    )
```

profile of v0, /device:TPU:109, one launch (start us, length us, event | category | flops | bytes accessed | tf_op | source)
XLA Modules:
  0.0 421.4 jit_solution(6203049172755790283)
XLA Ops:
  8.0 1.8 bitcast_multiply_fusion.1
  9.9 1.9 copy.82
  11.8 31.3 %all-to-all-start = ((bf16[4,1,32,8,256]{4,3,0,1,2:T(8,128)(2,1)}), bf16[4,1,32,8,256]{4,3,0,1,2:T(8,128)(2,1)S(1)}, u32[]{:S(2)}, u32[]{:S(2)}) async-start(bf16[4,1,32,8,256]{4,3,0,1,2:T(8,128)(2,1)} %bitcast.42), calls=%async_computation | async-start | bytes 1048576 | tf_op jit(solution)/shard_map/all_to_all | solution.py:89
  44.5 65.8 %all-to-all-done = bf16[4,1,32,8,256]{4,3,0,1,2:T(8,128)(2,1)S(1)} async-done(((bf16[4,1,32,8,256]{4,3,0,1,2:T(8,128)(2,1)}), bf16[4,1,32,8,256]{4,3,0,1,2:T(8,128)(2,1)S(1)}, u32[]{:S(2)}, u32[]{:S(2)}) %all-to-all-start) | async-done | bytes 524320 | tf_op jit(solution)/shard_map/all_to_all | solution.py:89
  111.2 82.3 %all-gather.4.cloned.1.call-done = f32[32,4,16384]{2,1,0:T(4,128)} async-done(((f32[1,4,16384]{2,1,0:T(4,128)}), f32[32,4,16384]{2,1,0:T(4,128)}) %all-gather.4.cloned.1.call-update) | async-done | bytes 8388624 | tf_op jit(solution)/shard_map/all_gather | solution.py:11
  193.5 42.3 %while.16 = (s32[]{:T(128)}, f32[4,16384]{1,0:T(4,128)S(1)}, s32[]{:T(128)}, f32[32,4,16384]{2,1,0:T(4,128)}, s32[]{:T(128)}, /*index=5*/s32[]{:T(128)}, s32[]{:T(128)}, s32[]{:T(128)}) while((s32[]{:T(128)}, f32[4,16384]{1,0:T(4,128)S(1)}, s32[]{:T(128)}, f32[32,4,16384]{2,1,0:T(4,128)}, s32[]{:T(128)}, /*index=5*/s32[]{:T(128)}, ...), condition=%wide.region_8.9_spmd.clone, body=%wide.region_7.8_spmd.clone.sunk | while | flops 196616 | bytes 786595 | solution.py:20
  194.8 1.3 add_select_fusion.2
  198.8 1.3 add_select_fusion.2
  227.8 1.3 add_select_fusion.2
  229.2 1.3 add_select_fusion.2
  235.8 4.9 %bitcast_multiply_fusion = f32[4,16,16384]{2,1,0:T(8,128)} fusion(f32[4,1,16,16384]{3,2,1,0:T(8,128)} %param.20, f32[4,16384]{1,0:T(4,128)S(1)} %get-tuple-element.114, f32[16,16384]{1,0:T(8,128)S(1)} %neg.13, f32[4]{0:T(128)S(1)} %compare_convert_fusion), kind=kLoop, calls=%fused_computation.2 | loop fusion | flops 3145728 | bytes 9699344 | tf_op jit(solution)/shard_map/mul | solution.py:55
  242.4 1.8 copy.71
  244.7 1.4 fusion.5
  248.1 1.4 copy.69
  249.6 13.5 %all-to-all-start.3 = ((f32[8,1,64]{0,1,2:T(1,128)}), f32[8,1,64]{0,1,2:T(1,128)}, u32[]{:S(2)}, u32[]{:S(2)}) async-start(f32[8,1,64]{0,1,2:T(1,128)} %bitcast.51), calls=%async_computation.3 | async-start | bytes 65536 | tf_op jit(solution)/shard_map/all_to_all | solution.py:146
  263.1 1.4 copy.60
  264.6 19.4 %all-to-all-done.3 = f32[8,1,64]{0,1,2:T(1,128)} async-done(((f32[8,1,64]{0,1,2:T(1,128)}), f32[8,1,64]{0,1,2:T(1,128)}, u32[]{:S(2)}, u32[]{:S(2)}) %all-to-all-start.3) | async-done | bytes 2080 | tf_op jit(solution)/shard_map/all_to_all | solution.py:146
  284.0 5.6 %all-to-all-start.2 = ((f32[8,1,64]{0,1,2:T(1,128)}), f32[8,1,64]{0,1,2:T(1,128)}, u32[]{:S(2)}, u32[]{:S(2)}) async-start(f32[8,1,64]{0,1,2:T(1,128)} %bitcast.50), calls=%async_computation.2 | async-start | bytes 65536 | tf_op jit(solution)/shard_map/all_to_all | solution.py:145
  291.6 18.9 %all-to-all-done.2 = f32[8,1,64]{0,1,2:T(1,128)} async-done(((f32[8,1,64]{0,1,2:T(1,128)}), f32[8,1,64]{0,1,2:T(1,128)}, u32[]{:S(2)}, u32[]{:S(2)}) %all-to-all-start.2) | async-done | bytes 2080 | tf_op jit(solution)/shard_map/all_to_all | solution.py:145
  310.4 5.3 %all-to-all-start.1 = ((f32[8,1,64,128]{3,0,1,2:T(8,128)}), f32[8,1,64,128]{3,0,1,2:T(8,128)S(1)}, u32[]{:S(2)}, u32[]{:S(2)}) async-start(f32[8,1,64,128]{3,0,1,2:T(8,128)} %copy.59), calls=%async_computation.1 | async-start | bytes 524288 | tf_op jit(solution)/shard_map/all_to_all | solution.py:147
  318.7 2.3 fusion.7
  322.7 26.6 %all-to-all-done.1 = f32[8,1,64,128]{3,0,1,2:T(8,128)S(1)} async-done(((f32[8,1,64,128]{3,0,1,2:T(8,128)}), f32[8,1,64,128]{3,0,1,2:T(8,128)S(1)}, u32[]{:S(2)}, u32[]{:S(2)}) %all-to-all-start.1) | async-done | bytes 262176 | tf_op jit(solution)/shard_map/all_to_all | solution.py:147
  350.1 39.6 %reduce-scatter.2.cloned.1.call-done = f32[4,16,512]{2,1,0:T(8,128)} async-done(((f32[4,16,16384]{2,1,0:T(8,128)}), f32[4,16,512]{2,1,0:T(8,128)}) %reduce-scatter.2.cloned.1.call-update) | async-done | bytes 131088 | tf_op jit(solution)/shard_map/reduce_scatter | solution.py:94
  390.7 22.0 %all_to_all.50 = f32[2,4,16,512]{3,1,2,0:T(4,128)S(1)} all-to-all(f32[2,4,16,512]{3,1,2,0:T(4,128)S(1)} %broadcast_in_dim.143), channel_id=1, replica_groups=mesh['groups'=4,'seq'=32,'batch'=2] {'batch'}, dimensions={0} | all-to-all | bytes 524288 | tf_op jit(solution)/shard_map/all_to_all | solution.py:25
  (106 shorter events, 54.3 us)
Async XLA Ops:
  7.2 239.0 %copy-start = (bf16[8,64,128]{2,1,0:T(8,128)(2,1)S(1)}, bf16[8,64,128]{2,1,0:T(8,128)(2,1)}, u32[]{:S(2)}) copy-start(bf16[8,64,128]{2,1,0:T(8,128)(2,1)} %param.27) | copy-start | bytes 393220
  7.2 186.3 %all-gather.4.cloned.1.call-start = ((), (), s32[]{:S(2)}) async-start(), calls=%async_computation.6 | async-start | bytes 8650752 | tf_op jit(solution)/shard_map/all_gather | solution.py:11
  11.8 98.5 %all-to-all-start = ((bf16[4,1,32,8,256]{4,3,0,1,2:T(8,128)(2,1)}), bf16[4,1,32,8,256]{4,3,0,1,2:T(8,128)(2,1)S(1)}, u32[]{:S(2)}, u32[]{:S(2)}) async-start(bf16[4,1,32,8,256]{4,3,0,1,2:T(8,128)(2,1)} %bitcast.42), calls=%async_computation | async-start | bytes 1048576 | tf_op jit(solution)/shard_map/all_to_all | solution.py:89
  43.1 199.2 %all-gather.6.cloned.1.call-start = ((), (), s32[]{:S(2)}) async-start(), calls=%async_computation.8 | async-start | bytes 1572864 | tf_op jit(solution)/shard_map/all_gather | solution.py:100
  111.2 278.5 %reduce-scatter.2.cloned.1.call-start = ((), (), s32[]{:S(2)}) async-start(), calls=%async_computation.7 | async-start | bytes 4325376 | tf_op jit(solution)/shard_map/reduce_scatter | solution.py:94
  240.6 1.0 copy-start.19
  240.6 4.0 copy-start.1
  240.7 4.0 copy-start.4
  241.3 4.8 %copy-start.15 = (s32[8]{0:T(128)}, s32[8]{0:T(128)S(1)}, u32[]{:S(2)}) copy-start(s32[8]{0:T(128)S(1)} %iota_add_fusion) | copy-start | bytes 100
  241.5 4.6 %copy-start.10 = (pred[8]{0:T(512)(128)(4,1)}, pred[8]{0:T(512)(128)(4,1)S(1)}, u32[]{:S(2)}) copy-start(pred[8]{0:T(512)(128)(4,1)S(1)} %compare_reduce_fusion) | copy-start | bytes 28
  242.3 3.8 copy-start.7
  242.3 3.8 copy-start.8
  242.3 3.8 copy-start.9
  244.2 73.9 %copy-start.5 = (f32[8,512]{1,0:T(8,128)S(1)}, f32[8,512]{1,0:T(8,128)}, u32[]{:S(2)}) copy-start(f32[8,512]{1,0:T(8,128)} %param.30) | copy-start | bytes 49156
  249.6 34.4 %all-to-all-start.3 = ((f32[8,1,64]{0,1,2:T(1,128)}), f32[8,1,64]{0,1,2:T(1,128)}, u32[]{:S(2)}, u32[]{:S(2)}) async-start(f32[8,1,64]{0,1,2:T(1,128)} %bitcast.51), calls=%async_computation.3 | async-start | bytes 65536 | tf_op jit(solution)/shard_map/all_to_all | solution.py:146
  284.0 26.5 %all-to-all-start.2 = ((f32[8,1,64]{0,1,2:T(1,128)}), f32[8,1,64]{0,1,2:T(1,128)}, u32[]{:S(2)}, u32[]{:S(2)}) async-start(f32[8,1,64]{0,1,2:T(1,128)} %bitcast.50), calls=%async_computation.2 | async-start | bytes 65536 | tf_op jit(solution)/shard_map/all_to_all | solution.py:145
  290.6 122.3 %copy-start.3 = (f32[8,16,512]{2,1,0:T(8,128)S(1)}, f32[8,16,512]{2,1,0:T(8,128)}, u32[]{:S(2)}) copy-start(f32[8,16,512]{2,1,0:T(8,128)} %param.28) | copy-start | bytes 786436
  290.6 122.3 %copy-start.11 = (pred[8]{0:T(512)(128)(4,1)S(1)}, pred[8]{0:T(512)(128)(4,1)}, u32[]{:S(2)}) copy-start(pred[8]{0:T(512)(128)(4,1)} %copy-done.10) | copy-start | bytes 28
  290.7 122.3 %copy-start.14 = (s32[8]{0:T(128)S(1)}, s32[8]{0:T(128)}, u32[]{:S(2)}) copy-start(s32[8]{0:T(128)} %param.23) | copy-start | bytes 100
  290.7 122.3 %copy-start.16 = (s32[8]{0:T(128)S(1)}, s32[8]{0:T(128)}, u32[]{:S(2)}) copy-start(s32[8]{0:T(128)} %copy-done.15) | copy-start | bytes 100
  290.7 123.6 %copy-start.6 = (bf16[8,512]{1,0:T(8,128)(2,1)S(1)}, bf16[8,512]{1,0:T(8,128)(2,1)}, u32[]{:S(2)}) copy-start(bf16[8,512]{1,0:T(8,128)(2,1)} %param.31) | copy-start | bytes 24580
  290.7 123.6 %copy-start.12 = (bf16[8,512]{1,0:T(8,128)(2,1)S(1)}, bf16[8,512]{1,0:T(8,128)(2,1)}, u32[]{:S(2)}) copy-start(bf16[8,512]{1,0:T(8,128)(2,1)} %param.32) | copy-start | bytes 24580
  290.7 123.6 %copy-start.18 = (f32[512]{0:T(512)S(1)}, f32[512]{0:T(512)}, u32[]{:S(2)}) copy-start(f32[512]{0:T(512)} %param.35) | copy-start | bytes 6148
  310.4 38.9 %all-to-all-start.1 = ((f32[8,1,64,128]{3,0,1,2:T(8,128)}), f32[8,1,64,128]{3,0,1,2:T(8,128)S(1)}, u32[]{:S(2)}, u32[]{:S(2)}) async-start(f32[8,1,64,128]{3,0,1,2:T(8,128)} %copy.59), calls=%async_computation.1 | async-start | bytes 524288 | tf_op jit(solution)/shard_map/all_to_all | solution.py:147
  (3 other events, 2.1 us)
Sparse Core Ops, SparseCore 0:
  10.4 183.0 all-gather.3
  195.9 35.7 all-gather.5
  240.8 148.8 reduce-scatter.1
where the time goes:
time: 424 us; the launch traced here: 421 us
  waiting for transfers between devices  253 us (60%)
  other arithmetic  60 us (14%)
  starting transfers between devices  56 us (13%)
  blocking collectives  22 us (5%)
  between operations  14.1 us (3%)
  local copies, waits for them, and re-layouts  13.7 us (3%)
    all_gather x1, waiting for transfers between devices, carried_in(): everything = lax.all_gather(shard, axis)  82.3 us
    all_to_all x1, waiting for transfers between devices, local(): lax.all_to_all(to_cyclic(prompt_cache, seq_count), 'seq', split_axis=2, c...  65.8 us
    select_n x32, other arithmetic, step(): return jnp.where(reached, new, before)  41.8 us
    reduce_scatter x1, waiting for transfers between devices, local(): lax.psum_scatter(decay_term(prompt_states[:, 0], behind, usable, decay_ra...  39.6 us
    all_to_all x1, starting transfers between devices, local(): lax.all_to_all(to_cyclic(prompt_cache, seq_count), 'seq', split_axis=2, c...  31.3 us
    all_to_all x1, waiting for transfers between devices, local(): lax.all_to_all(summed[:, None], 'seq', split_axis=2, concat_axis=1, tiled...  26.6 us
    all_to_all x1, blocking collectives, sent_to_all(): lax.all_to_all(jnp.broadcast_to(shard[None], (count, *shard.shape)), axis...  22 us
    all_to_all x1, waiting for transfers between devices, local(): lax.all_to_all(denominator[:, None], 'seq', split_axis=2, concat_axis=1,...  19.4 us
  transfers between devices with their start and end apart: 7, of which 6 were waited for; matrix products, arithmetic and copies ran while one was open for 16% of the time, Pallas kernels for 0%

commit v1 on v0

v1 whole, which is shorter than its diff:
```python
import functools
import math

import jax
import jax.numpy as jnp
from jax import lax
from jax.experimental import pallas as pl
from jax.experimental.pallas import tpu as pltpu
from jax.sharding import PartitionSpec as P


STATE_SCALE = 128.0
HALF_SPLIT = 8193.0
KERNEL_VMEM = 8 * 1024 * 1024


def split_half(value):
    spread = value * HALF_SPLIT
    high = spread - (spread - value)
    return high, value - high


def hop_kernel(
    flags,
    usable,
    up_in,
    down_in,
    up_state,
    up_step,
    up_rate,
    down_state,
    down_step,
    down_rate,
    up_out,
    down_out,
    *,
    initial,
    with_down,
):
    count, state = up_state.shape[0], up_state.shape[1]
    rows = count * state
    first, last, frozen = flags[0] == 1, flags[1] == 1, flags[2] == 1

    @pl.loop(0, count)
    def _(p):
        here = pl.ds(pl.multiple_of(p * state, state), state)
        rest = pl.ds(pl.multiple_of(rows + p * state, state), state)
        there = pl.ds(pl.multiple_of(2 * rows + p * state, state), state)
        wide, narrow = pl.ds(3 * rows + p, 1), pl.ds(3 * rows + count + p, 1)
        use = usable[p]
        own = up_state[p] * (use * STATE_SCALE)
        step = up_step[pl.ds(p, 1), :] * use
        if initial:
            acc, aside, span = own, jnp.zeros_like(own), step
        else:
            came, kept = up_in[here, :] + up_in[rest, :], up_in[there, :]
            acc = jnp.exp(-up_rate[...] * step) * jnp.where(first, 0.0, came) + own
            aside = jnp.where(first, came, kept)
            span = up_in[wide, :] + up_in[narrow, :]
            span = jnp.where(frozen, span, span + step)
        up_out[here, :], up_out[rest, :] = split_half(acc)
        up_out[there, :] = aside
        up_out[wide, :], up_out[narrow, :] = split_half(span)
        if not with_down:
            return
        own = down_state[p] * (use * STATE_SCALE)
        step = down_step[pl.ds(p, 1), :] * use
        if initial:
            acc, aside, span = own, jnp.zeros_like(own), step
        else:
            came, kept = down_in[here, :] + down_in[rest, :], down_in[there, :]
            span = jnp.where(last, 0.0, down_in[wide, :] + down_in[narrow, :])
            acc = jnp.where(last, 0.0, came) + jnp.exp(-down_rate[...] * span) * own
            aside = jnp.where(last, came, kept)
            span = span + step
        down_out[here, :], down_out[rest, :] = split_half(acc)
        down_out[there, :] = aside
        down_out[wide, :], down_out[narrow, :] = split_half(span)


def last_kernel(
    flags, usable, up_in, down_in, own_state, own_step, own_rate, handed
):
    count, state = own_state.shape[0], own_state.shape[1]
    rows = count * state
    first, last, outside = flags[0] == 1, flags[1] == 1, flags[2] == 1
    rate = own_rate[...]

    @pl.loop(0, count)
    def _(p):
        here = pl.ds(pl.multiple_of(p * state, state), state)
        rest = pl.ds(pl.multiple_of(rows + p * state, state), state)
        there = pl.ds(pl.multiple_of(2 * rows + p * state, state), state)
        wide, narrow = pl.ds(3 * rows + p, 1), pl.ds(3 * rows + count + p, 1)
        use = usable[p]
        own = own_state[p] * (use * STATE_SCALE)
        step = own_step[pl.ds(p, 1), :] * use
        came, kept = up_in[here, :] + up_in[rest, :], up_in[there, :]
        newest = jnp.where(first, came, kept)
        earlier = jnp.where(first, 0.0, came)
        span = up_in[wide, :] + up_in[narrow, :]
        came, kept = down_in[here, :] + down_in[rest, :], down_in[there, :]
        oldest = jnp.where(last, came, kept)
        later = jnp.where(last, 0.0, came)
        span_down = jnp.where(last, 0.0, down_in[wide, :] + down_in[narrow, :])
        outer = jnp.where(outside, span, 0.0)
        inner = earlier + jnp.exp(-rate * span) * oldest
        inner = later + jnp.exp(-rate * span_down) * (own + jnp.exp(-rate * step) * inner)
        handed[p] = (newest + jnp.exp(-rate * outer) * inner) * (1.0 / STATE_SCALE)


def smem():
    return pl.BlockSpec(memory_space=pltpu.SMEM)


def vmem():
    return pl.BlockSpec(memory_space=pltpu.VMEM)


def hand_over(states, steps, rates, usable, seq_count, seq_index):
    count, state, channels = states.shape
    width = channels // seq_count
    half = seq_count // 2
    ahead = [(k, (k + 1) % seq_count) for k in range(seq_count)]
    behind = [(k, (k - 1) % seq_count) for k in range(seq_count)]
    rows = 3 * count * state + 2 * count
    payload = jax.ShapeDtypeStruct((rows, width), jnp.float32)

    def fetched(chunk):
        at = chunk * width
        return (
            lax.dynamic_slice_in_dim(states, at, width, 2),
            lax.dynamic_slice_in_dim(steps, at, width, 1),
            lax.dynamic_slice_in_dim(rates, at, width, 1),
        )

    def flags(third):
        return jnp.stack(
            [seq_index == 0, seq_index == seq_count - 1, third]
        ).astype(jnp.int32)

    cost = pl.CostEstimate(
        flops=16 * rows * width, bytes_accessed=16 * rows * width, transcendentals=rows * width
    )
    up = down = jnp.zeros((8, 128), jnp.float32)
    for hop in range(half):
        with jax.named_scope(f"ring_{hop}"):
            with_down = hop < half - 1
            ups = fetched((seq_index + half - hop) % seq_count)
            downs = fetched((seq_index - (half - 1) + hop) % seq_count) if with_down else ups
            operands = (flags(seq_index < hop), usable, up, down, *ups, *downs)
            outs = pl.pallas_call(
                functools.partial(hop_kernel, initial=hop == 0, with_down=with_down)
                if with_down
                else functools.partial(
                    lambda *refs, **kw: hop_kernel(*refs, None, **kw),
                    initial=hop == 0,
                    with_down=False,
                ),
                out_shape=(payload, payload) if with_down else (payload,),
                in_specs=[smem(), smem()] + [vmem()] * 8,
                out_specs=(vmem(), vmem()) if with_down else (vmem(),),
                cost_estimate=cost,
                compiler_params=pltpu.CompilerParams(vmem_limit_bytes=KERNEL_VMEM),
                name=f"hop_{'first' if hop == 0 else 'both' if with_down else 'up'}",
            )(*operands)
            sent = lax.ppermute(outs[0].astype(jnp.float16), "seq", ahead)
            if with_down:
                down = lax.ppermute(outs[1].astype(jnp.float16), "seq", behind)
                down = down.astype(jnp.float32)
            up = sent.astype(jnp.float32)
    return pl.pallas_call(
        last_kernel,
        out_shape=jax.ShapeDtypeStruct((count, state, width), jnp.float32),
        in_specs=[smem(), smem()] + [vmem()] * 5,
        out_specs=vmem(),
        cost_estimate=cost,
        compiler_params=pltpu.CompilerParams(vmem_limit_bytes=KERNEL_VMEM),
        name="hop_last",
    )(flags(seq_index < half), usable, up, down, *fetched(seq_index))


def swapped(array):
    return lax.ppermute(array, "batch", [(0, 1), (1, 0)])


def local(
    prompt_cache,
    prompt_states,
    block_steps,
    prompt_lengths,
    target_slots,
    cache_lengths,
    resident_cache,
    token_cache,
    queries,
    resident_states,
    decay_rates,
    step_sizes,
    inner_input,
    inner_gate,
    state_input,
    state_readout,
    skip_gain,
):
    seq_count = lax.axis_size("seq")
    seq_index = lax.axis_index("seq")
    batch_index = lax.axis_index("batch")
    local_prompts, block_len, kv_heads, kv_width = prompt_cache.shape
    head_dim = kv_width // 2
    requests = resident_cache.shape[0]
    channels = decay_rates.shape[1]
    local_channels = channels // seq_count

    own_at = batch_index * local_prompts
    peer_at = (1 - batch_index) * local_prompts
    slot_ids = batch_index * requests + jnp.arange(requests, dtype=jnp.int32)
    matches = target_slots[None, :] == slot_ids[:, None]
    fresh = jnp.any(matches, axis=1)
    chosen_len = jnp.sum(jnp.where(matches, prompt_lengths[None, :], 0), axis=1)
    lengths = jnp.where(fresh, chosen_len, cache_lengths)
    own_match = lax.dynamic_slice_in_dim(matches, own_at, local_prompts, 1)
    peer_match = lax.dynamic_slice_in_dim(matches, peer_at, local_prompts, 1)
    own_lengths = lax.dynamic_slice_in_dim(prompt_lengths, own_at, local_prompts)
    usable = (seq_index * block_len < own_lengths).astype(jnp.float32)

    moved = lax.all_to_all(
        jnp.swapaxes(prompt_cache, 0, 1), "seq", split_axis=0, concat_axis=0, tiled=True
    )
    handed = hand_over(
        prompt_states[:, 0], block_steps[:, 0], decay_rates, usable, seq_count, seq_index
    )

    peer_moved = swapped(moved)
    flat = (block_len, local_prompts, kv_heads * kv_width)
    picked = jnp.einsum(
        "rp,ipx->rix",
        own_match.astype(jnp.bfloat16),
        moved.reshape(flat),
        preferred_element_type=jnp.float32,
    ) + jnp.einsum(
        "rp,ipx->rix",
        peer_match.astype(jnp.bfloat16),
        peer_moved.reshape(flat),
        preferred_element_type=jnp.float32,
    )
    picked = picked.astype(jnp.bfloat16).reshape(requests, block_len, kv_heads, kv_width)
    position = jnp.arange(block_len, dtype=jnp.int32) * seq_count + seq_index
    merged = jnp.where(fresh[:, None, None, None], picked, resident_cache[:, :, 0])
    merged = jnp.where(
        (position[None, :] < lengths[:, None])[:, :, None, None],
        merged,
        jnp.zeros((), jnp.bfloat16),
    )
    merged = jnp.where(
        (position[None, :] == lengths[:, None])[:, :, None, None], token_cache[:, None], merged
    )
    heads = queries.shape[1]
    group = heads // kv_heads
    grouped = queries.reshape(requests, kv_heads, group, head_dim)
    scores = jnp.einsum(
        "rgqd,rtgd->rgqt", grouped, merged[..., :head_dim], preferred_element_type=jnp.float32
    ) * (1.0 / math.sqrt(head_dim))
    seen = (position[None, :] <= lengths[:, None])[:, None, None, :]
    masked = jnp.where(seen, scores, -1e30)
    highest = jnp.max(masked, axis=3)
    weights = jnp.where(seen, jnp.exp(masked - highest[..., None]), 0.0)
    denominator = jnp.sum(weights, axis=3)
    summed = jnp.einsum(
        "rgqt,rtgd->rgqd",
        weights.astype(jnp.bfloat16),
        merged[..., head_dim:],
        preferred_element_type=jnp.float32,
    )
    owned = heads // seq_count
    rows = requests * owned
    sums = summed.reshape(requests, seq_count, owned, head_dim)
    sums = jnp.moveaxis(sums, 1, 0).reshape(seq_count, rows, head_dim)
    extra = jnp.stack([highest, denominator]).reshape(2, requests, seq_count, owned)
    extra = jnp.moveaxis(extra, 2, 0).reshape(seq_count, 2 * rows)
    extra = jnp.pad(extra, ((0, 0), (0, head_dim - 2 * rows)))[:, None]
    parcels = lax.all_to_all(
        jnp.concatenate([sums, extra], axis=1), "seq", split_axis=0, concat_axis=0, tiled=True
    )
    peer_sum = parcels[:, :rows]
    peer_top = parcels[:, rows, :rows]
    peer_total = parcels[:, rows, rows : 2 * rows]
    common_top = jnp.max(peer_top, axis=0)
    factor = jnp.exp(peer_top - common_top[None])
    owner_total = jnp.sum(peer_total * factor, axis=0)
    owner_sum = jnp.sum(peer_sum * factor[..., None], axis=0)
    attention = (owner_sum / owner_total[..., None]).astype(jnp.bfloat16)
    attention = attention.reshape(requests, owned, head_dim)

    rates_here = lax.dynamic_slice_in_dim(
        decay_rates, seq_index * local_channels, local_channels, 1
    )
    peer_handed = swapped(handed)
    chosen_state = jnp.sum(
        jnp.where(own_match[:, :, None, None], handed[None], 0.0), axis=1
    ) + jnp.sum(jnp.where(peer_match[:, :, None, None], peer_handed[None], 0.0), axis=1)
    start = jnp.where(fresh[:, None, None], chosen_state, resident_states)
    inner = inner_input.astype(jnp.float32)
    next_states = (
        jnp.exp(-rates_here[None] * step_sizes[:, None, :]) * start
        + (step_sizes * inner)[:, None, :] * state_input[:, :, None]
    )
    readout = jnp.sum(state_readout[:, :, None] * next_states, axis=1) + skip_gain[None, :] * inner
    mamba_output = (readout * jax.nn.silu(inner_gate.astype(jnp.float32))).astype(jnp.bfloat16)
    return (merged[:, :, None], attention, next_states, mamba_output)


def solution(mesh):
    return jax.shard_map(
        local,
        mesh=mesh,
        in_specs=(
            P(("groups", "batch"), "seq", None, None),
            P(("groups", "batch"), "seq", None, None),
            P(("groups", "batch"), "seq", None),
            P("groups"),
            P("groups"),
            P(("groups", "batch")),
            P(("groups", "batch"), None, "seq", None, None),
            P(("groups", "batch"), None, None),
            P(("groups", "batch"), None, None),
            P(("groups", "batch"), None, "seq"),
            P(),
            P(("groups", "batch"), "seq"),
            P(("groups", "batch"), "seq"),
            P(("groups", "batch"), "seq"),
            P(("groups", "batch"), None),
            P(("groups", "batch"), None),
            P("seq"),
        ),
        out_specs=(
            P(("groups", "batch"), None, "seq", None, None),
            P(("groups", "batch"), "seq", None),
            P(("groups", "batch"), None, "seq"),
            P(("groups", "batch"), "seq"),
        ),
        check_vma=False,
    )
```

time: 424 us -> 296 us (0.70)
  waiting for transfers between devices: 253 us -> 129 us
  starting transfers between devices: 56 us -> 108 us
  other arithmetic: 60 us -> 17.4 us
  blocking collectives: 22 us -> 0 us
  Pallas kernels: 0 us -> 12.4 us
  between operations: 14.1 us -> 2.66 us
    all_to_all x4 -> x2, waiting for transfers between devices: 131 us -> 0.01 us  [the longest x1 0.01 us: local(): lax.all_to_all(jnp.swapaxes(prompt_cache, 0, 1), 'seq', split_axis=0, con...]
    ppermute x0 -> x33, waiting for transfers between devices: none -> 129 us  [the longest x16 104 us: hand_over(): sent = lax.ppermute(outs[0].astype(jnp.float16), 'seq', ahead)]
    all_gather x2 -> x0, waiting for transfers between devices: 82.3 us -> none  [the longest x1 82.3 us: carried_in(): everything = lax.all_gather(shard, axis)]
    ppermute x0 -> x33, starting transfers between devices: none -> 60.1 us  [the longest x16 39.1 us: hand_over(): sent = lax.ppermute(outs[0].astype(jnp.float16), 'seq', ahead)]
    select_n x32 -> x0, other arithmetic: 41.8 us -> none  [step(): return jnp.where(reached, new, before)]
    reduce_scatter x1 -> x0, waiting for transfers between devices: 39.6 us -> none  [local(): lax.psum_scatter(decay_term(prompt_states[:, 0], behind, usable, decay_ra...]
    all_to_all x1 -> x0, blocking collectives: 22 us -> none  [sent_to_all(): lax.all_to_all(jnp.broadcast_to(shard[None], (count, *shard.shape)), axis...]
    pallas_call x0 -> x17, Pallas kernels: none -> 12.4 us  [the longest x16 11.7 us: hand_over(): pl.pallas_call(functools.partial(hop_kernel, initial=hop == 0, with_down=...]
  transfers between devices with their start and end apart: 7 -> 35, of which waited for: 6 -> 27; matrix products, arithmetic and copies ran while one was open for 16% -> 12% of each run, Pallas kernels for 0% -> 4%
where the time goes in v1:
time: 296 us; the launch traced here: 291 us
  waiting for transfers between devices  129 us (44%)
  starting transfers between devices  108 us (36%)
  other arithmetic  17.4 us (6%)
  local copies, waits for them, and re-layouts  15.5 us (5%)
  Pallas kernels  12.4 us (4%)
  matrix products  5.82 us (2%)
    ppermute x16, waiting for transfers between devices, hand_over(): sent = lax.ppermute(outs[0].astype(jnp.float16), 'seq', ahead)  104 us
    ppermute x16, starting transfers between devices, hand_over(): sent = lax.ppermute(outs[0].astype(jnp.float16), 'seq', ahead)  39.1 us
    all_to_all x1, starting transfers between devices, local(): lax.all_to_all(jnp.swapaxes(prompt_cache, 0, 1), 'seq', split_axis=0, con...  31.3 us
    ppermute x15, waiting for transfers between devices, hand_over(): down = lax.ppermute(outs[1].astype(jnp.float16), 'seq', behind)  24.2 us
    all_to_all x1, starting transfers between devices, local(): lax.all_to_all(jnp.concatenate([sums, extra], axis=1), 'seq', split_axis=...  16.3 us
    ppermute x2, starting transfers between devices, swapped(): return lax.ppermute(array, 'batch', [(0, 1), (1, 0)])  16.1 us
    pallas_call x16, Pallas kernels, hand_over(): pl.pallas_call(functools.partial(hop_kernel, initial=hop == 0, with_down=...  11.7 us
  transfers between devices with their start and end apart: 35, of which 27 were waited for; matrix products, arithmetic and copies ran while one was open for 12% of the time, Pallas kernels for 4%

profile of v1, /device:TPU:109, one launch (start us, length us, event | category | flops | bytes accessed | tf_op | source)
XLA Modules:
  0.0 290.5 jit_solution(359030943176950762)
XLA Ops:
  2.6 31.3 %all-to-all-start = ((bf16[32,4,8,256]{3,2,1,0:T(8,128)(2,1)}), bf16[32,4,8,256]{3,2,1,0:T(8,128)(2,1)}, u32[]{:S(2)}, u32[]{:S(2)}) async-start(bf16[32,4,8,256]{3,2,1,0:T(8,128)(2,1)} %bitcast.192), calls=%async_computation | async-start | bytes 1048576 | tf_op jit(solution)/shard_map/all_to_all | solution.py:227
  48.5 33.4 %collective-permute-done.1 = f16[200,512]{1,0:T(8,128)(2,1)} collective-permute-done((f16[200,512]{1,0:T(8,128)(2,1)}, f16[200,512]{1,0:T(8,128)(2,1)}, u32[]{:S(2)}, u32[]{:S(2)}) %collective-permute-start.1) | collective-permute-done | bytes 204832 | tf_op jit(solution)/shard_map/ring_0/ppermute | solution.py:167
  84.7 2.5 collective-permute-start.3
  88.0 3.7 %collective-permute-done.3 = f16[200,512]{1,0:T(8,128)(2,1)S(1)} collective-permute-done((f16[200,512]{1,0:T(8,128)(2,1)S(1)}, f16[200,512]{1,0:T(8,128)(2,1)S(1)}, u32[]{:S(2)}, u32[]{:S(2)}) %collective-permute-start.3) | collective-permute-done | bytes 204832 | tf_op jit(solution)/shard_map/ring_1/ppermute | solution.py:167
  94.4 3.1 %collective-permute-start.5 = (f16[200,512]{1,0:T(8,128)(2,1)S(1)}, f16[200,512]{1,0:T(8,128)(2,1)S(1)}, u32[]{:S(2)}, u32[]{:S(2)}) collective-permute-start(f16[200,512]{1,0:T(8,128)(2,1)S(1)} %convert_element_type.292), channel_id=1, source_target_pairs={{0,2},{2,4},{4,6},{6,8},{8,10},{10,12},{12,14},{14,16},{16,18},{18... | collective-permute-start | bytes 614408 | tf_op jit(solution)/shard_map/ring_2/ppermute | solution.py:167
  97.7 2.8 collective-permute-done.5
  100.6 3.3 %collective-permute-done.6 = f16[200,512]{1,0:T(8,128)(2,1)S(1)} collective-permute-done((f16[200,512]{1,0:T(8,128)(2,1)S(1)}, f16[200,512]{1,0:T(8,128)(2,1)S(1)}, u32[]{:S(2)}, u32[]{:S(2)}) %collective-permute-start.6) | collective-permute-done | bytes 204832 | tf_op jit(solution)/shard_map/ring_2/ppermute | solution.py:169
  106.4 3.0 %collective-permute-done.7 = f16[200,512]{1,0:T(8,128)(2,1)S(1)} collective-permute-done((f16[200,512]{1,0:T(8,128)(2,1)S(1)}, f16[200,512]{1,0:T(8,128)(2,1)S(1)}, u32[]{:S(2)}, u32[]{:S(2)}) %collective-permute-start.7) | collective-permute-done | bytes 204832 | tf_op jit(solution)/shard_map/ring_3/ppermute | solution.py:167
  116.5 3.5 %collective-permute-done.10 = f16[200,512]{1,0:T(8,128)(2,1)S(1)} collective-permute-done((f16[200,512]{1,0:T(8,128)(2,1)S(1)}, f16[200,512]{1,0:T(8,128)(2,1)S(1)}, u32[]{:S(2)}, u32[]{:S(2)}) %collective-permute-start.10) | collective-permute-done | bytes 204832 | tf_op jit(solution)/shard_map/ring_4/ppermute | solution.py:169
  122.5 3.0 %collective-permute-done.11 = f16[200,512]{1,0:T(8,128)(2,1)S(1)} collective-permute-done((f16[200,512]{1,0:T(8,128)(2,1)S(1)}, f16[200,512]{1,0:T(8,128)(2,1)S(1)}, u32[]{:S(2)}, u32[]{:S(2)}) %collective-permute-start.11) | collective-permute-done | bytes 204832 | tf_op jit(solution)/shard_map/ring_5/ppermute | solution.py:167
  129.8 3.3 %collective-permute-done.13 = f16[200,512]{1,0:T(8,128)(2,1)S(1)} collective-permute-done((f16[200,512]{1,0:T(8,128)(2,1)S(1)}, f16[200,512]{1,0:T(8,128)(2,1)S(1)}, u32[]{:S(2)}, u32[]{:S(2)}) %collective-permute-start.13) | collective-permute-done | bytes 204832 | tf_op jit(solution)/shard_map/ring_6/ppermute | solution.py:167
  137.8 4.7 %collective-permute-done.15 = f16[200,512]{1,0:T(8,128)(2,1)S(1)} collective-permute-done((f16[200,512]{1,0:T(8,128)(2,1)S(1)}, f16[200,512]{1,0:T(8,128)(2,1)S(1)}, u32[]{:S(2)}, u32[]{:S(2)}) %collective-permute-start.15) | collective-permute-done | bytes 204832 | tf_op jit(solution)/shard_map/ring_7/ppermute | solution.py:167
  142.6 2.4 collective-permute-done.16
  147.6 4.5 %collective-permute-done.17 = f16[200,512]{1,0:T(8,128)(2,1)S(1)} collective-permute-done((f16[200,512]{1,0:T(8,128)(2,1)S(1)}, f16[200,512]{1,0:T(8,128)(2,1)S(1)}, u32[]{:S(2)}, u32[]{:S(2)}) %collective-permute-start.17) | collective-permute-done | bytes 204832 | tf_op jit(solution)/shard_map/ring_8/ppermute | solution.py:167
  156.3 11.6 %collective-permute-start = (bf16[32,4,8,256]{3,2,1,0:T(8,128)(2,1)}, bf16[32,4,8,256]{3,2,1,0:T(8,128)(2,1)}, u32[]{:S(2)}, u32[]{:S(2)}) collective-permute-start(bf16[32,4,8,256]{3,2,1,0:T(8,128)(2,1)} %all-to-all-done), channel_id=1, source_target_pairs={{0,1},{1,0},{2,3},{3,2},{4,5},{5,4},{6,7},{7,6},{8,9},{9,8},{10,11... | collective-permute-start | bytes 1572872 | tf_op jit(solution)/shard_map/ppermute | solution.py:184
  170.9 2.8 collective-permute-done.21
  177.1 11.5 %collective-permute-start.23 = (f16[200,512]{1,0:T(8,128)(2,1)}, f16[200,512]{1,0:T(8,128)(2,1)}, u32[]{:S(2)}, u32[]{:S(2)}) collective-permute-start(f16[200,512]{1,0:T(8,128)(2,1)} %convert_element_type.328), channel_id=1, source_target_pairs={{0,2},{2,4},{4,6},{6,8},{8,10},{10,12},{12,14},{14,16},{16,18},{18... | collective-permute-start | bytes 614408 | tf_op jit(solution)/shard_map/ring_11/ppermute | solution.py:167
  202.3 16.3 %all-to-all-start.1 = ((f32[32,17,128]{2,1,0:T(8,128)}), f32[32,17,128]{2,1,0:T(8,128)S(1)}, u32[]{:S(2)}, u32[]{:S(2)}) async-start(f32[32,17,128]{2,1,0:T(8,128)} %copy.67), calls=%async_computation.1 | async-start | bytes 786432 | tf_op jit(solution)/shard_map/all_to_all | solution.py:282
  223.2 31.0 %collective-permute-done.25 = f16[200,512]{1,0:T(8,128)(2,1)S(1)} collective-permute-done((f16[200,512]{1,0:T(8,128)(2,1)S(1)}, f16[200,512]{1,0:T(8,128)(2,1)S(1)}, u32[]{:S(2)}, u32[]{:S(2)}) %collective-permute-start.25) | collective-permute-done | bytes 204832 | tf_op jit(solution)/shard_map/ring_12/ppermute | solution.py:167
  258.7 4.1 %collective-permute-done.27 = f16[200,512]{1,0:T(8,128)(2,1)S(1)} collective-permute-done((f16[200,512]{1,0:T(8,128)(2,1)S(1)}, f16[200,512]{1,0:T(8,128)(2,1)S(1)}, u32[]{:S(2)}, u32[]{:S(2)}) %collective-permute-start.27) | collective-permute-done | bytes 204832 | tf_op jit(solution)/shard_map/ring_13/ppermute | solution.py:167
  264.9 3.1 %collective-permute-start.29 = (f16[200,512]{1,0:T(8,128)(2,1)S(1)}, f16[200,512]{1,0:T(8,128)(2,1)S(1)}, u32[]{:S(2)}, u32[]{:S(2)}) collective-permute-start(f16[200,512]{1,0:T(8,128)(2,1)S(1)} %convert_element_type.340), channel_id=1, source_target_pairs={{0,2},{2,4},{4,6},{6,8},{8,10},{10,12},{12,14},{14,16},{16,18},{18... | collective-permute-start | bytes 614408 | tf_op jit(solution)/shard_map/ring_14/ppermute | solution.py:167
  270.7 3.5 %collective-permute-done.30 = f16[200,512]{1,0:T(8,128)(2,1)S(1)} collective-permute-done((f16[200,512]{1,0:T(8,128)(2,1)S(1)}, f16[200,512]{1,0:T(8,128)(2,1)S(1)}, u32[]{:S(2)}, u32[]{:S(2)}) %collective-permute-start.30) | collective-permute-done | bytes 204832 | tf_op jit(solution)/shard_map/ring_14/ppermute | solution.py:169
  276.6 3.1 %collective-permute-done.31 = f16[200,512]{1,0:T(8,128)(2,1)S(1)} collective-permute-done((f16[200,512]{1,0:T(8,128)(2,1)S(1)}, f16[200,512]{1,0:T(8,128)(2,1)S(1)}, u32[]{:S(2)}, u32[]{:S(2)}) %collective-permute-start.31) | collective-permute-done | bytes 204832 | tf_op jit(solution)/shard_map/ring_15/ppermute | solution.py:167
  280.6 4.5 %collective-permute-start.32 = (f32[4,16,512]{2,1,0:T(8,128)S(1)}, f32[4,16,512]{2,1,0:T(8,128)S(1)}, u32[]{:S(2)}, u32[]{:S(2)}) collective-permute-start(f32[4,16,512]{2,1,0:T(8,128)S(1)} %hop_last.1), channel_id=1, source_target_pairs={{0,1},{1,0},{2,3},{3,2},{4,5},{5,4},{6,7},{7,6},{8,9},{9,8},{10,11... | collective-permute-start | bytes 393224 | tf_op jit(solution)/shard_map/ppermute | solution.py:184
  (321 shorter events, 91.9 us)
Async XLA Ops:
  2.6 153.7 %all-to-all-start = ((bf16[32,4,8,256]{3,2,1,0:T(8,128)(2,1)}), bf16[32,4,8,256]{3,2,1,0:T(8,128)(2,1)}, u32[]{:S(2)}, u32[]{:S(2)}) async-start(bf16[32,4,8,256]{3,2,1,0:T(8,128)(2,1)} %bitcast.192), calls=%async_computation | async-start | bytes 1048576 | tf_op jit(solution)/shard_map/all_to_all | solution.py:227
  40.3 41.6 %collective-permute-start.1 = (f16[200,512]{1,0:T(8,128)(2,1)}, f16[200,512]{1,0:T(8,128)(2,1)}, u32[]{:S(2)}, u32[]{:S(2)}) collective-permute-start(f16[200,512]{1,0:T(8,128)(2,1)} %convert_element_type.284), channel_id=1, source_target_pairs={{0,2},{2,4},{4,6},{6,8},{8,10},{10,12},{12,14},{14,16},{16,18},{18... | collective-permute-start | bytes 614408 | tf_op jit(solution)/shard_map/ring_0/ppermute | solution.py:167
  42.2 40.7 %collective-permute-start.2 = (f16[200,512]{1,0:T(8,128)(2,1)}, f16[200,512]{1,0:T(8,128)(2,1)}, u32[]{:S(2)}, u32[]{:S(2)}) collective-permute-start(f16[200,512]{1,0:T(8,128)(2,1)} %convert_element_type.286), channel_id=1, source_target_pairs={{0,62},{2,0},{4,2},{6,4},{8,6},{10,8},{12,10},{14,12},{16,14},{18,... | collective-permute-start | bytes 614408 | tf_op jit(solution)/shard_map/ring_0/ppermute | solution.py:169
  84.7 7.0 %collective-permute-start.3 = (f16[200,512]{1,0:T(8,128)(2,1)S(1)}, f16[200,512]{1,0:T(8,128)(2,1)S(1)}, u32[]{:S(2)}, u32[]{:S(2)}) collective-permute-start(f16[200,512]{1,0:T(8,128)(2,1)S(1)} %convert_element_type.288), channel_id=1, source_target_pairs={{0,2},{2,4},{4,6},{6,8},{8,10},{10,12},{12,14},{14,16},{16,18},{18... | collective-permute-start | bytes 614408 | tf_op jit(solution)/shard_map/ring_1/ppermute | solution.py:167
  87.2 6.3 %collective-permute-start.4 = (f16[200,512]{1,0:T(8,128)(2,1)S(1)}, f16[200,512]{1,0:T(8,128)(2,1)S(1)}, u32[]{:S(2)}, u32[]{:S(2)}) collective-permute-start(f16[200,512]{1,0:T(8,128)(2,1)S(1)} %convert_element_type.290), channel_id=1, source_target_pairs={{0,62},{2,0},{4,2},{6,4},{8,6},{10,8},{12,10},{14,12},{16,14},{18,... | collective-permute-start | bytes 614408 | tf_op jit(solution)/shard_map/ring_1/ppermute | solution.py:169
  94.4 6.1 %collective-permute-start.5 = (f16[200,512]{1,0:T(8,128)(2,1)S(1)}, f16[200,512]{1,0:T(8,128)(2,1)S(1)}, u32[]{:S(2)}, u32[]{:S(2)}) collective-permute-start(f16[200,512]{1,0:T(8,128)(2,1)S(1)} %convert_element_type.292), channel_id=1, source_target_pairs={{0,2},{2,4},{4,6},{6,8},{8,10},{10,12},{12,14},{14,16},{16,18},{18... | collective-permute-start | bytes 614408 | tf_op jit(solution)/shard_map/ring_2/ppermute | solution.py:167
  97.5 6.3 %collective-permute-start.6 = (f16[200,512]{1,0:T(8,128)(2,1)S(1)}, f16[200,512]{1,0:T(8,128)(2,1)S(1)}, u32[]{:S(2)}, u32[]{:S(2)}) collective-permute-start(f16[200,512]{1,0:T(8,128)(2,1)S(1)} %convert_element_type.294), channel_id=1, source_target_pairs={{0,62},{2,0},{4,2},{6,4},{8,6},{10,8},{12,10},{14,12},{16,14},{18,... | collective-permute-start | bytes 614408 | tf_op jit(solution)/shard_map/ring_2/ppermute | solution.py:169
  113.7 6.2 %collective-permute-start.10 = (f16[200,512]{1,0:T(8,128)(2,1)S(1)}, f16[200,512]{1,0:T(8,128)(2,1)S(1)}, u32[]{:S(2)}, u32[]{:S(2)}) collective-permute-start(f16[200,512]{1,0:T(8,128)(2,1)S(1)} %convert_element_type.302), channel_id=1, source_target_pairs={{0,62},{2,0},{4,2},{6,4},{8,6},{10,8},{12,10},{14,12},{16,14},{18,... | collective-permute-start | bytes 614408 | tf_op jit(solution)/shard_map/ring_4/ppermute | solution.py:169
  135.8 6.8 %collective-permute-start.15 = (f16[200,512]{1,0:T(8,128)(2,1)S(1)}, f16[200,512]{1,0:T(8,128)(2,1)S(1)}, u32[]{:S(2)}, u32[]{:S(2)}) collective-permute-start(f16[200,512]{1,0:T(8,128)(2,1)S(1)} %convert_element_type.312), channel_id=1, source_target_pairs={{0,2},{2,4},{4,6},{6,8},{8,10},{10,12},{12,14},{14,16},{16,18},{18... | collective-permute-start | bytes 614408 | tf_op jit(solution)/shard_map/ring_7/ppermute | solution.py:167
  137.6 7.3 %collective-permute-start.16 = (f16[200,512]{1,0:T(8,128)(2,1)S(1)}, f16[200,512]{1,0:T(8,128)(2,1)S(1)}, u32[]{:S(2)}, u32[]{:S(2)}) collective-permute-start(f16[200,512]{1,0:T(8,128)(2,1)S(1)} %convert_element_type.314), channel_id=1, source_target_pairs={{0,62},{2,0},{4,2},{6,4},{8,6},{10,8},{12,10},{14,12},{16,14},{18,... | collective-permute-start | bytes 614408 | tf_op jit(solution)/shard_map/ring_7/ppermute | solution.py:169
  145.8 6.3 %collective-permute-start.17 = (f16[200,512]{1,0:T(8,128)(2,1)S(1)}, f16[200,512]{1,0:T(8,128)(2,1)S(1)}, u32[]{:S(2)}, u32[]{:S(2)}) collective-permute-start(f16[200,512]{1,0:T(8,128)(2,1)S(1)} %convert_element_type.316), channel_id=1, source_target_pairs={{0,2},{2,4},{4,6},{6,8},{8,10},{10,12},{12,14},{14,16},{16,18},{18... | collective-permute-start | bytes 614408 | tf_op jit(solution)/shard_map/ring_8/ppermute | solution.py:167
  146.7 6.2 %collective-permute-start.18 = (f16[200,512]{1,0:T(8,128)(2,1)S(1)}, f16[200,512]{1,0:T(8,128)(2,1)S(1)}, u32[]{:S(2)}, u32[]{:S(2)}) collective-permute-start(f16[200,512]{1,0:T(8,128)(2,1)S(1)} %convert_element_type.318), channel_id=1, source_target_pairs={{0,62},{2,0},{4,2},{6,4},{8,6},{10,8},{12,10},{14,12},{16,14},{18,... | collective-permute-start | bytes 614408 | tf_op jit(solution)/shard_map/ring_8/ppermute | solution.py:169
  153.8 14.2 %collective-permute-start.19 = (f16[200,512]{1,0:T(8,128)(2,1)S(1)}, f16[200,512]{1,0:T(8,128)(2,1)S(1)}, u32[]{:S(2)}, u32[]{:S(2)}) collective-permute-start(f16[200,512]{1,0:T(8,128)(2,1)S(1)} %convert_element_type.320), channel_id=1, source_target_pairs={{0,2},{2,4},{4,6},{6,8},{8,10},{10,12},{12,14},{14,16},{16,18},{18... | collective-permute-start | bytes 614408 | tf_op jit(solution)/shard_map/ring_9/ppermute | solution.py:167
  156.1 11.9 %collective-permute-start.20 = (f16[200,512]{1,0:T(8,128)(2,1)S(1)}, f16[200,512]{1,0:T(8,128)(2,1)S(1)}, u32[]{:S(2)}, u32[]{:S(2)}) collective-permute-start(f16[200,512]{1,0:T(8,128)(2,1)S(1)} %convert_element_type.322), channel_id=1, source_target_pairs={{0,62},{2,0},{4,2},{6,4},{8,6},{10,8},{12,10},{14,12},{16,14},{18,... | collective-permute-start | bytes 614408 | tf_op jit(solution)/shard_map/ring_9/ppermute | solution.py:169
  156.3 36.3 %collective-permute-start = (bf16[32,4,8,256]{3,2,1,0:T(8,128)(2,1)}, bf16[32,4,8,256]{3,2,1,0:T(8,128)(2,1)}, u32[]{:S(2)}, u32[]{:S(2)}) collective-permute-start(bf16[32,4,8,256]{3,2,1,0:T(8,128)(2,1)} %all-to-all-done), channel_id=1, source_target_pairs={{0,1},{1,0},{2,3},{3,2},{4,5},{5,4},{6,7},{7,6},{8,9},{9,8},{10,11... | collective-permute-start | bytes 1572872 | tf_op jit(solution)/shard_map/ppermute | solution.py:184
  177.1 41.6 %collective-permute-start.23 = (f16[200,512]{1,0:T(8,128)(2,1)}, f16[200,512]{1,0:T(8,128)(2,1)}, u32[]{:S(2)}, u32[]{:S(2)}) collective-permute-start(f16[200,512]{1,0:T(8,128)(2,1)} %convert_element_type.328), channel_id=1, source_target_pairs={{0,2},{2,4},{4,6},{6,8},{8,10},{10,12},{12,14},{14,16},{16,18},{18... | collective-permute-start | bytes 614408 | tf_op jit(solution)/shard_map/ring_11/ppermute | solution.py:167
  189.4 30.4 %collective-permute-start.24 = (f16[200,512]{1,0:T(8,128)(2,1)}, f16[200,512]{1,0:T(8,128)(2,1)}, u32[]{:S(2)}, u32[]{:S(2)}) collective-permute-start(f16[200,512]{1,0:T(8,128)(2,1)} %convert_element_type.330), channel_id=1, source_target_pairs={{0,62},{2,0},{4,2},{6,4},{8,6},{10,8},{12,10},{14,12},{16,14},{18,... | collective-permute-start | bytes 614408 | tf_op jit(solution)/shard_map/ring_11/ppermute | solution.py:169
  202.3 87.0 %all-to-all-start.1 = ((f32[32,17,128]{2,1,0:T(8,128)}), f32[32,17,128]{2,1,0:T(8,128)S(1)}, u32[]{:S(2)}, u32[]{:S(2)}) async-start(f32[32,17,128]{2,1,0:T(8,128)} %copy.67), calls=%async_computation.1 | async-start | bytes 786432 | tf_op jit(solution)/shard_map/all_to_all | solution.py:282
  221.5 32.7 %collective-permute-start.25 = (f16[200,512]{1,0:T(8,128)(2,1)S(1)}, f16[200,512]{1,0:T(8,128)(2,1)S(1)}, u32[]{:S(2)}, u32[]{:S(2)}) collective-permute-start(f16[200,512]{1,0:T(8,128)(2,1)S(1)} %convert_element_type.332), channel_id=1, source_target_pairs={{0,2},{2,4},{4,6},{6,8},{8,10},{10,12},{12,14},{14,16},{16,18},{18... | collective-permute-start | bytes 614408 | tf_op jit(solution)/shard_map/ring_12/ppermute | solution.py:167
  222.8 32.5 %collective-permute-start.26 = (f16[200,512]{1,0:T(8,128)(2,1)S(1)}, f16[200,512]{1,0:T(8,128)(2,1)S(1)}, u32[]{:S(2)}, u32[]{:S(2)}) collective-permute-start(f16[200,512]{1,0:T(8,128)(2,1)S(1)} %convert_element_type.334), channel_id=1, source_target_pairs={{0,62},{2,0},{4,2},{6,4},{8,6},{10,8},{12,10},{14,12},{16,14},{18,... | collective-permute-start | bytes 614408 | tf_op jit(solution)/shard_map/ring_12/ppermute | solution.py:169
  256.1 6.7 %collective-permute-start.27 = (f16[200,512]{1,0:T(8,128)(2,1)S(1)}, f16[200,512]{1,0:T(8,128)(2,1)S(1)}, u32[]{:S(2)}, u32[]{:S(2)}) collective-permute-start(f16[200,512]{1,0:T(8,128)(2,1)S(1)} %convert_element_type.336), channel_id=1, source_target_pairs={{0,2},{2,4},{4,6},{6,8},{8,10},{10,12},{12,14},{14,16},{16,18},{18... | collective-permute-start | bytes 614408 | tf_op jit(solution)/shard_map/ring_13/ppermute | solution.py:167
  258.0 6.1 %collective-permute-start.28 = (f16[200,512]{1,0:T(8,128)(2,1)S(1)}, f16[200,512]{1,0:T(8,128)(2,1)S(1)}, u32[]{:S(2)}, u32[]{:S(2)}) collective-permute-start(f16[200,512]{1,0:T(8,128)(2,1)S(1)} %convert_element_type.338), channel_id=1, source_target_pairs={{0,62},{2,0},{4,2},{6,4},{8,6},{10,8},{12,10},{14,12},{16,14},{18,... | collective-permute-start | bytes 614408 | tf_op jit(solution)/shard_map/ring_13/ppermute | solution.py:169
  264.9 5.8 %collective-permute-start.29 = (f16[200,512]{1,0:T(8,128)(2,1)S(1)}, f16[200,512]{1,0:T(8,128)(2,1)S(1)}, u32[]{:S(2)}, u32[]{:S(2)}) collective-permute-start(f16[200,512]{1,0:T(8,128)(2,1)S(1)} %convert_element_type.340), channel_id=1, source_target_pairs={{0,2},{2,4},{4,6},{6,8},{8,10},{10,12},{12,14},{14,16},{16,18},{18... | collective-permute-start | bytes 614408 | tf_op jit(solution)/shard_map/ring_14/ppermute | solution.py:167
  268.0 6.2 %collective-permute-start.30 = (f16[200,512]{1,0:T(8,128)(2,1)S(1)}, f16[200,512]{1,0:T(8,128)(2,1)S(1)}, u32[]{:S(2)}, u32[]{:S(2)}) collective-permute-start(f16[200,512]{1,0:T(8,128)(2,1)S(1)} %convert_element_type.342), channel_id=1, source_target_pairs={{0,62},{2,0},{4,2},{6,4},{8,6},{10,8},{12,10},{14,12},{16,14},{18,... | collective-permute-start | bytes 614408 | tf_op jit(solution)/shard_map/ring_14/ppermute | solution.py:169
  (75 other events, 1234.0 us)

commit v2 on v0

v2 whole, which is shorter than its diff:
```python
import functools
import math

import jax
import jax.numpy as jnp
from jax import lax
from jax.experimental import pallas as pl
from jax.experimental.pallas import tpu as pltpu
from jax.sharding import PartitionSpec as P


STATE_SCALE = 128.0
HALF_SPLIT = 8193.0
KERNEL_VMEM = 8 * 1024 * 1024
PAIRS_A_STEP = 4


def split_half(value):
    spread = value * HALF_SPLIT
    high = spread - (spread - value)
    return high, value - high


def smem():
    return pl.BlockSpec(memory_space=pltpu.SMEM)


def vmem():
    return pl.BlockSpec(memory_space=pltpu.VMEM)


def pick_kernel(flags, usable, state_in, step_in, state_out, step_out, *, width):
    count = state_in.shape[0]
    for q in range(PAIRS_A_STEP):
        source = pl.ds(pl.multiple_of(2 * q * width + flags[0] * width, 128), width)
        target = pl.ds(q * width, width)
        for p in range(count):
            use = usable[p]
            state_out[p, :, target] = state_in[p, :, source] * (use * STATE_SCALE)
            step_out[p : p + 1, target] = step_in[p : p + 1, source] * use


def fold_kernel(
    flags, usable, state_in, step_in, rate_in, came_state, came_step, state_out, step_out, rate_out,
    *, width,
):
    count = state_in.shape[0]
    older = flags[1] == 1
    for q in range(PAIRS_A_STEP):
        source = pl.ds(pl.multiple_of(2 * q * width + flags[0] * width, 128), width)
        target = pl.ds(q * width, width)
        rate = rate_in[:, source]
        rate_out[:, target] = rate
        for p in range(count):
            use = usable[p]
            own = state_in[p, :, source] * (use * STATE_SCALE)
            step = step_in[p : p + 1, source] * use
            came, came_by = came_state[p, :, target], came_step[p : p + 1, target]
            early, late = jnp.where(older, own, came), jnp.where(older, came, own)
            late_by = jnp.where(older, came_by, step)
            state_out[p, :, target] = jnp.exp(-rate * late_by) * early + late
            step_out[p : p + 1, target] = step + came_by


def hop_kernel(
    flags, states, steps, rates, up_in, down_in, up_out, down_out=None, *, width, initial
):
    count, state = states.shape[0], states.shape[1]
    rows = count * state
    up_at = pl.ds(pl.multiple_of(flags[0] * width, 128), width)
    down_at = pl.ds(pl.multiple_of(flags[1] * width, 128), width)
    first, last = flags[2] == 1, flags[3] == 1
    up_wrapped, down_wrapped = flags[4] == 1, flags[5] == 1
    up_rate, down_rate = rates[:, up_at], rates[:, down_at]

    @pl.loop(0, count)
    def _(p):
        here = pl.ds(pl.multiple_of(p * state, state), state)
        there = pl.ds(pl.multiple_of(rows + p * state, state), state)
        wide, narrow = pl.ds(2 * rows + p, 1), pl.ds(2 * rows + count + p, 1)
        own, step = states[p, :, up_at], steps[pl.ds(p, 1), up_at]
        if initial:
            acc, aside, span = own, jnp.zeros_like(own), step
        else:
            high, other = up_in[here, :], up_in[there, :]
            whole = high + other
            acc = jnp.where(first, 0.0, jnp.where(up_wrapped, high, whole))
            acc = jnp.exp(-up_rate * step) * acc + own
            aside = jnp.where(first, whole, other)
            span = up_in[wide, :] + up_in[narrow, :]
            span = jnp.where(up_wrapped, span, span + step)
        high, low = split_half(acc)
        up_out[here, :] = high
        up_out[there, :] = low if initial else jnp.where(up_wrapped, aside, low)
        up_out[wide, :], up_out[narrow, :] = split_half(span)
        if down_out is None:
            return
        own, step = states[p, :, down_at], steps[pl.ds(p, 1), down_at]
        if initial:
            acc, aside, span = own, jnp.zeros_like(own), step
        else:
            high, other = down_in[here, :], down_in[there, :]
            whole = high + other
            span = jnp.where(last, 0.0, down_in[wide, :] + down_in[narrow, :])
            acc = jnp.where(last, 0.0, jnp.where(down_wrapped, high, whole))
            acc = acc + jnp.exp(-down_rate * span) * own
            aside = jnp.where(last, whole, other)
            span = span + step
        high, low = split_half(acc)
        down_out[here, :] = high
        down_out[there, :] = low if initial else jnp.where(down_wrapped, aside, low)
        down_out[wide, :], down_out[narrow, :] = split_half(span)


def last_kernel(flags, states, steps, rates, up_in, down_in, handed, *, width):
    count, state = states.shape[0], states.shape[1]
    rows = count * state
    at = pl.ds(pl.multiple_of(flags[0] * width, 128), width)
    first, last = flags[2] == 1, flags[3] == 1
    up_wrapped, down_wrapped = flags[4] == 1, flags[5] == 1
    rate = rates[:, at]

    @pl.loop(0, count)
    def _(p):
        here = pl.ds(pl.multiple_of(p * state, state), state)
        there = pl.ds(pl.multiple_of(rows + p * state, state), state)
        wide, narrow = pl.ds(2 * rows + p, 1), pl.ds(2 * rows + count + p, 1)
        own, step = states[p, :, at], steps[pl.ds(p, 1), at]
        high, other = up_in[here, :], up_in[there, :]
        whole = high + other
        newest = jnp.where(first, whole, jnp.where(up_wrapped, other, 0.0))
        earlier = jnp.where(first, 0.0, jnp.where(up_wrapped, high, whole))
        span = up_in[wide, :] + up_in[narrow, :]
        high, other = down_in[here, :], down_in[there, :]
        whole = high + other
        oldest = jnp.where(last, whole, jnp.where(down_wrapped, other, 0.0))
        later = jnp.where(last, 0.0, jnp.where(down_wrapped, high, whole))
        span_down = jnp.where(last, 0.0, down_in[wide, :] + down_in[narrow, :])
        outer = jnp.where(up_wrapped, span, 0.0)
        inner = earlier + jnp.exp(-rate * span) * oldest
        inner = later + jnp.exp(-rate * span_down) * (own + jnp.exp(-rate * step) * inner)
        handed[p] = (newest + jnp.exp(-rate * outer) * inner) * (1.0 / STATE_SCALE)


def numbers(*values):
    return jnp.stack([jnp.asarray(v) for v in values]).astype(jnp.int32)


def picked_for_pair(states, steps, usable, seq_index, width):
    count, state, channels = states.shape
    wide = PAIRS_A_STEP * width
    return pl.pallas_call(
        functools.partial(pick_kernel, width=width),
        grid=(channels // (2 * wide),),
        out_shape=(
            jax.ShapeDtypeStruct((count, state, channels // 2), jnp.float32),
            jax.ShapeDtypeStruct((count, channels // 2), jnp.float32),
        ),
        in_specs=[
            smem(),
            smem(),
            pl.BlockSpec((count, state, 2 * wide), lambda n: (0, 0, n)),
            pl.BlockSpec((count, 2 * wide), lambda n: (0, n)),
        ],
        out_specs=(
            pl.BlockSpec((count, state, wide), lambda n: (0, 0, n)),
            pl.BlockSpec((count, wide), lambda n: (0, n)),
        ),
        cost_estimate=pl.CostEstimate(
            flops=states.size, bytes_accessed=6 * states.size, transcendentals=0
        ),
        compiler_params=pltpu.CompilerParams(vmem_limit_bytes=2 * KERNEL_VMEM),
        name="pick_for_pair",
    )(numbers(1 - seq_index % 2), usable, states, steps)


def folded_pair(states, steps, rates, usable, came_state, came_step, seq_index, width):
    count, state, channels = states.shape
    wide = PAIRS_A_STEP * width
    parity = seq_index % 2
    return pl.pallas_call(
        functools.partial(fold_kernel, width=width),
        grid=(channels // (2 * wide),),
        out_shape=(
            jax.ShapeDtypeStruct((count, state, channels // 2), jnp.float32),
            jax.ShapeDtypeStruct((count, channels // 2), jnp.float32),
            jax.ShapeDtypeStruct((state, channels // 2), jnp.float32),
        ),
        in_specs=[
            smem(),
            smem(),
            pl.BlockSpec((count, state, 2 * wide), lambda n: (0, 0, n)),
            pl.BlockSpec((count, 2 * wide), lambda n: (0, n)),
            pl.BlockSpec((state, 2 * wide), lambda n: (0, n)),
            pl.BlockSpec((count, state, wide), lambda n: (0, 0, n)),
            pl.BlockSpec((count, wide), lambda n: (0, n)),
        ],
        out_specs=(
            pl.BlockSpec((count, state, wide), lambda n: (0, 0, n)),
            pl.BlockSpec((count, wide), lambda n: (0, n)),
            pl.BlockSpec((state, wide), lambda n: (0, n)),
        ),
        cost_estimate=pl.CostEstimate(
            flops=4 * states.size, bytes_accessed=10 * states.size, transcendentals=states.size
        ),
        compiler_params=pltpu.CompilerParams(vmem_limit_bytes=2 * KERNEL_VMEM),
        name="fold_pair",
    )(numbers(parity, parity == 0), usable, states, steps, rates, came_state, came_step)


def hand_over(states, steps, rates, width, nodes, node):
    count, state, _ = states.shape
    half = nodes // 2
    ring = 2 * nodes
    ahead = [(k, (k + 2) % ring) for k in range(ring)]
    behind = [(k, (k - 2) % ring) for k in range(ring)]
    rows = 2 * count * state + 2 * count
    payload = jax.ShapeDtypeStruct((rows, width), jnp.float32)
    cost = pl.CostEstimate(
        flops=16 * rows * width, bytes_accessed=16 * rows * width, transcendentals=rows * width
    )
    first, last = node == 0, node == nodes - 1
    up = down = jnp.zeros((8, 128), jnp.float32)
    for hop in range(half):
        both = hop < half - 1
        outs = pl.pallas_call(
            functools.partial(hop_kernel, width=width, initial=hop == 0),
            out_shape=(payload, payload) if both else (payload,),
            in_specs=[smem()] + [vmem()] * 5,
            out_specs=(vmem(), vmem()) if both else (vmem(),),
            cost_estimate=cost,
            compiler_params=pltpu.CompilerParams(vmem_limit_bytes=KERNEL_VMEM),
            name="hop_first" if hop == 0 else "hop_both" if both else "hop_up",
        )(
            numbers(
                (node + half - hop) % nodes,
                (node - (half - 1) + hop) % nodes,
                first,
                last,
                node < hop,
                node + hop >= nodes,
            ),
            states,
            steps,
            rates,
            up,
            down,
        )
        sent = lax.ppermute(outs[0].astype(jnp.float16), "seq", ahead)
        if both:
            down = lax.ppermute(outs[1].astype(jnp.float16), "seq", behind)
            down = down.astype(jnp.float32)
        up = sent.astype(jnp.float32)
    return pl.pallas_call(
        functools.partial(last_kernel, width=width),
        out_shape=jax.ShapeDtypeStruct((count, state, width), jnp.float32),
        in_specs=[smem()] + [vmem()] * 5,
        out_specs=vmem(),
        cost_estimate=cost,
        compiler_params=pltpu.CompilerParams(vmem_limit_bytes=KERNEL_VMEM),
        name="hop_last",
    )(
        numbers(node, node, first, last, node < half, node + half - 1 >= nodes),
        states,
        steps,
        rates,
        up,
        down,
    )


def in_pieces(value):
    pieces = []
    for _ in range(3):
        piece = lax.reduce_precision(value, 5, 10)
        pieces.append(piece)
        value = value - piece
    return jnp.stack(pieces)


def swapped(array):
    return lax.ppermute(array, "batch", [(0, 1), (1, 0)])


def local(
    prompt_cache,
    prompt_states,
    block_steps,
    prompt_lengths,
    target_slots,
    cache_lengths,
    resident_cache,
    token_cache,
    queries,
    resident_states,
    decay_rates,
    step_sizes,
    inner_input,
    inner_gate,
    state_input,
    state_readout,
    skip_gain,
):
    seq_count = lax.axis_size("seq")
    seq_index = lax.axis_index("seq")
    batch_index = lax.axis_index("batch")
    local_prompts, block_len, kv_heads, kv_width = prompt_cache.shape
    head_dim = kv_width // 2
    requests = resident_cache.shape[0]
    channels = decay_rates.shape[1]
    local_channels = channels // seq_count

    own_at = batch_index * local_prompts
    peer_at = (1 - batch_index) * local_prompts
    slot_ids = batch_index * requests + jnp.arange(requests, dtype=jnp.int32)
    matches = target_slots[None, :] == slot_ids[:, None]
    fresh = jnp.any(matches, axis=1)
    chosen_len = jnp.sum(jnp.where(matches, prompt_lengths[None, :], 0), axis=1)
    lengths = jnp.where(fresh, chosen_len, cache_lengths)
    own_match = lax.dynamic_slice_in_dim(matches, own_at, local_prompts, 1)
    peer_match = lax.dynamic_slice_in_dim(matches, peer_at, local_prompts, 1)
    own_lengths = lax.dynamic_slice_in_dim(prompt_lengths, own_at, local_prompts)
    usable = (seq_index * block_len < own_lengths).astype(jnp.float32)

    states, steps = prompt_states[:, 0], block_steps[:, 0]
    pairs = [(k, k ^ 1) for k in range(seq_count)]
    sent_state, sent_step = picked_for_pair(states, steps, usable, seq_index, local_channels)
    came_state = lax.ppermute(sent_state.astype(jnp.float16), "seq", pairs)
    came_step = lax.ppermute(sent_step, "seq", pairs)
    moved = lax.all_to_all(
        jnp.swapaxes(prompt_cache, 0, 1), "seq", split_axis=0, concat_axis=0, tiled=True
    )
    folded = folded_pair(
        states,
        steps,
        decay_rates,
        usable,
        came_state.astype(jnp.float32),
        came_step,
        seq_index,
        local_channels,
    )
    handed = hand_over(*folded, local_channels, seq_count // 2, seq_index // 2)

    peer_moved = swapped(moved)
    flat = (block_len, local_prompts, kv_heads * kv_width)
    picked = jnp.einsum(
        "rp,ipx->rix",
        own_match.astype(jnp.bfloat16),
        moved.reshape(flat),
        preferred_element_type=jnp.float32,
    ) + jnp.einsum(
        "rp,ipx->rix",
        peer_match.astype(jnp.bfloat16),
        peer_moved.reshape(flat),
        preferred_element_type=jnp.float32,
    )
    picked = picked.astype(jnp.bfloat16).reshape(requests, block_len, kv_heads, kv_width)
    position = jnp.arange(block_len, dtype=jnp.int32) * seq_count + seq_index
    merged = jnp.where(fresh[:, None, None, None], picked, resident_cache[:, :, 0])
    merged = jnp.where(
        (position[None, :] < lengths[:, None])[:, :, None, None],
        merged,
        jnp.zeros((), jnp.bfloat16),
    )
    merged = jnp.where(
        (position[None, :] == lengths[:, None])[:, :, None, None], token_cache[:, None], merged
    )
    heads = queries.shape[1]
    group = heads // kv_heads
    grouped = queries.reshape(requests, kv_heads, group, head_dim)
    scores = jnp.einsum(
        "rgqd,rtgd->rgqt", grouped, merged[..., :head_dim], preferred_element_type=jnp.float32
    ) * (1.0 / math.sqrt(head_dim))
    seen = (position[None, :] <= lengths[:, None])[:, None, None, :]
    masked = jnp.where(seen, scores, -1e30)
    highest = jnp.max(masked, axis=3)
    weights = jnp.where(seen, jnp.exp(masked - highest[..., None]), 0.0)
    denominator = jnp.sum(weights, axis=3)
    summed = jnp.einsum(
        "rgqt,rtgd->rgqd",
        weights.astype(jnp.bfloat16),
        merged[..., head_dim:],
        preferred_element_type=jnp.float32,
    )
    owned = heads // seq_count
    rows = requests * owned
    sums = summed.reshape(requests, seq_count, owned, head_dim)
    sums = jnp.moveaxis(sums, 1, 0).reshape(seq_count, rows, head_dim)
    extra = in_pieces(jnp.stack([highest, denominator])).reshape(6, requests, seq_count, owned)
    extra = jnp.moveaxis(extra, 2, 0).reshape(seq_count, 6 * rows)
    extra = jnp.pad(extra, ((0, 0), (0, head_dim - 6 * rows)))[:, None]
    parcels = lax.all_to_all(
        jnp.concatenate([sums, extra], axis=1).astype(jnp.float16),
        "seq",
        split_axis=0,
        concat_axis=0,
        tiled=True,
    ).astype(jnp.float32)
    peer_sum = parcels[:, :rows]
    peer_extra = parcels[:, rows, : 6 * rows].reshape(seq_count, 3, 2, rows)
    peer_extra = (peer_extra[:, 2] + peer_extra[:, 1]) + peer_extra[:, 0]
    peer_top, peer_total = peer_extra[:, 0], peer_extra[:, 1]
    common_top = jnp.max(peer_top, axis=0)
    factor = jnp.exp(peer_top - common_top[None])
    owner_total = jnp.sum(peer_total * factor, axis=0)
    owner_sum = jnp.sum(peer_sum * factor[..., None], axis=0)
    attention = (owner_sum / owner_total[..., None]).astype(jnp.bfloat16)
    attention = attention.reshape(requests, owned, head_dim)

    rates_here = lax.dynamic_slice_in_dim(
        decay_rates, seq_index * local_channels, local_channels, 1
    )
    peer_handed = swapped(handed)
    chosen_state = jnp.sum(
        jnp.where(own_match[:, :, None, None], handed[None], 0.0), axis=1
    ) + jnp.sum(jnp.where(peer_match[:, :, None, None], peer_handed[None], 0.0), axis=1)
    start = jnp.where(fresh[:, None, None], chosen_state, resident_states)
    inner = inner_input.astype(jnp.float32)
    next_states = (
        jnp.exp(-rates_here[None] * step_sizes[:, None, :]) * start
        + (step_sizes * inner)[:, None, :] * state_input[:, :, None]
    )
    readout = jnp.sum(state_readout[:, :, None] * next_states, axis=1) + skip_gain[None, :] * inner
    mamba_output = (readout * jax.nn.silu(inner_gate.astype(jnp.float32))).astype(jnp.bfloat16)
    return (merged[:, :, None], attention, next_states, mamba_output)


def solution(mesh):
    return jax.shard_map(
        local,
        mesh=mesh,
        in_specs=(
            P(("groups", "batch"), "seq", None, None),
            P(("groups", "batch"), "seq", None, None),
            P(("groups", "batch"), "seq", None),
            P("groups"),
            P("groups"),
            P(("groups", "batch")),
            P(("groups", "batch"), None, "seq", None, None),
            P(("groups", "batch"), None, None),
            P(("groups", "batch"), None, None),
            P(("groups", "batch"), None, "seq"),
            P(),
            P(("groups", "batch"), "seq"),
            P(("groups", "batch"), "seq"),
            P(("groups", "batch"), "seq"),
            P(("groups", "batch"), None),
            P(("groups", "batch"), None),
            P("seq"),
        ),
        out_specs=(
            P(("groups", "batch"), None, "seq", None, None),
            P(("groups", "batch"), "seq", None),
            P(("groups", "batch"), None, "seq"),
            P(("groups", "batch"), "seq"),
        ),
        check_vma=False,
    )
```

time: 424 us -> 266 us (0.63)
  the two profiles are of different devices: /device:TPU:109 before, /device:TPU:46 now
where the time goes in v2:
time: 266 us; the launch traced here: 265 us
  waiting for transfers between devices  132 us (50%)
  starting transfers between devices  84.5 us (32%)
  local copies, waits for them, and re-layouts  18.7 us (7%)
  other arithmetic  12.4 us (5%)
  Pallas kernels  9.58 us (4%)
  matrix products  6.7 us (3%)
    ppermute x1, waiting for transfers between devices, local(): came_state = lax.ppermute(sent_state.astype(jnp.float16), 'seq', pairs)  62.9 us
    all_to_all x1, starting transfers between devices, local(): lax.all_to_all(jnp.swapaxes(prompt_cache, 0, 1), 'seq', split_axis=0, con...  32.7 us
    ppermute x8, starting transfers between devices, hand_over(): sent = lax.ppermute(outs[0].astype(jnp.float16), 'seq', ahead)  28.7 us
    all_to_all x1, waiting for transfers between devices, local(): lax.all_to_all(jnp.concatenate([sums, extra], axis=1).astype(jnp.float16)...  23.7 us
    ppermute x8, waiting for transfers between devices, hand_over(): sent = lax.ppermute(outs[0].astype(jnp.float16), 'seq', ahead)  21.7 us
    ppermute x7, waiting for transfers between devices, hand_over(): down = lax.ppermute(outs[1].astype(jnp.float16), 'seq', behind)  20.4 us
    all_to_all x1, starting transfers between devices, local(): lax.all_to_all(jnp.concatenate([sums, extra], axis=1).astype(jnp.float16)...  15.8 us
    unnamed x67, local copies, waits for them, and re-layouts  7.94 us
  transfers between devices with their start and end apart: 21, of which 18 were waited for; matrix products, arithmetic and copies ran while one was open for 11% of the time, Pallas kernels for 4%

profile of v2, /device:TPU:46, one launch (start us, length us, event | category | flops | bytes accessed | tf_op | source)
XLA Modules:
  0.0 264.9 jit_solution(6049490615863376713)
XLA Ops:
  2.6 32.7 %all-to-all-start = ((bf16[32,4,8,256]{3,2,1,0:T(8,128)(2,1)}), bf16[32,4,8,256]{3,2,1,0:T(8,128)(2,1)}, u32[]{:S(2)}, u32[]{:S(2)}) async-start(bf16[32,4,8,256]{3,2,1,0:T(8,128)(2,1)} %bitcast.98), calls=%async_computation | async-start | bytes 1048576 | tf_op jit(solution)/shard_map/all_to_all | solution.py:330
  42.2 62.9 %collective-permute-done.1 = f16[4,16,8192]{2,1,0:T(8,128)(2,1)S(1)} collective-permute-done((f16[4,16,8192]{2,1,0:T(8,128)(2,1)}, f16[4,16,8192]{2,1,0:T(8,128)(2,1)S(1)}, u32[]{:S(2)}, u32[]{:S(2)}) %collective-permute-start.1) | collective-permute-done | bytes 1048608 | tf_op jit(solution)/shard_map/ppermute | solution.py:328
  112.9 2.6 collective-permute-start.3
  117.4 3.3 %collective-permute-done.3 = f16[136,512]{1,0:T(8,128)(2,1)S(1)} collective-permute-done((f16[136,512]{1,0:T(8,128)(2,1)S(1)}, f16[136,512]{1,0:T(8,128)(2,1)S(1)}, u32[]{:S(2)}, u32[]{:S(2)}) %collective-permute-start.3) | collective-permute-done | bytes 139296 | tf_op jit(solution)/shard_map/ppermute | solution.py:249
  120.7 4.1 %collective-permute-done.4 = f16[136,512]{1,0:T(8,128)(2,1)S(1)} collective-permute-done((f16[136,512]{1,0:T(8,128)(2,1)S(1)}, f16[136,512]{1,0:T(8,128)(2,1)S(1)}, u32[]{:S(2)}, u32[]{:S(2)}) %collective-permute-start.4) | collective-permute-done | bytes 139296 | tf_op jit(solution)/shard_map/ppermute | solution.py:251
  125.6 3.9 %collective-permute-start.5 = (f16[136,512]{1,0:T(8,128)(2,1)S(1)}, f16[136,512]{1,0:T(8,128)(2,1)S(1)}, u32[]{:S(2)}, u32[]{:S(2)}) collective-permute-start(f16[136,512]{1,0:T(8,128)(2,1)S(1)} %convert_element_type.174), channel_id=1, source_target_pairs={{0,4},{2,6},{4,8},{6,10},{8,12},{10,14},{12,16},{14,18},{16,20},{1... | collective-permute-start | bytes 417800 | tf_op jit(solution)/shard_map/ppermute | solution.py:249
  130.1 4.0 %collective-permute-done.5 = f16[136,512]{1,0:T(8,128)(2,1)S(1)} collective-permute-done((f16[136,512]{1,0:T(8,128)(2,1)S(1)}, f16[136,512]{1,0:T(8,128)(2,1)S(1)}, u32[]{:S(2)}, u32[]{:S(2)}) %collective-permute-start.5) | collective-permute-done | bytes 139296 | tf_op jit(solution)/shard_map/ppermute | solution.py:249
  134.1 2.9 %collective-permute-done.6 = f16[136,512]{1,0:T(8,128)(2,1)S(1)} collective-permute-done((f16[136,512]{1,0:T(8,128)(2,1)S(1)}, f16[136,512]{1,0:T(8,128)(2,1)S(1)}, u32[]{:S(2)}, u32[]{:S(2)}) %collective-permute-start.6) | collective-permute-done | bytes 139296 | tf_op jit(solution)/shard_map/ppermute | solution.py:251
  137.8 3.9 %collective-permute-start.7 = (f16[136,512]{1,0:T(8,128)(2,1)S(1)}, f16[136,512]{1,0:T(8,128)(2,1)S(1)}, u32[]{:S(2)}, u32[]{:S(2)}) collective-permute-start(f16[136,512]{1,0:T(8,128)(2,1)S(1)} %convert_element_type.178), channel_id=1, source_target_pairs={{0,4},{2,6},{4,8},{6,10},{8,12},{10,14},{12,16},{14,18},{16,20},{1... | collective-permute-start | bytes 417800 | tf_op jit(solution)/shard_map/ppermute | solution.py:249
  142.2 3.0 %collective-permute-done.7 = f16[136,512]{1,0:T(8,128)(2,1)S(1)} collective-permute-done((f16[136,512]{1,0:T(8,128)(2,1)S(1)}, f16[136,512]{1,0:T(8,128)(2,1)S(1)}, u32[]{:S(2)}, u32[]{:S(2)}) %collective-permute-start.7) | collective-permute-done | bytes 139296 | tf_op jit(solution)/shard_map/ppermute | solution.py:249
  145.2 2.8 %collective-permute-done.8 = f16[136,512]{1,0:T(8,128)(2,1)S(1)} collective-permute-done((f16[136,512]{1,0:T(8,128)(2,1)S(1)}, f16[136,512]{1,0:T(8,128)(2,1)S(1)}, u32[]{:S(2)}, u32[]{:S(2)}) %collective-permute-start.8) | collective-permute-done | bytes 139296 | tf_op jit(solution)/shard_map/ppermute | solution.py:251
  148.8 4.8 %collective-permute-start.9 = (f16[136,512]{1,0:T(8,128)(2,1)S(1)}, f16[136,512]{1,0:T(8,128)(2,1)S(1)}, u32[]{:S(2)}, u32[]{:S(2)}) collective-permute-start(f16[136,512]{1,0:T(8,128)(2,1)S(1)} %convert_element_type.182), channel_id=1, source_target_pairs={{0,4},{2,6},{4,8},{6,10},{8,12},{10,14},{12,16},{14,18},{16,20},{1... | collective-permute-start | bytes 417800 | tf_op jit(solution)/shard_map/ppermute | solution.py:249
  156.3 5.0 %collective-permute-done.10 = f16[136,512]{1,0:T(8,128)(2,1)S(1)} collective-permute-done((f16[136,512]{1,0:T(8,128)(2,1)S(1)}, f16[136,512]{1,0:T(8,128)(2,1)S(1)}, u32[]{:S(2)}, u32[]{:S(2)}) %collective-permute-start.10) | collective-permute-done | bytes 139296 | tf_op jit(solution)/shard_map/ppermute | solution.py:251
  162.0 2.7 %collective-permute-start.11 = (f16[136,512]{1,0:T(8,128)(2,1)S(1)}, f16[136,512]{1,0:T(8,128)(2,1)S(1)}, u32[]{:S(2)}, u32[]{:S(2)}) collective-permute-start(f16[136,512]{1,0:T(8,128)(2,1)S(1)} %convert_element_type.186), channel_id=1, source_target_pairs={{0,4},{2,6},{4,8},{6,10},{8,12},{10,14},{12,16},{14,18},{16,20},{1... | collective-permute-start | bytes 417800 | tf_op jit(solution)/shard_map/ppermute | solution.py:249
  166.7 4.1 %collective-permute-done.11 = f16[136,512]{1,0:T(8,128)(2,1)S(1)} collective-permute-done((f16[136,512]{1,0:T(8,128)(2,1)S(1)}, f16[136,512]{1,0:T(8,128)(2,1)S(1)}, u32[]{:S(2)}, u32[]{:S(2)}) %collective-permute-start.11) | collective-permute-done | bytes 139296 | tf_op jit(solution)/shard_map/ppermute | solution.py:249
  172.9 4.6 %collective-permute-start.13 = (f16[136,512]{1,0:T(8,128)(2,1)S(1)}, f16[136,512]{1,0:T(8,128)(2,1)S(1)}, u32[]{:S(2)}, u32[]{:S(2)}) collective-permute-start(f16[136,512]{1,0:T(8,128)(2,1)S(1)} %convert_element_type.190), channel_id=1, source_target_pairs={{0,4},{2,6},{4,8},{6,10},{8,12},{10,14},{12,16},{14,18},{16,20},{1... | collective-permute-start | bytes 417800 | tf_op jit(solution)/shard_map/ppermute | solution.py:249
  177.8 4.0 %collective-permute-done.13 = f16[136,512]{1,0:T(8,128)(2,1)S(1)} collective-permute-done((f16[136,512]{1,0:T(8,128)(2,1)S(1)}, f16[136,512]{1,0:T(8,128)(2,1)S(1)}, u32[]{:S(2)}, u32[]{:S(2)}) %collective-permute-start.13) | collective-permute-done | bytes 139296 | tf_op jit(solution)/shard_map/ppermute | solution.py:249
  184.4 4.0 %collective-permute-start.15 = (f16[136,512]{1,0:T(8,128)(2,1)S(1)}, f16[136,512]{1,0:T(8,128)(2,1)S(1)}, u32[]{:S(2)}, u32[]{:S(2)}) collective-permute-start(f16[136,512]{1,0:T(8,128)(2,1)S(1)} %convert_element_type.194), channel_id=1, source_target_pairs={{0,4},{2,6},{4,8},{6,10},{8,12},{10,14},{12,16},{14,18},{16,20},{1... | collective-permute-start | bytes 417800 | tf_op jit(solution)/shard_map/ppermute | solution.py:249
  191.7 2.8 %collective-permute-done.16 = f16[136,512]{1,0:T(8,128)(2,1)S(1)} collective-permute-done((f16[136,512]{1,0:T(8,128)(2,1)S(1)}, f16[136,512]{1,0:T(8,128)(2,1)S(1)}, u32[]{:S(2)}, u32[]{:S(2)}) %collective-permute-start.16) | collective-permute-done | bytes 139296 | tf_op jit(solution)/shard_map/ppermute | solution.py:251
  199.7 2.9 %fusion.30 = f32[8,32,2048]{2,0,1:T(8,128)} fusion(bf16[32,4,2048]{2,1,0:T(4,128)(2,1)} %reshape.278, pred[8,4]{0,1:T(4,128)(4,1)S(1)} %get-tuple-element.55), kind=kOutput, calls=%fused_computation.67 | convolution fusion | flops 4194304 | bytes 2621472 | tf_op jit(solution)/shard_map/rp,ipx->rix/dot_general | solution.py:347
  202.6 2.2 reshape.279
  204.8 2.4 fusion
  212.7 15.8 %all-to-all-start.1 = ((f16[32,17,128]{2,1,0:T(8,128)(2,1)}), f16[32,17,128]{2,1,0:T(8,128)(2,1)S(1)}, u32[]{:S(2)}, u32[]{:S(2)}) async-start(f16[32,17,128]{2,1,0:T(8,128)(2,1)} %copy.61), calls=%async_computation.1 | async-start | bytes 393216 | tf_op jit(solution)/shard_map/all_to_all | solution.py:393
  239.1 23.7 %all-to-all-done.1 = f16[32,17,128]{2,1,0:T(8,128)(2,1)S(1)} async-done(((f16[32,17,128]{2,1,0:T(8,128)(2,1)}), f16[32,17,128]{2,1,0:T(8,128)(2,1)S(1)}, u32[]{:S(2)}, u32[]{:S(2)}) %all-to-all-start.1) | async-done | bytes 139296 | tf_op jit(solution)/shard_map/all_to_all | solution.py:393
  (181 shorter events, 58.5 us)
Async XLA Ops:
  0.6 208.0 %copy-start = (bf16[8,64,128]{2,1,0:T(8,128)(2,1)S(1)}, bf16[8,64,128]{2,1,0:T(8,128)(2,1)}, u32[]{:S(2)}) copy-start(bf16[8,64,128]{2,1,0:T(8,128)(2,1)} %param.25) | copy-start | bytes 393220
  0.6 34.7 %copy-start.8 = (f32[4,1,16384]{2,1,0:T(1,128)S(1)}, f32[4,1,16384]{2,1,0:T(1,128)}, u32[]{:S(2)}) copy-start(f32[4,1,16384]{2,1,0:T(1,128)} %param.19) | copy-start | bytes 786436
  0.7 34.8 %copy-start.25 = (s32[8]{0:T(128)S(1)}, s32[8]{0:T(128)}, u32[]{:S(2)}) copy-start(s32[8]{0:T(128)} %param.20) | copy-start | bytes 100
  2.6 186.2 %all-to-all-start = ((bf16[32,4,8,256]{3,2,1,0:T(8,128)(2,1)}), bf16[32,4,8,256]{3,2,1,0:T(8,128)(2,1)}, u32[]{:S(2)}, u32[]{:S(2)}) async-start(bf16[32,4,8,256]{3,2,1,0:T(8,128)(2,1)} %bitcast.98), calls=%async_computation | async-start | bytes 1048576 | tf_op jit(solution)/shard_map/all_to_all | solution.py:330
  40.0 65.1 %collective-permute-start.1 = (f16[4,16,8192]{2,1,0:T(8,128)(2,1)}, f16[4,16,8192]{2,1,0:T(8,128)(2,1)S(1)}, u32[]{:S(2)}, u32[]{:S(2)}) collective-permute-start(f16[4,16,8192]{2,1,0:T(8,128)(2,1)} %convert_element_type.168), channel_id=1, source_target_pairs={{0,2},{2,0},{4,6},{6,4},{8,10},{10,8},{12,14},{14,12},{16,18},{18,... | collective-permute-start | bytes 3145736 | tf_op jit(solution)/shard_map/ppermute | solution.py:328
  41.4 65.6 %collective-permute-start.2 = (f32[4,8192]{1,0:T(4,128)S(1)}, f32[4,8192]{1,0:T(4,128)S(1)}, u32[]{:S(2)}, u32[]{:S(2)}) collective-permute-start(f32[4,8192]{1,0:T(4,128)S(1)} %get-tuple-element.24), channel_id=1, source_target_pairs={{0,2},{2,0},{4,6},{6,4},{8,10},{10,8},{12,14},{14,12},{16,18},{18,... | collective-permute-start | bytes 393224 | tf_op jit(solution)/shard_map/ppermute | solution.py:329
  112.9 7.7 %collective-permute-start.3 = (f16[136,512]{1,0:T(8,128)(2,1)S(1)}, f16[136,512]{1,0:T(8,128)(2,1)S(1)}, u32[]{:S(2)}, u32[]{:S(2)}) collective-permute-start(f16[136,512]{1,0:T(8,128)(2,1)S(1)} %convert_element_type.170), channel_id=1, source_target_pairs={{0,4},{2,6},{4,8},{6,10},{8,12},{10,14},{12,16},{14,18},{16,20},{1... | collective-permute-start | bytes 417800 | tf_op jit(solution)/shard_map/ppermute | solution.py:249
  115.5 9.3 %collective-permute-start.4 = (f16[136,512]{1,0:T(8,128)(2,1)S(1)}, f16[136,512]{1,0:T(8,128)(2,1)S(1)}, u32[]{:S(2)}, u32[]{:S(2)}) collective-permute-start(f16[136,512]{1,0:T(8,128)(2,1)S(1)} %convert_element_type.172), channel_id=1, source_target_pairs={{0,60},{2,62},{4,0},{6,2},{8,4},{10,6},{12,8},{14,10},{16,12},{18,... | collective-permute-start | bytes 417800 | tf_op jit(solution)/shard_map/ppermute | solution.py:251
  125.6 8.5 %collective-permute-start.5 = (f16[136,512]{1,0:T(8,128)(2,1)S(1)}, f16[136,512]{1,0:T(8,128)(2,1)S(1)}, u32[]{:S(2)}, u32[]{:S(2)}) collective-permute-start(f16[136,512]{1,0:T(8,128)(2,1)S(1)} %convert_element_type.174), channel_id=1, source_target_pairs={{0,4},{2,6},{4,8},{6,10},{8,12},{10,14},{12,16},{14,18},{16,20},{1... | collective-permute-start | bytes 417800 | tf_op jit(solution)/shard_map/ppermute | solution.py:249
  129.6 7.4 %collective-permute-start.6 = (f16[136,512]{1,0:T(8,128)(2,1)S(1)}, f16[136,512]{1,0:T(8,128)(2,1)S(1)}, u32[]{:S(2)}, u32[]{:S(2)}) collective-permute-start(f16[136,512]{1,0:T(8,128)(2,1)S(1)} %convert_element_type.176), channel_id=1, source_target_pairs={{0,60},{2,62},{4,0},{6,2},{8,4},{10,6},{12,8},{14,10},{16,12},{18,... | collective-permute-start | bytes 417800 | tf_op jit(solution)/shard_map/ppermute | solution.py:251
  137.8 7.5 %collective-permute-start.7 = (f16[136,512]{1,0:T(8,128)(2,1)S(1)}, f16[136,512]{1,0:T(8,128)(2,1)S(1)}, u32[]{:S(2)}, u32[]{:S(2)}) collective-permute-start(f16[136,512]{1,0:T(8,128)(2,1)S(1)} %convert_element_type.178), channel_id=1, source_target_pairs={{0,4},{2,6},{4,8},{6,10},{8,12},{10,14},{12,16},{14,18},{16,20},{1... | collective-permute-start | bytes 417800 | tf_op jit(solution)/shard_map/ppermute | solution.py:249
  141.7 6.4 %collective-permute-start.8 = (f16[136,512]{1,0:T(8,128)(2,1)S(1)}, f16[136,512]{1,0:T(8,128)(2,1)S(1)}, u32[]{:S(2)}, u32[]{:S(2)}) collective-permute-start(f16[136,512]{1,0:T(8,128)(2,1)S(1)} %convert_element_type.180), channel_id=1, source_target_pairs={{0,60},{2,62},{4,0},{6,2},{8,4},{10,6},{12,8},{14,10},{16,12},{18,... | collective-permute-start | bytes 417800 | tf_op jit(solution)/shard_map/ppermute | solution.py:251
  148.8 7.4 %collective-permute-start.9 = (f16[136,512]{1,0:T(8,128)(2,1)S(1)}, f16[136,512]{1,0:T(8,128)(2,1)S(1)}, u32[]{:S(2)}, u32[]{:S(2)}) collective-permute-start(f16[136,512]{1,0:T(8,128)(2,1)S(1)} %convert_element_type.182), channel_id=1, source_target_pairs={{0,4},{2,6},{4,8},{6,10},{8,12},{10,14},{12,16},{14,18},{16,20},{1... | collective-permute-start | bytes 417800 | tf_op jit(solution)/shard_map/ppermute | solution.py:249
  153.7 7.6 %collective-permute-start.10 = (f16[136,512]{1,0:T(8,128)(2,1)S(1)}, f16[136,512]{1,0:T(8,128)(2,1)S(1)}, u32[]{:S(2)}, u32[]{:S(2)}) collective-permute-start(f16[136,512]{1,0:T(8,128)(2,1)S(1)} %convert_element_type.184), channel_id=1, source_target_pairs={{0,60},{2,62},{4,0},{6,2},{8,4},{10,6},{12,8},{14,10},{16,12},{18,... | collective-permute-start | bytes 417800 | tf_op jit(solution)/shard_map/ppermute | solution.py:251
  162.0 8.8 %collective-permute-start.11 = (f16[136,512]{1,0:T(8,128)(2,1)S(1)}, f16[136,512]{1,0:T(8,128)(2,1)S(1)}, u32[]{:S(2)}, u32[]{:S(2)}) collective-permute-start(f16[136,512]{1,0:T(8,128)(2,1)S(1)} %convert_element_type.186), channel_id=1, source_target_pairs={{0,4},{2,6},{4,8},{6,10},{8,12},{10,14},{12,16},{14,18},{16,20},{1... | collective-permute-start | bytes 417800 | tf_op jit(solution)/shard_map/ppermute | solution.py:249
  164.8 7.3 %collective-permute-start.12 = (f16[136,512]{1,0:T(8,128)(2,1)S(1)}, f16[136,512]{1,0:T(8,128)(2,1)S(1)}, u32[]{:S(2)}, u32[]{:S(2)}) collective-permute-start(f16[136,512]{1,0:T(8,128)(2,1)S(1)} %convert_element_type.188), channel_id=1, source_target_pairs={{0,60},{2,62},{4,0},{6,2},{8,4},{10,6},{12,8},{14,10},{16,12},{18,... | collective-permute-start | bytes 417800 | tf_op jit(solution)/shard_map/ppermute | solution.py:251
  172.9 9.0 %collective-permute-start.13 = (f16[136,512]{1,0:T(8,128)(2,1)S(1)}, f16[136,512]{1,0:T(8,128)(2,1)S(1)}, u32[]{:S(2)}, u32[]{:S(2)}) collective-permute-start(f16[136,512]{1,0:T(8,128)(2,1)S(1)} %convert_element_type.190), channel_id=1, source_target_pairs={{0,4},{2,6},{4,8},{6,10},{8,12},{10,14},{12,16},{14,18},{16,20},{1... | collective-permute-start | bytes 417800 | tf_op jit(solution)/shard_map/ppermute | solution.py:249
  177.5 6.1 %collective-permute-start.14 = (f16[136,512]{1,0:T(8,128)(2,1)S(1)}, f16[136,512]{1,0:T(8,128)(2,1)S(1)}, u32[]{:S(2)}, u32[]{:S(2)}) collective-permute-start(f16[136,512]{1,0:T(8,128)(2,1)S(1)} %convert_element_type.192), channel_id=1, source_target_pairs={{0,60},{2,62},{4,0},{6,2},{8,4},{10,6},{12,8},{14,10},{16,12},{18,... | collective-permute-start | bytes 417800 | tf_op jit(solution)/shard_map/ppermute | solution.py:251
  184.4 7.3 %collective-permute-start.15 = (f16[136,512]{1,0:T(8,128)(2,1)S(1)}, f16[136,512]{1,0:T(8,128)(2,1)S(1)}, u32[]{:S(2)}, u32[]{:S(2)}) collective-permute-start(f16[136,512]{1,0:T(8,128)(2,1)S(1)} %convert_element_type.194), channel_id=1, source_target_pairs={{0,4},{2,6},{4,8},{6,10},{8,12},{10,14},{12,16},{14,18},{16,20},{1... | collective-permute-start | bytes 417800 | tf_op jit(solution)/shard_map/ppermute | solution.py:249
  188.4 6.1 %collective-permute-start.16 = (f16[136,512]{1,0:T(8,128)(2,1)S(1)}, f16[136,512]{1,0:T(8,128)(2,1)S(1)}, u32[]{:S(2)}, u32[]{:S(2)}) collective-permute-start(f16[136,512]{1,0:T(8,128)(2,1)S(1)} %convert_element_type.196), channel_id=1, source_target_pairs={{0,60},{2,62},{4,0},{6,2},{8,4},{10,6},{12,8},{14,10},{16,12},{18,... | collective-permute-start | bytes 417800 | tf_op jit(solution)/shard_map/ppermute | solution.py:251
  188.8 13.8 %collective-permute-start = (bf16[32,4,8,256]{3,2,1,0:T(8,128)(2,1)}, bf16[32,4,8,256]{3,2,1,0:T(8,128)(2,1)}, u32[]{:S(2)}, u32[]{:S(2)}) collective-permute-start(bf16[32,4,8,256]{3,2,1,0:T(8,128)(2,1)} %all-to-all-done), channel_id=1, source_target_pairs={{0,1},{1,0},{2,3},{3,2},{4,5},{5,4},{6,7},{7,6},{8,9},{9,8},{10,11... | collective-permute-start | bytes 1572872 | tf_op jit(solution)/shard_map/ppermute | solution.py:282
  195.2 37.3 %collective-permute-start.17 = (f16[136,512]{1,0:T(8,128)(2,1)S(1)}, f16[136,512]{1,0:T(8,128)(2,1)}, u32[]{:S(2)}, u32[]{:S(2)}) collective-permute-start(f16[136,512]{1,0:T(8,128)(2,1)S(1)} %convert_element_type.198), channel_id=1, source_target_pairs={{0,4},{2,6},{4,8},{6,10},{8,12},{10,14},{12,16},{14,18},{16,20},{1... | collective-permute-start | bytes 417800 | tf_op jit(solution)/shard_map/ppermute | solution.py:249
  212.7 50.1 %all-to-all-start.1 = ((f16[32,17,128]{2,1,0:T(8,128)(2,1)}), f16[32,17,128]{2,1,0:T(8,128)(2,1)S(1)}, u32[]{:S(2)}, u32[]{:S(2)}) async-start(f16[32,17,128]{2,1,0:T(8,128)(2,1)} %copy.61), calls=%async_computation.1 | async-start | bytes 393216 | tf_op jit(solution)/shard_map/all_to_all | solution.py:393
  234.4 1.5 collective-permute-start.18
  (29 other events, 100.2 us)

commit v3 on v2

--- a/solution.py
+++ b/solution.py
@@ -29,37 +29,41 @@
     return pl.BlockSpec(memory_space=pltpu.VMEM)
 
 
-def pick_kernel(flags, usable, state_in, step_in, state_out, step_out, *, width):
-    count = state_in.shape[0]
-    for q in range(PAIRS_A_STEP):
-        source = pl.ds(pl.multiple_of(2 * q * width + flags[0] * width, 128), width)
-        target = pl.ds(q * width, width)
-        for p in range(count):
-            use = usable[p]
-            state_out[p, :, target] = state_in[p, :, source] * (use * STATE_SCALE)
-            step_out[p : p + 1, target] = step_in[p : p + 1, source] * use
-
-
-def fold_kernel(
-    flags, usable, state_in, step_in, rate_in, came_state, came_step, state_out, step_out, rate_out,
+def pick_kernel(
+    flags, usable, state_in, step_in, rate_in, sent_state, sent_step, own_state, own_step, own_rate,
     *, width,
 ):
     count = state_in.shape[0]
-    older = flags[1] == 1
     for q in range(PAIRS_A_STEP):
-        source = pl.ds(pl.multiple_of(2 * q * width + flags[0] * width, 128), width)
+        own = pl.ds(pl.multiple_of((2 * q + flags[0]) * width, 128), width)
+        other = pl.ds(pl.multiple_of((2 * q + flags[1]) * width, 128), width)
         target = pl.ds(q * width, width)
-        rate = rate_in[:, source]
-        rate_out[:, target] = rate
+        own_rate[:, target] = rate_in[:, own]
         for p in range(count):
             use = usable[p]
-            own = state_in[p, :, source] * (use * STATE_SCALE)
-            step = step_in[p : p + 1, source] * use
-            came, came_by = came_state[p, :, target], came_step[p : p + 1, target]
+            sent_state[p, :, target] = state_in[p, :, other] * (use * STATE_SCALE)
+            own_state[p, :, target] = state_in[p, :, own] * (use * STATE_SCALE)
+            sent_step[p : p + 1, target] = step_in[p, :, other] * use
+            own_step[p : p + 1, target] = step_in[p, :, own] * use
+
+
+def fold_kernel(
+    flags, own_state, own_step, rates, came_state, came_step, state_out, step_out, *, width
+):
+    count = own_state.shape[0]
+    older = flags[0] == 0
+
+    @pl.loop(0, own_state.shape[2] // width)
+    def _(q):
+        at = pl.ds(pl.multiple_of(q * width, 128), width)
+        rate = rates[:, at]
+        for p in range(count):
+            own, came = own_state[p, :, at], came_state[p, :, at]
+            step, came_by = own_step[p : p + 1, at], came_step[p : p + 1, at]
             early, late = jnp.where(older, own, came), jnp.where(older, came, own)
             late_by = jnp.where(older, came_by, step)
-            state_out[p, :, target] = jnp.exp(-rate * late_by) * early + late
-            step_out[p : p + 1, target] = step + came_by
+            state_out[p, :, at] = jnp.exp(-rate * late_by) * early + late
+            step_out[p : p + 1, at] = step + came_by
 
 
 def hop_kernel(
@@ -73,7 +77,7 @@
     up_wrapped, down_wrapped = flags[4] == 1, flags[5] == 1
     up_rate, down_rate = rates[:, up_at], rates[:, down_at]
 
-    @pl.loop(0, count)
+    @pl.loop(0, count, unroll=True)
     def _(p):
         here = pl.ds(pl.multiple_of(p * state, state), state)
         there = pl.ds(pl.multiple_of(rows + p * state, state), state)
@@ -120,7 +124,7 @@
     up_wrapped, down_wrapped = flags[4] == 1, flags[5] == 1
     rate = rates[:, at]
 
-    @pl.loop(0, count)
+    @pl.loop(0, count, unroll=True)
     def _(p):
         here = pl.ds(pl.multiple_of(p * state, state), state)
         there = pl.ds(pl.multiple_of(rows + p * state, state), state)
@@ -146,66 +150,56 @@
     return jnp.stack([jnp.asarray(v) for v in values]).astype(jnp.int32)
 
 
-def picked_for_pair(states, steps, usable, seq_index, width):
+def picked_for_pair(states, steps, rates, usable, seq_index, width):
     count, state, channels = states.shape
     wide = PAIRS_A_STEP * width
+    blocks = (
+        pl.BlockSpec((count, state, wide), lambda n: (0, 0, n)),
+        pl.BlockSpec((count, wide), lambda n: (0, n)),
+    )
+    shapes = (
+        jax.ShapeDtypeStruct((count, state, channels // 2), jnp.float32),
+        jax.ShapeDtypeStruct((count, channels // 2), jnp.float32),
+    )
     return pl.pallas_call(
         functools.partial(pick_kernel, width=width),
         grid=(channels // (2 * wide),),
-        out_shape=(
-            jax.ShapeDtypeStruct((count, state, channels // 2), jnp.float32),
-            jax.ShapeDtypeStruct((count, channels // 2), jnp.float32),
-        ),
+        out_shape=shapes
+        + shapes
+        + (jax.ShapeDtypeStruct((state, channels // 2), jnp.float32),),
         in_specs=[
             smem(),
             smem(),
             pl.BlockSpec((count, state, 2 * wide), lambda n: (0, 0, n)),
-            pl.BlockSpec((count, 2 * wide), lambda n: (0, n)),
+            pl.BlockSpec((count, 1, 2 * wide), lambda n: (0, 0, n)),
+            pl.BlockSpec((state, 2 * wide), lambda n: (0, n)),
         ],
-        out_specs=(
-            pl.BlockSpec((count, state, wide), lambda n: (0, 0, n)),
-            pl.BlockSpec((count, wide), lambda n: (0, n)),
+        out_specs=blocks + blocks + (pl.BlockSpec((state, wide), lambda n: (0, n)),),
+        cost_estimate=pl.CostEstimate(
+            flops=states.size, bytes_accessed=8 * states.size, transcendentals=0
         ),
-        cost_estimate=pl.CostEstimate(
-            flops=states.size, bytes_accessed=6 * states.size, transcendentals=0
-        ),
-        compiler_params=pltpu.CompilerParams(vmem_limit_bytes=2 * KERNEL_VMEM),
+        compiler_params=pltpu.CompilerParams(vmem_limit_bytes=7 * KERNEL_VMEM),
         name="pick_for_pair",
-    )(numbers(1 - seq_index % 2), usable, states, steps)
-
-
-def folded_pair(states, steps, rates, usable, came_state, came_step, seq_index, width):
-    count, state, channels = states.shape
-    wide = PAIRS_A_STEP * width
-    parity = seq_index % 2
+    )(numbers(seq_index % 2, 1 - seq_index % 2), usable, states, steps, rates)
+
+
+def folded_pair(own_state, own_step, rates, came_state, came_step, seq_index, width):
     return pl.pallas_call(
         functools.partial(fold_kernel, width=width),
-        grid=(channels // (2 * wide),),
         out_shape=(
-            jax.ShapeDtypeStruct((count, state, channels // 2), jnp.float32),
-            jax.ShapeDtypeStruct((count, channels // 2), jnp.float32),
-            jax.ShapeDtypeStruct((state, channels // 2), jnp.float32),
+            jax.ShapeDtypeStruct(own_state.shape, jnp.float32),
+            jax.ShapeDtypeStruct(own_step.shape, jnp.float32),
         ),
-        in_specs=[
-            smem(),
-            smem(),
-            pl.BlockSpec((count, state, 2 * wide), lambda n: (0, 0, n)),
-            pl.BlockSpec((count, 2 * wide), lambda n: (0, n)),
-            pl.BlockSpec((state, 2 * wide), lambda n: (0, n)),
-            pl.BlockSpec((count, state, wide), lambda n: (0, 0, n)),
-            pl.BlockSpec((count, wide), lambda n: (0, n)),
-        ],
-        out_specs=(
-            pl.BlockSpec((count, state, wide), lambda n: (0, 0, n)),
-            pl.BlockSpec((count, wide), lambda n: (0, n)),
-            pl.BlockSpec((state, wide), lambda n: (0, n)),
+        in_specs=[smem()] + [vmem()] * 5,
+        out_specs=(vmem(), vmem()),
+        cost_estimate=pl.CostEstimate(
+            flops=4 * own_state.size,
+            bytes_accessed=12 * own_state.size,
+            transcendentals=own_state.size,
         ),
-        cost_estimate=pl.CostEstimate(
-            flops=4 * states.size, bytes_accessed=10 * states.size, transcendentals=states.size
-        ),
-        compiler_params=pltpu.CompilerParams(vmem_limit_bytes=2 * KERNEL_VMEM),
+        compiler_params=pltpu.CompilerParams(vmem_limit_bytes=KERNEL_VMEM),
         name="fold_pair",
-    )(numbers(parity, parity == 0), usable, states, steps, rates, came_state, came_step)
+    )(numbers(seq_index % 2), own_state, own_step, rates, came_state, came_step)
 
 
 def hand_over(states, steps, rates, width, nodes, node):
@@ -322,25 +316,25 @@
     own_lengths = lax.dynamic_slice_in_dim(prompt_lengths, own_at, local_prompts)
     usable = (seq_index * block_len < own_lengths).astype(jnp.float32)
 
-    states, steps = prompt_states[:, 0], block_steps[:, 0]
     pairs = [(k, k ^ 1) for k in range(seq_count)]
-    sent_state, sent_step = picked_for_pair(states, steps, usable, seq_index, local_channels)
+    sent_state, sent_step, own_state, own_step, rates = picked_for_pair(
+        prompt_states[:, 0], block_steps, decay_rates, usable, seq_index, local_channels
+    )
     came_state = lax.ppermute(sent_state.astype(jnp.float16), "seq", pairs)
     came_step = lax.ppermute(sent_step, "seq", pairs)
     moved = lax.all_to_all(
         jnp.swapaxes(prompt_cache, 0, 1), "seq", split_axis=0, concat_axis=0, tiled=True
     )
     folded = folded_pair(
-        states,
-        steps,
-        decay_rates,
-        usable,
+        own_state,
+        own_step,
+        rates,
         came_state.astype(jnp.float32),
         came_step,
         seq_index,
         local_channels,
     )
-    handed = hand_over(*folded, local_channels, seq_count // 2, seq_index // 2)
+    handed = hand_over(*folded, rates, local_channels, seq_count // 2, seq_index // 2)
 
     peer_moved = swapped(moved)
     flat = (block_len, local_prompts, kv_heads * kv_width)

time: 266 us -> 262 us (0.985)
  the two profiles are of different devices: /device:TPU:46 before, /device:TPU:38 now
where the time goes in v3:
time: 262 us; the launch traced here: 261 us
  waiting for transfers between devices  129 us (49%)
  starting transfers between devices  84.1 us (32%)
  local copies, waits for them, and re-layouts  14.5 us (6%)
  other arithmetic  14.1 us (5%)
  Pallas kernels  12 us (5%)
  matrix products  6.7 us (3%)
    ppermute x1, waiting for transfers between devices, local(): came_state = lax.ppermute(sent_state.astype(jnp.float16), 'seq', pairs)  59.4 us
    all_to_all x1, starting transfers between devices, local(): lax.all_to_all(jnp.swapaxes(prompt_cache, 0, 1), 'seq', split_axis=0, con...  32.7 us
    ppermute x8, starting transfers between devices, hand_over(): sent = lax.ppermute(outs[0].astype(jnp.float16), 'seq', ahead)  28.5 us
    all_to_all x1, waiting for transfers between devices, local(): lax.all_to_all(jnp.concatenate([sums, extra], axis=1).astype(jnp.float16)...  23.8 us
    ppermute x8, waiting for transfers between devices, hand_over(): sent = lax.ppermute(outs[0].astype(jnp.float16), 'seq', ahead)  21.9 us
    ppermute x7, waiting for transfers between devices, hand_over(): down = lax.ppermute(outs[1].astype(jnp.float16), 'seq', behind)  20.5 us
    all_to_all x1, starting transfers between devices, local(): lax.all_to_all(jnp.concatenate([sums, extra], axis=1).astype(jnp.float16)...  15.5 us
    pallas_call x8, Pallas kernels, hand_over(): pl.pallas_call(functools.partial(hop_kernel, width=width, initial=hop ==...  5.37 us
  transfers between devices with their start and end apart: 21, of which 18 were waited for; matrix products, arithmetic and copies ran while one was open for 11% of the time, Pallas kernels for 5%

profile of v3, /device:TPU:38, one launch (start us, length us, event | category | flops | bytes accessed | tf_op | source)
XLA Modules:
  0.0 261.3 jit_solution(11645892523318664077)
XLA Ops:
  2.6 32.7 %all-to-all-start = ((bf16[32,4,8,256]{3,2,1,0:T(8,128)(2,1)}), bf16[32,4,8,256]{3,2,1,0:T(8,128)(2,1)}, u32[]{:S(2)}, u32[]{:S(2)}) async-start(bf16[32,4,8,256]{3,2,1,0:T(8,128)(2,1)} %bitcast.95), calls=%async_computation | async-start | bytes 1048576 | tf_op jit(solution)/shard_map/all_to_all | solution.py:325
  36.5 5.2 %pick_for_pair.1 = (f32[4,16,8192]{2,1,0:T(8,128)}, f32[4,8192]{1,0:T(4,128)}, f32[4,16,8192]{2,1,0:T(8,128)}, f32[4,8192]{1,0:T(4,128)}, f32[16,8192]{1,0:T(8,128)}) custom-call(s32[2]{0:T(128)} %pad_add_fusion.flags, f32[4]{0:T(128)} %compare_convert_fusion.usable, f32[4,16,16384]{2,1,0:T(8,128)} %bitcast.98, f32[4,1,16384]{2,1,0:T(1,128)} %step_in.1, ...), custom_call_target="tpu_custom_call" | custom-call | flops 1048576 | bytes 8388608 | tf_op jit(solution)/shard_map/pick_for_pair/pallas_call | solution.py:164
  45.7 59.4 %collective-permute-done.1 = f16[4,16,8192]{2,1,0:T(8,128)(2,1)S(1)} collective-permute-done((f16[4,16,8192]{2,1,0:T(8,128)(2,1)S(1)}, f16[4,16,8192]{2,1,0:T(8,128)(2,1)S(1)}, u32[]{:S(2)}, u32[]{:S(2)}) %collective-permute-start.1) | collective-permute-done | bytes 1048608 | tf_op jit(solution)/shard_map/ppermute | solution.py:323
  109.9 2.6 collective-permute-start.3
  114.3 3.3 %collective-permute-done.3 = f16[136,512]{1,0:T(8,128)(2,1)S(1)} collective-permute-done((f16[136,512]{1,0:T(8,128)(2,1)S(1)}, f16[136,512]{1,0:T(8,128)(2,1)S(1)}, u32[]{:S(2)}, u32[]{:S(2)}) %collective-permute-start.3) | collective-permute-done | bytes 139296 | tf_op jit(solution)/shard_map/ppermute | solution.py:243
  117.6 4.1 %collective-permute-done.4 = f16[136,512]{1,0:T(8,128)(2,1)S(1)} collective-permute-done((f16[136,512]{1,0:T(8,128)(2,1)S(1)}, f16[136,512]{1,0:T(8,128)(2,1)S(1)}, u32[]{:S(2)}, u32[]{:S(2)}) %collective-permute-start.4) | collective-permute-done | bytes 139296 | tf_op jit(solution)/shard_map/ppermute | solution.py:245
  122.5 3.9 %collective-permute-start.5 = (f16[136,512]{1,0:T(8,128)(2,1)S(1)}, f16[136,512]{1,0:T(8,128)(2,1)S(1)}, u32[]{:S(2)}, u32[]{:S(2)}) collective-permute-start(f16[136,512]{1,0:T(8,128)(2,1)S(1)} %convert_element_type.173), channel_id=1, source_target_pairs={{0,4},{2,6},{4,8},{6,10},{8,12},{10,14},{12,16},{14,18},{16,20},{1... | collective-permute-start | bytes 417800 | tf_op jit(solution)/shard_map/ppermute | solution.py:243
  127.0 4.0 %collective-permute-done.5 = f16[136,512]{1,0:T(8,128)(2,1)S(1)} collective-permute-done((f16[136,512]{1,0:T(8,128)(2,1)S(1)}, f16[136,512]{1,0:T(8,128)(2,1)S(1)}, u32[]{:S(2)}, u32[]{:S(2)}) %collective-permute-start.5) | collective-permute-done | bytes 139296 | tf_op jit(solution)/shard_map/ppermute | solution.py:243
  131.0 2.8 %collective-permute-done.6 = f16[136,512]{1,0:T(8,128)(2,1)S(1)} collective-permute-done((f16[136,512]{1,0:T(8,128)(2,1)S(1)}, f16[136,512]{1,0:T(8,128)(2,1)S(1)}, u32[]{:S(2)}, u32[]{:S(2)}) %collective-permute-start.6) | collective-permute-done | bytes 139296 | tf_op jit(solution)/shard_map/ppermute | solution.py:245
  134.6 3.9 %collective-permute-start.7 = (f16[136,512]{1,0:T(8,128)(2,1)S(1)}, f16[136,512]{1,0:T(8,128)(2,1)S(1)}, u32[]{:S(2)}, u32[]{:S(2)}) collective-permute-start(f16[136,512]{1,0:T(8,128)(2,1)S(1)} %convert_element_type.177), channel_id=1, source_target_pairs={{0,4},{2,6},{4,8},{6,10},{8,12},{10,14},{12,16},{14,18},{16,20},{1... | collective-permute-start | bytes 417800 | tf_op jit(solution)/shard_map/ppermute | solution.py:243
  139.1 3.0 %collective-permute-done.7 = f16[136,512]{1,0:T(8,128)(2,1)S(1)} collective-permute-done((f16[136,512]{1,0:T(8,128)(2,1)S(1)}, f16[136,512]{1,0:T(8,128)(2,1)S(1)}, u32[]{:S(2)}, u32[]{:S(2)}) %collective-permute-start.7) | collective-permute-done | bytes 139296 | tf_op jit(solution)/shard_map/ppermute | solution.py:243
  142.1 2.8 %collective-permute-done.8 = f16[136,512]{1,0:T(8,128)(2,1)S(1)} collective-permute-done((f16[136,512]{1,0:T(8,128)(2,1)S(1)}, f16[136,512]{1,0:T(8,128)(2,1)S(1)}, u32[]{:S(2)}, u32[]{:S(2)}) %collective-permute-start.8) | collective-permute-done | bytes 139296 | tf_op jit(solution)/shard_map/ppermute | solution.py:245
  145.6 4.8 %collective-permute-start.9 = (f16[136,512]{1,0:T(8,128)(2,1)S(1)}, f16[136,512]{1,0:T(8,128)(2,1)S(1)}, u32[]{:S(2)}, u32[]{:S(2)}) collective-permute-start(f16[136,512]{1,0:T(8,128)(2,1)S(1)} %convert_element_type.181), channel_id=1, source_target_pairs={{0,4},{2,6},{4,8},{6,10},{8,12},{10,14},{12,16},{14,18},{16,20},{1... | collective-permute-start | bytes 417800 | tf_op jit(solution)/shard_map/ppermute | solution.py:243
  153.0 4.9 %collective-permute-done.10 = f16[136,512]{1,0:T(8,128)(2,1)S(1)} collective-permute-done((f16[136,512]{1,0:T(8,128)(2,1)S(1)}, f16[136,512]{1,0:T(8,128)(2,1)S(1)}, u32[]{:S(2)}, u32[]{:S(2)}) %collective-permute-start.10) | collective-permute-done | bytes 139296 | tf_op jit(solution)/shard_map/ppermute | solution.py:245
  158.7 2.8 %collective-permute-start.11 = (f16[136,512]{1,0:T(8,128)(2,1)S(1)}, f16[136,512]{1,0:T(8,128)(2,1)S(1)}, u32[]{:S(2)}, u32[]{:S(2)}) collective-permute-start(f16[136,512]{1,0:T(8,128)(2,1)S(1)} %convert_element_type.185), channel_id=1, source_target_pairs={{0,4},{2,6},{4,8},{6,10},{8,12},{10,14},{12,16},{14,18},{16,20},{1... | collective-permute-start | bytes 417800 | tf_op jit(solution)/shard_map/ppermute | solution.py:243
  163.4 4.1 %collective-permute-done.11 = f16[136,512]{1,0:T(8,128)(2,1)S(1)} collective-permute-done((f16[136,512]{1,0:T(8,128)(2,1)S(1)}, f16[136,512]{1,0:T(8,128)(2,1)S(1)}, u32[]{:S(2)}, u32[]{:S(2)}) %collective-permute-start.11) | collective-permute-done | bytes 139296 | tf_op jit(solution)/shard_map/ppermute | solution.py:243
  169.9 4.3 %collective-permute-start.13 = (f16[136,512]{1,0:T(8,128)(2,1)S(1)}, f16[136,512]{1,0:T(8,128)(2,1)S(1)}, u32[]{:S(2)}, u32[]{:S(2)}) collective-permute-start(f16[136,512]{1,0:T(8,128)(2,1)S(1)} %convert_element_type.189), channel_id=1, source_target_pairs={{0,4},{2,6},{4,8},{6,10},{8,12},{10,14},{12,16},{14,18},{16,20},{1... | collective-permute-start | bytes 417800 | tf_op jit(solution)/shard_map/ppermute | solution.py:243
  174.5 4.2 %collective-permute-done.13 = f16[136,512]{1,0:T(8,128)(2,1)S(1)} collective-permute-done((f16[136,512]{1,0:T(8,128)(2,1)S(1)}, f16[136,512]{1,0:T(8,128)(2,1)S(1)}, u32[]{:S(2)}, u32[]{:S(2)}) %collective-permute-start.13) | collective-permute-done | bytes 139296 | tf_op jit(solution)/shard_map/ppermute | solution.py:243
  181.1 4.0 %collective-permute-start.15 = (f16[136,512]{1,0:T(8,128)(2,1)S(1)}, f16[136,512]{1,0:T(8,128)(2,1)S(1)}, u32[]{:S(2)}, u32[]{:S(2)}) collective-permute-start(f16[136,512]{1,0:T(8,128)(2,1)S(1)} %convert_element_type.193), channel_id=1, source_target_pairs={{0,4},{2,6},{4,8},{6,10},{8,12},{10,14},{12,16},{14,18},{16,20},{1... | collective-permute-start | bytes 417800 | tf_op jit(solution)/shard_map/ppermute | solution.py:243
  188.4 2.8 %collective-permute-done.16 = f16[136,512]{1,0:T(8,128)(2,1)S(1)} collective-permute-done((f16[136,512]{1,0:T(8,128)(2,1)S(1)}, f16[136,512]{1,0:T(8,128)(2,1)S(1)}, u32[]{:S(2)}, u32[]{:S(2)}) %collective-permute-start.16) | collective-permute-done | bytes 139296 | tf_op jit(solution)/shard_map/ppermute | solution.py:245
  196.4 2.9 %fusion.30 = f32[8,32,2048]{2,0,1:T(8,128)} fusion(bf16[32,4,2048]{2,1,0:T(4,128)(2,1)} %reshape.278, pred[8,4]{0,1:T(4,128)(4,1)S(1)} %get-tuple-element.59), kind=kOutput, calls=%fused_computation.66 | convolution fusion | flops 4194304 | bytes 2621472 | tf_op jit(solution)/shard_map/rp,ipx->rix/dot_general | solution.py:341
  201.5 2.4 fusion
  209.4 15.5 %all-to-all-start.1 = ((f16[32,17,128]{2,1,0:T(8,128)(2,1)}), f16[32,17,128]{2,1,0:T(8,128)(2,1)S(1)}, u32[]{:S(2)}, u32[]{:S(2)}) async-start(f16[32,17,128]{2,1,0:T(8,128)(2,1)} %copy.61), calls=%async_computation.1 | async-start | bytes 393216 | tf_op jit(solution)/shard_map/all_to_all | solution.py:387
  235.4 23.8 %all-to-all-done.1 = f16[32,17,128]{2,1,0:T(8,128)(2,1)S(1)} async-done(((f16[32,17,128]{2,1,0:T(8,128)(2,1)}), f16[32,17,128]{2,1,0:T(8,128)(2,1)S(1)}, u32[]{:S(2)}, u32[]{:S(2)}) %all-to-all-start.1) | async-done | bytes 139296 | tf_op jit(solution)/shard_map/all_to_all | solution.py:387
  (180 shorter events, 55.7 us)
Async XLA Ops:
  0.6 204.7 %copy-start = (bf16[8,64,128]{2,1,0:T(8,128)(2,1)S(1)}, bf16[8,64,128]{2,1,0:T(8,128)(2,1)}, u32[]{:S(2)}) copy-start(bf16[8,64,128]{2,1,0:T(8,128)(2,1)} %param.25) | copy-start | bytes 393220
  2.6 182.9 %all-to-all-start = ((bf16[32,4,8,256]{3,2,1,0:T(8,128)(2,1)}), bf16[32,4,8,256]{3,2,1,0:T(8,128)(2,1)}, u32[]{:S(2)}, u32[]{:S(2)}) async-start(bf16[32,4,8,256]{3,2,1,0:T(8,128)(2,1)} %bitcast.95), calls=%async_computation | async-start | bytes 1048576 | tf_op jit(solution)/shard_map/all_to_all | solution.py:325
  43.4 63.5 %copy-start.1 = (f32[16,8192]{1,0:T(8,128)S(1)}, f32[16,8192]{1,0:T(8,128)}, u32[]{:S(2)}) copy-start(f32[16,8192]{1,0:T(8,128)} %get-tuple-element.27.rates) | copy-start | bytes 1572868
  43.4 63.5 %copy-start.3 = (f32[4,8192]{1,0:T(4,128)S(1)}, f32[4,8192]{1,0:T(4,128)}, u32[]{:S(2)}) copy-start(f32[4,8192]{1,0:T(4,128)} %get-tuple-element.26.own_step) | copy-start | bytes 393220
  43.4 61.7 %collective-permute-start.1 = (f16[4,16,8192]{2,1,0:T(8,128)(2,1)S(1)}, f16[4,16,8192]{2,1,0:T(8,128)(2,1)S(1)}, u32[]{:S(2)}, u32[]{:S(2)}) collective-permute-start(f16[4,16,8192]{2,1,0:T(8,128)(2,1)S(1)} %convert_element_type.167), channel_id=1, source_target_pairs={{0,2},{2,0},{4,6},{6,4},{8,10},{10,8},{12,14},{14,12},{16,18},{18,... | collective-permute-start | bytes 3145736 | tf_op jit(solution)/shard_map/ppermute | solution.py:323
  44.9 62.0 %collective-permute-start.2 = (f32[4,8192]{1,0:T(4,128)S(1)}, f32[4,8192]{1,0:T(4,128)S(1)}, u32[]{:S(2)}, u32[]{:S(2)}) collective-permute-start(f32[4,8192]{1,0:T(4,128)S(1)} %copy-done.31), channel_id=1, source_target_pairs={{0,2},{2,0},{4,6},{6,4},{8,10},{10,8},{12,14},{14,12},{16,18},{18,... | collective-permute-start | bytes 393224 | tf_op jit(solution)/shard_map/ppermute | solution.py:324
  109.9 7.7 %collective-permute-start.3 = (f16[136,512]{1,0:T(8,128)(2,1)S(1)}, f16[136,512]{1,0:T(8,128)(2,1)S(1)}, u32[]{:S(2)}, u32[]{:S(2)}) collective-permute-start(f16[136,512]{1,0:T(8,128)(2,1)S(1)} %convert_element_type.169), channel_id=1, source_target_pairs={{0,4},{2,6},{4,8},{6,10},{8,12},{10,14},{12,16},{14,18},{16,20},{1... | collective-permute-start | bytes 417800 | tf_op jit(solution)/shard_map/ppermute | solution.py:243
  112.5 9.3 %collective-permute-start.4 = (f16[136,512]{1,0:T(8,128)(2,1)S(1)}, f16[136,512]{1,0:T(8,128)(2,1)S(1)}, u32[]{:S(2)}, u32[]{:S(2)}) collective-permute-start(f16[136,512]{1,0:T(8,128)(2,1)S(1)} %convert_element_type.171), channel_id=1, source_target_pairs={{0,60},{2,62},{4,0},{6,2},{8,4},{10,6},{12,8},{14,10},{16,12},{18,... | collective-permute-start | bytes 417800 | tf_op jit(solution)/shard_map/ppermute | solution.py:245
  122.5 8.5 %collective-permute-start.5 = (f16[136,512]{1,0:T(8,128)(2,1)S(1)}, f16[136,512]{1,0:T(8,128)(2,1)S(1)}, u32[]{:S(2)}, u32[]{:S(2)}) collective-permute-start(f16[136,512]{1,0:T(8,128)(2,1)S(1)} %convert_element_type.173), channel_id=1, source_target_pairs={{0,4},{2,6},{4,8},{6,10},{8,12},{10,14},{12,16},{14,18},{16,20},{1... | collective-permute-start | bytes 417800 | tf_op jit(solution)/shard_map/ppermute | solution.py:243
  126.5 7.4 %collective-permute-start.6 = (f16[136,512]{1,0:T(8,128)(2,1)S(1)}, f16[136,512]{1,0:T(8,128)(2,1)S(1)}, u32[]{:S(2)}, u32[]{:S(2)}) collective-permute-start(f16[136,512]{1,0:T(8,128)(2,1)S(1)} %convert_element_type.175), channel_id=1, source_target_pairs={{0,60},{2,62},{4,0},{6,2},{8,4},{10,6},{12,8},{14,10},{16,12},{18,... | collective-permute-start | bytes 417800 | tf_op jit(solution)/shard_map/ppermute | solution.py:245
  134.6 7.4 %collective-permute-start.7 = (f16[136,512]{1,0:T(8,128)(2,1)S(1)}, f16[136,512]{1,0:T(8,128)(2,1)S(1)}, u32[]{:S(2)}, u32[]{:S(2)}) collective-permute-start(f16[136,512]{1,0:T(8,128)(2,1)S(1)} %convert_element_type.177), channel_id=1, source_target_pairs={{0,4},{2,6},{4,8},{6,10},{8,12},{10,14},{12,16},{14,18},{16,20},{1... | collective-permute-start | bytes 417800 | tf_op jit(solution)/shard_map/ppermute | solution.py:243
  138.5 6.4 %collective-permute-start.8 = (f16[136,512]{1,0:T(8,128)(2,1)S(1)}, f16[136,512]{1,0:T(8,128)(2,1)S(1)}, u32[]{:S(2)}, u32[]{:S(2)}) collective-permute-start(f16[136,512]{1,0:T(8,128)(2,1)S(1)} %convert_element_type.179), channel_id=1, source_target_pairs={{0,60},{2,62},{4,0},{6,2},{8,4},{10,6},{12,8},{14,10},{16,12},{18,... | collective-permute-start | bytes 417800 | tf_op jit(solution)/shard_map/ppermute | solution.py:245
  145.6 7.4 %collective-permute-start.9 = (f16[136,512]{1,0:T(8,128)(2,1)S(1)}, f16[136,512]{1,0:T(8,128)(2,1)S(1)}, u32[]{:S(2)}, u32[]{:S(2)}) collective-permute-start(f16[136,512]{1,0:T(8,128)(2,1)S(1)} %convert_element_type.181), channel_id=1, source_target_pairs={{0,4},{2,6},{4,8},{6,10},{8,12},{10,14},{12,16},{14,18},{16,20},{1... | collective-permute-start | bytes 417800 | tf_op jit(solution)/shard_map/ppermute | solution.py:243
  150.4 7.5 %collective-permute-start.10 = (f16[136,512]{1,0:T(8,128)(2,1)S(1)}, f16[136,512]{1,0:T(8,128)(2,1)S(1)}, u32[]{:S(2)}, u32[]{:S(2)}) collective-permute-start(f16[136,512]{1,0:T(8,128)(2,1)S(1)} %convert_element_type.183), channel_id=1, source_target_pairs={{0,60},{2,62},{4,0},{6,2},{8,4},{10,6},{12,8},{14,10},{16,12},{18,... | collective-permute-start | bytes 417800 | tf_op jit(solution)/shard_map/ppermute | solution.py:245
  158.7 8.8 %collective-permute-start.11 = (f16[136,512]{1,0:T(8,128)(2,1)S(1)}, f16[136,512]{1,0:T(8,128)(2,1)S(1)}, u32[]{:S(2)}, u32[]{:S(2)}) collective-permute-start(f16[136,512]{1,0:T(8,128)(2,1)S(1)} %convert_element_type.185), channel_id=1, source_target_pairs={{0,4},{2,6},{4,8},{6,10},{8,12},{10,14},{12,16},{14,18},{16,20},{1... | collective-permute-start | bytes 417800 | tf_op jit(solution)/shard_map/ppermute | solution.py:243
  161.5 7.6 %collective-permute-start.12 = (f16[136,512]{1,0:T(8,128)(2,1)S(1)}, f16[136,512]{1,0:T(8,128)(2,1)S(1)}, u32[]{:S(2)}, u32[]{:S(2)}) collective-permute-start(f16[136,512]{1,0:T(8,128)(2,1)S(1)} %convert_element_type.187), channel_id=1, source_target_pairs={{0,60},{2,62},{4,0},{6,2},{8,4},{10,6},{12,8},{14,10},{16,12},{18,... | collective-permute-start | bytes 417800 | tf_op jit(solution)/shard_map/ppermute | solution.py:245
  169.9 8.9 %collective-permute-start.13 = (f16[136,512]{1,0:T(8,128)(2,1)S(1)}, f16[136,512]{1,0:T(8,128)(2,1)S(1)}, u32[]{:S(2)}, u32[]{:S(2)}) collective-permute-start(f16[136,512]{1,0:T(8,128)(2,1)S(1)} %convert_element_type.189), channel_id=1, source_target_pairs={{0,4},{2,6},{4,8},{6,10},{8,12},{10,14},{12,16},{14,18},{16,20},{1... | collective-permute-start | bytes 417800 | tf_op jit(solution)/shard_map/ppermute | solution.py:243
  174.2 6.1 %collective-permute-start.14 = (f16[136,512]{1,0:T(8,128)(2,1)S(1)}, f16[136,512]{1,0:T(8,128)(2,1)S(1)}, u32[]{:S(2)}, u32[]{:S(2)}) collective-permute-start(f16[136,512]{1,0:T(8,128)(2,1)S(1)} %convert_element_type.191), channel_id=1, source_target_pairs={{0,60},{2,62},{4,0},{6,2},{8,4},{10,6},{12,8},{14,10},{16,12},{18,... | collective-permute-start | bytes 417800 | tf_op jit(solution)/shard_map/ppermute | solution.py:245
  181.1 7.3 %collective-permute-start.15 = (f16[136,512]{1,0:T(8,128)(2,1)S(1)}, f16[136,512]{1,0:T(8,128)(2,1)S(1)}, u32[]{:S(2)}, u32[]{:S(2)}) collective-permute-start(f16[136,512]{1,0:T(8,128)(2,1)S(1)} %convert_element_type.193), channel_id=1, source_target_pairs={{0,4},{2,6},{4,8},{6,10},{8,12},{10,14},{12,16},{14,18},{16,20},{1... | collective-permute-start | bytes 417800 | tf_op jit(solution)/shard_map/ppermute | solution.py:243
  185.1 6.1 %collective-permute-start.16 = (f16[136,512]{1,0:T(8,128)(2,1)S(1)}, f16[136,512]{1,0:T(8,128)(2,1)S(1)}, u32[]{:S(2)}, u32[]{:S(2)}) collective-permute-start(f16[136,512]{1,0:T(8,128)(2,1)S(1)} %convert_element_type.195), channel_id=1, source_target_pairs={{0,60},{2,62},{4,0},{6,2},{8,4},{10,6},{12,8},{14,10},{16,12},{18,... | collective-permute-start | bytes 417800 | tf_op jit(solution)/shard_map/ppermute | solution.py:245
  185.5 13.8 %collective-permute-start = (bf16[32,4,8,256]{3,2,1,0:T(8,128)(2,1)}, bf16[32,4,8,256]{3,2,1,0:T(8,128)(2,1)}, u32[]{:S(2)}, u32[]{:S(2)}) collective-permute-start(bf16[32,4,8,256]{3,2,1,0:T(8,128)(2,1)} %all-to-all-done), channel_id=1, source_target_pairs={{0,1},{1,0},{2,3},{3,2},{4,5},{5,4},{6,7},{7,6},{8,9},{9,8},{10,11... | collective-permute-start | bytes 1572872 | tf_op jit(solution)/shard_map/ppermute | solution.py:276
  191.8 37.1 %collective-permute-start.17 = (f16[136,512]{1,0:T(8,128)(2,1)S(1)}, f16[136,512]{1,0:T(8,128)(2,1)}, u32[]{:S(2)}, u32[]{:S(2)}) collective-permute-start(f16[136,512]{1,0:T(8,128)(2,1)S(1)} %convert_element_type.197), channel_id=1, source_target_pairs={{0,4},{2,6},{4,8},{6,10},{8,12},{10,14},{12,16},{14,18},{16,20},{1... | collective-permute-start | bytes 417800 | tf_op jit(solution)/shard_map/ppermute | solution.py:243
  209.4 49.9 %all-to-all-start.1 = ((f16[32,17,128]{2,1,0:T(8,128)(2,1)}), f16[32,17,128]{2,1,0:T(8,128)(2,1)S(1)}, u32[]{:S(2)}, u32[]{:S(2)}) async-start(f16[32,17,128]{2,1,0:T(8,128)(2,1)} %copy.61), calls=%async_computation.1 | async-start | bytes 393216 | tf_op jit(solution)/shard_map/all_to_all | solution.py:387
  230.7 1.5 collective-permute-start.18
  (29 other events, 133.2 us)

commit v4 on v3

--- a/solution.py
+++ b/solution.py
@@ -29,22 +29,21 @@
     return pl.BlockSpec(memory_space=pltpu.VMEM)
 
 
-def pick_kernel(
-    flags, usable, state_in, step_in, rate_in, sent_state, sent_step, own_state, own_step, own_rate,
-    *, width,
-):
+def pick_kernel(where, lengths, state_in, step_in, state_out, step_out, *, width):
     count = state_in.shape[0]
+    for p in range(count):
+        use = jnp.where(where[1] < lengths[where[2] + p], 1.0, 0.0)
+        for q in range(PAIRS_A_STEP):
+            source = pl.ds(pl.multiple_of((2 * q + where[0]) * width, 128), width)
+            target = pl.ds(q * width, width)
+            state_out[p, :, target] = state_in[p, :, source] * (use * STATE_SCALE)
+            step_out[p : p + 1, target] = step_in[p, :, source] * use
+
+
+def rate_kernel(where, rate_in, rate_out, *, width):
     for q in range(PAIRS_A_STEP):
-        own = pl.ds(pl.multiple_of((2 * q + flags[0]) * width, 128), width)
-        other = pl.ds(pl.multiple_of((2 * q + flags[1]) * width, 128), width)
-        target = pl.ds(q * width, width)
-        own_rate[:, target] = rate_in[:, own]
-        for p in range(count):
-            use = usable[p]
-            sent_state[p, :, target] = state_in[p, :, other] * (use * STATE_SCALE)
-            own_state[p, :, target] = state_in[p, :, own] * (use * STATE_SCALE)
-            sent_step[p : p + 1, target] = step_in[p, :, other] * use
-            own_step[p : p + 1, target] = step_in[p, :, own] * use
+        source = pl.ds(pl.multiple_of((2 * q + where[0]) * width, 128), width)
+        rate_out[:, q * width : (q + 1) * width] = rate_in[:, source]
 
 
 def fold_kernel(
@@ -150,37 +149,48 @@
     return jnp.stack([jnp.asarray(v) for v in values]).astype(jnp.int32)
 
 
-def picked_for_pair(states, steps, rates, usable, seq_index, width):
+def pick(where, lengths, states, steps, width):
     count, state, channels = states.shape
     wide = PAIRS_A_STEP * width
-    blocks = (
-        pl.BlockSpec((count, state, wide), lambda n: (0, 0, n)),
-        pl.BlockSpec((count, wide), lambda n: (0, n)),
-    )
-    shapes = (
-        jax.ShapeDtypeStruct((count, state, channels // 2), jnp.float32),
-        jax.ShapeDtypeStruct((count, channels // 2), jnp.float32),
-    )
     return pl.pallas_call(
         functools.partial(pick_kernel, width=width),
         grid=(channels // (2 * wide),),
-        out_shape=shapes
-        + shapes
-        + (jax.ShapeDtypeStruct((state, channels // 2), jnp.float32),),
+        out_shape=(
+            jax.ShapeDtypeStruct((count, state, channels // 2), jnp.float32),
+            jax.ShapeDtypeStruct((count, channels // 2), jnp.float32),
+        ),
         in_specs=[
             smem(),
             smem(),
             pl.BlockSpec((count, state, 2 * wide), lambda n: (0, 0, n)),
             pl.BlockSpec((count, 1, 2 * wide), lambda n: (0, 0, n)),
-            pl.BlockSpec((state, 2 * wide), lambda n: (0, n)),
         ],
-        out_specs=blocks + blocks + (pl.BlockSpec((state, wide), lambda n: (0, n)),),
+        out_specs=(
+            pl.BlockSpec((count, state, wide), lambda n: (0, 0, n)),
+            pl.BlockSpec((count, wide), lambda n: (0, n)),
+        ),
         cost_estimate=pl.CostEstimate(
-            flops=states.size, bytes_accessed=8 * states.size, transcendentals=0
-        ),
-        compiler_params=pltpu.CompilerParams(vmem_limit_bytes=7 * KERNEL_VMEM),
-        name="pick_for_pair",
-    )(numbers(seq_index % 2, 1 - seq_index % 2), usable, states, steps, rates)
+            flops=states.size, bytes_accessed=6 * states.size, transcendentals=0
+        ),
+        compiler_params=pltpu.CompilerParams(vmem_limit_bytes=56 * 1024 * 1024),
+    )(where, lengths, states, steps)
+
+
+def picked_rates(where, rates, width):
+    state, channels = rates.shape
+    wide = PAIRS_A_STEP * width
+    return pl.pallas_call(
+        functools.partial(rate_kernel, width=width),
+        grid=(channels // (2 * wide),),
+        out_shape=jax.ShapeDtypeStruct((state, channels // 2), jnp.float32),
+        in_specs=[smem(), pl.BlockSpec((state, 2 * wide), lambda n: (0, n))],
+        out_specs=pl.BlockSpec((state, wide), lambda n: (0, n)),
+        cost_estimate=pl.CostEstimate(
+            flops=0, bytes_accessed=6 * rates.size, transcendentals=0
+        ),
+        compiler_params=pltpu.CompilerParams(vmem_limit_bytes=56 * 1024 * 1024),
+        name="pick_rates",
+    )(where, rates)
 
 
 def folded_pair(own_state, own_step, rates, came_state, came_step, seq_index, width):
@@ -263,13 +273,35 @@
     )
 
 
-def in_pieces(value):
-    pieces = []
-    for _ in range(3):
-        piece = lax.reduce_precision(value, 5, 10)
-        pieces.append(piece)
-        value = value - piece
-    return jnp.stack(pieces)
+def owners_first(value, seq_count, owned, *minor):
+    bits = seq_count.bit_length() - 1
+    requests = value.shape[0]
+    value = value.reshape(requests, *(2,) * bits, owned, *minor)
+    value = value.transpose(*range(bits, 0, -1), 0, *range(bits + 1, value.ndim))
+    return value.reshape(seq_count, requests * owned, *minor)
+
+
+def merged_over(top, total, sums, seq_count, seq_index):
+    reach = 1
+    while reach < seq_count:
+        half = top.shape[0] // 2
+        bit = (seq_index // reach) % 2
+        pairs = [(k, k ^ reach) for k in range(seq_count)]
+
+        def chosen(index):
+            return [lax.dynamic_slice_in_dim(x, index * half, half, 0) for x in (top, total, sums)]
+
+        sent_top, sent_total, sent_sums = chosen(1 - bit)
+        top, total, sums = chosen(bit)
+        came_sums = lax.ppermute(sent_sums, "seq", pairs)
+        came_top, came_total = lax.ppermute(jnp.stack([sent_top, sent_total]), "seq", pairs)
+        common = jnp.maximum(top, came_top)
+        own_factor, came_factor = jnp.exp(top - common), jnp.exp(came_top - common)
+        top = common
+        total = total * own_factor + came_total * came_factor
+        sums = sums * own_factor[..., None] + came_sums * came_factor[..., None]
+        reach *= 2
+    return top, total, sums
 
 
 def swapped(array):
@@ -313,18 +345,23 @@
     lengths = jnp.where(fresh, chosen_len, cache_lengths)
     own_match = lax.dynamic_slice_in_dim(matches, own_at, local_prompts, 1)
     peer_match = lax.dynamic_slice_in_dim(matches, peer_at, local_prompts, 1)
-    own_lengths = lax.dynamic_slice_in_dim(prompt_lengths, own_at, local_prompts)
-    usable = (seq_index * block_len < own_lengths).astype(jnp.float32)
 
     pairs = [(k, k ^ 1) for k in range(seq_count)]
-    sent_state, sent_step, own_state, own_step, rates = picked_for_pair(
-        prompt_states[:, 0], block_steps, decay_rates, usable, seq_index, local_channels
+    parity = seq_index % 2
+    there = numbers(1 - parity, seq_index * block_len, own_at)
+    here = numbers(parity, seq_index * block_len, own_at)
+    sent_state, sent_step = pick(
+        there, prompt_lengths, prompt_states[:, 0], block_steps, local_channels
     )
     came_state = lax.ppermute(sent_state.astype(jnp.float16), "seq", pairs)
     came_step = lax.ppermute(sent_step, "seq", pairs)
     moved = lax.all_to_all(
         jnp.swapaxes(prompt_cache, 0, 1), "seq", split_axis=0, concat_axis=0, tiled=True
     )
+    own_state, own_step = pick(
+        here, prompt_lengths, prompt_states[:, 0], block_steps, local_channels
+    )
+    rates = picked_rates(here, decay_rates, local_channels)
     folded = folded_pair(
         own_state,
         own_step,
@@ -338,12 +375,13 @@
 
     peer_moved = swapped(moved)
     flat = (block_len, local_prompts, kv_heads * kv_width)
-    picked = jnp.einsum(
+    own_picked = jnp.einsum(
         "rp,ipx->rix",
         own_match.astype(jnp.bfloat16),
         moved.reshape(flat),
         preferred_element_type=jnp.float32,
-    ) + jnp.einsum(
+    )
+    picked = own_picked + jnp.einsum(
         "rp,ipx->rix",
         peer_match.astype(jnp.bfloat16),
         peer_moved.reshape(flat),
@@ -378,28 +416,15 @@
         preferred_element_type=jnp.float32,
     )
     owned = heads // seq_count
-    rows = requests * owned
-    sums = summed.reshape(requests, seq_count, owned, head_dim)
-    sums = jnp.moveaxis(sums, 1, 0).reshape(seq_count, rows, head_dim)
-    extra = in_pieces(jnp.stack([highest, denominator])).reshape(6, requests, seq_count, owned)
-    extra = jnp.moveaxis(extra, 2, 0).reshape(seq_count, 6 * rows)
-    extra = jnp.pad(extra, ((0, 0), (0, head_dim - 6 * rows)))[:, None]
-    parcels = lax.all_to_all(
-        jnp.concatenate([sums, extra], axis=1).astype(jnp.float16),
-        "seq",
-        split_axis=0,
-        concat_axis=0,
-        tiled=True,
-    ).astype(jnp.float32)
-    peer_sum = parcels[:, :rows]
-    peer_extra = parcels[:, rows, : 6 * rows].reshape(seq_count, 3, 2, rows)
-    peer_extra = (peer_extra[:, 2] + peer_extra[:, 1]) + peer_extra[:, 0]
-    peer_top, peer_total = peer_extra[:, 0], peer_extra[:, 1]
-    common_top = jnp.max(peer_top, axis=0)
-    factor = jnp.exp(peer_top - common_top[None])
-    owner_total = jnp.sum(peer_total * factor, axis=0)
-    owner_sum = jnp.sum(peer_sum * factor[..., None], axis=0)
-    attention = (owner_sum / owner_total[..., None]).astype(jnp.bfloat16)
+    part = merged_over(
+        owners_first(highest, seq_count, owned),
+        owners_first(denominator, seq_count, owned),
+        owners_first(summed, seq_count, owned, head_dim),
+        seq_count,
+        seq_index,
+    )
+    _, owner_total, owner_sum = part
+    attention = (owner_sum[0] / owner_total[0][:, None]).astype(jnp.bfloat16)
     attention = attention.reshape(requests, owned, head_dim)
 
     rates_here = lax.dynamic_slice_in_dim(

time: 262 us -> 310 us (1.18)
  the two profiles are of different devices: /device:TPU:38 before, /device:TPU:44 now
where the time goes in v4:
time: 310 us; the launch traced here: 309 us
  starting transfers between devices  131 us (42%)
  waiting for transfers between devices  118 us (38%)
  Pallas kernels  18.6 us (6%)
  local copies, waits for them, and re-layouts  18.1 us (6%)
  other arithmetic  16.7 us (5%)
  matrix products  4.3 us (1%)
    ppermute x1, waiting for transfers between devices, local(): came_state = lax.ppermute(sent_state.astype(jnp.float16), 'seq', pairs)  52.7 us
    ppermute x5, starting transfers between devices, merged_over(): came_sums = lax.ppermute(sent_sums, 'seq', pairs)  34.7 us
    all_to_all x1, starting transfers between devices, local(): lax.all_to_all(jnp.swapaxes(prompt_cache, 0, 1), 'seq', split_axis=0, con...  32.7 us
    ppermute x8, starting transfers between devices, hand_over(): sent = lax.ppermute(outs[0].astype(jnp.float16), 'seq', ahead)  28.5 us
    ppermute x5, starting transfers between devices, merged_over(): lax.ppermute(jnp.stack([sent_top, sent_total]), 'seq', pairs)  27.8 us
    ppermute x8, waiting for transfers between devices, hand_over(): sent = lax.ppermute(outs[0].astype(jnp.float16), 'seq', ahead)  26.3 us
    ppermute x7, waiting for transfers between devices, hand_over(): down = lax.ppermute(outs[1].astype(jnp.float16), 'seq', behind)  21.5 us
    ppermute x5, waiting for transfers between devices, merged_over(): came_sums = lax.ppermute(sent_sums, 'seq', pairs)  10.2 us
  transfers between devices with their start and end apart: 30, of which 25 were waited for; matrix products, arithmetic and copies ran while one was open for 6% of the time, Pallas kernels for 6%

profile of v4, /device:TPU:44, one launch (start us, length us, event | category | flops | bytes accessed | tf_op | source)
XLA Modules:
  0.0 308.8 jit_solution(685574916140846407)
XLA Ops:
  2.6 32.7 %all-to-all-start = ((bf16[32,4,8,256]{3,2,1,0:T(8,128)(2,1)}), bf16[32,4,8,256]{3,2,1,0:T(8,128)(2,1)}, u32[]{:S(2)}, u32[]{:S(2)}) async-start(bf16[32,4,8,256]{3,2,1,0:T(8,128)(2,1)} %bitcast.177), calls=%async_computation | async-start | bytes 1048576 | tf_op jit(solution)/shard_map/all_to_all | solution.py:358
  36.0 4.3 %shard_map.193 = (f32[4,16,8192]{2,1,0:T(8,128)}, f32[4,8192]{1,0:T(4,128)}) custom-call(s32[3]{0:T(128)} %add_add_fusion.1.where, s32[8]{0:T(128)} %lengths.3, f32[4,16,16384]{2,1,0:T(8,128)} %bitcast.178, f32[4,1,16384]{2,1,0:T(1,128)} %step_in.3), custom_call_target="tpu_custom_call" | custom-call | flops 1048576 | bytes 6291456 | tf_op jit(solution)/shard_map/pallas_call | solution.py:155
  44.8 3.3 %pick_rates.1.rates = f32[16,8192]{1,0:T(8,128)} custom-call(s32[3]{0:T(128)} %add_add_fusion.where, f32[16,16384]{1,0:T(8,128)} %rate_in.1), custom_call_target="tpu_custom_call" | custom-call | bytes 1572864 | tf_op jit(solution)/shard_map/pick_rates/pallas_call | solution.py:182
  48.1 4.3 %shard_map.192 = (f32[4,16,8192]{2,1,0:T(8,128)}, f32[4,8192]{1,0:T(4,128)}) custom-call(s32[3]{0:T(128)} %add_add_fusion.where, s32[8]{0:T(128)} %lengths.3, f32[4,16,16384]{2,1,0:T(8,128)} %bitcast.179, f32[4,1,16384]{2,1,0:T(1,128)} %step_in.3), custom_call_target="tpu_custom_call" | custom-call | flops 1048576 | bytes 6291456 | tf_op jit(solution)/shard_map/pallas_call | solution.py:155
  52.4 52.7 %collective-permute-done.11 = f16[4,16,8192]{2,1,0:T(8,128)(2,1)S(1)} collective-permute-done((f16[4,16,8192]{2,1,0:T(8,128)(2,1)S(1)}, f16[4,16,8192]{2,1,0:T(8,128)(2,1)S(1)}, u32[]{:S(2)}, u32[]{:S(2)}) %collective-permute-start.11) | collective-permute-done | bytes 1048608 | tf_op jit(solution)/shard_map/ppermute | solution.py:356
  112.7 3.3 %collective-permute-done.13 = f16[136,512]{1,0:T(8,128)(2,1)S(1)} collective-permute-done((f16[136,512]{1,0:T(8,128)(2,1)S(1)}, f16[136,512]{1,0:T(8,128)(2,1)S(1)}, u32[]{:S(2)}, u32[]{:S(2)}) %collective-permute-start.13) | collective-permute-done | bytes 139296 | tf_op jit(solution)/shard_map/ppermute | solution.py:253
  116.0 4.1 %collective-permute-done.14 = f16[136,512]{1,0:T(8,128)(2,1)S(1)} collective-permute-done((f16[136,512]{1,0:T(8,128)(2,1)S(1)}, f16[136,512]{1,0:T(8,128)(2,1)S(1)}, u32[]{:S(2)}, u32[]{:S(2)}) %collective-permute-start.14) | collective-permute-done | bytes 139296 | tf_op jit(solution)/shard_map/ppermute | solution.py:255
  120.9 3.9 %collective-permute-start.15 = (f16[136,512]{1,0:T(8,128)(2,1)S(1)}, f16[136,512]{1,0:T(8,128)(2,1)S(1)}, u32[]{:S(2)}, u32[]{:S(2)}) collective-permute-start(f16[136,512]{1,0:T(8,128)(2,1)S(1)} %convert_element_type.162), channel_id=1, source_target_pairs={{0,4},{2,6},{4,8},{6,10},{8,12},{10,14},{12,16},{14,18},{16,20},{1... | collective-permute-start | bytes 417800 | tf_op jit(solution)/shard_map/ppermute | solution.py:253
  125.4 4.0 %collective-permute-done.15 = f16[136,512]{1,0:T(8,128)(2,1)S(1)} collective-permute-done((f16[136,512]{1,0:T(8,128)(2,1)S(1)}, f16[136,512]{1,0:T(8,128)(2,1)S(1)}, u32[]{:S(2)}, u32[]{:S(2)}) %collective-permute-start.15) | collective-permute-done | bytes 139296 | tf_op jit(solution)/shard_map/ppermute | solution.py:253
  133.0 3.9 %collective-permute-start.17 = (f16[136,512]{1,0:T(8,128)(2,1)S(1)}, f16[136,512]{1,0:T(8,128)(2,1)S(1)}, u32[]{:S(2)}, u32[]{:S(2)}) collective-permute-start(f16[136,512]{1,0:T(8,128)(2,1)S(1)} %convert_element_type.166), channel_id=1, source_target_pairs={{0,4},{2,6},{4,8},{6,10},{8,12},{10,14},{12,16},{14,18},{16,20},{1... | collective-permute-start | bytes 417800 | tf_op jit(solution)/shard_map/ppermute | solution.py:253
  144.0 4.8 %collective-permute-start.19 = (f16[136,512]{1,0:T(8,128)(2,1)S(1)}, f16[136,512]{1,0:T(8,128)(2,1)S(1)}, u32[]{:S(2)}, u32[]{:S(2)}) collective-permute-start(f16[136,512]{1,0:T(8,128)(2,1)S(1)} %convert_element_type.170), channel_id=1, source_target_pairs={{0,4},{2,6},{4,8},{6,10},{8,12},{10,14},{12,16},{14,18},{16,20},{1... | collective-permute-start | bytes 417800 | tf_op jit(solution)/shard_map/ppermute | solution.py:253
  151.4 4.9 %collective-permute-done.20 = f16[136,512]{1,0:T(8,128)(2,1)S(1)} collective-permute-done((f16[136,512]{1,0:T(8,128)(2,1)S(1)}, f16[136,512]{1,0:T(8,128)(2,1)S(1)}, u32[]{:S(2)}, u32[]{:S(2)}) %collective-permute-start.20) | collective-permute-done | bytes 139296 | tf_op jit(solution)/shard_map/ppermute | solution.py:255
  161.8 4.1 %collective-permute-done.21 = f16[136,512]{1,0:T(8,128)(2,1)S(1)} collective-permute-done((f16[136,512]{1,0:T(8,128)(2,1)S(1)}, f16[136,512]{1,0:T(8,128)(2,1)S(1)}, u32[]{:S(2)}, u32[]{:S(2)}) %collective-permute-start.21) | collective-permute-done | bytes 139296 | tf_op jit(solution)/shard_map/ppermute | solution.py:253
  168.3 4.3 %collective-permute-start.23 = (f16[136,512]{1,0:T(8,128)(2,1)S(1)}, f16[136,512]{1,0:T(8,128)(2,1)S(1)}, u32[]{:S(2)}, u32[]{:S(2)}) collective-permute-start(f16[136,512]{1,0:T(8,128)(2,1)S(1)} %convert_element_type.178), channel_id=1, source_target_pairs={{0,4},{2,6},{4,8},{6,10},{8,12},{10,14},{12,16},{14,18},{16,20},{1... | collective-permute-start | bytes 417800 | tf_op jit(solution)/shard_map/ppermute | solution.py:253
  180.5 4.0 %collective-permute-start.25 = (f16[136,512]{1,0:T(8,128)(2,1)S(1)}, f16[136,512]{1,0:T(8,128)(2,1)S(1)}, u32[]{:S(2)}, u32[]{:S(2)}) collective-permute-start(f16[136,512]{1,0:T(8,128)(2,1)S(1)} %convert_element_type.182), channel_id=1, source_target_pairs={{0,4},{2,6},{4,8},{6,10},{8,12},{10,14},{12,16},{14,18},{16,20},{1... | collective-permute-start | bytes 417800 | tf_op jit(solution)/shard_map/ppermute | solution.py:253
  194.8 3.8 %collective-permute-done.27 = f16[136,512]{1,0:T(8,128)(2,1)S(1)} collective-permute-done((f16[136,512]{1,0:T(8,128)(2,1)S(1)}, f16[136,512]{1,0:T(8,128)(2,1)S(1)}, u32[]{:S(2)}, u32[]{:S(2)}) %collective-permute-start.27) | collective-permute-done | bytes 139296 | tf_op jit(solution)/shard_map/ppermute | solution.py:253
  223.0 5.4 %collective-permute-start.1 = (f32[2,16,16]{2,1,0:T(8,128)}, f32[2,16,16]{2,1,0:T(8,128)}, u32[]{:S(2)}, u32[]{:S(2)}) collective-permute-start(f32[2,16,16]{2,1,0:T(8,128)} %pad_maximum_fusion), channel_id=1, source_target_pairs={{0,2},{2,0},{4,6},{6,4},{8,10},{10,8},{12,14},{14,12},{16,18},{18,... | collective-permute-start | bytes 6152 | tf_op jit(solution)/shard_map/ppermute | solution.py:297
  236.9 5.0 %collective-permute-start.5 = (f32[2,4,16]{2,1,0:T(4,128)S(1)}, f32[2,4,16]{2,1,0:T(4,128)S(1)}, u32[]{:S(2)}, u32[]{:S(2)}) collective-permute-start(f32[2,4,16]{2,1,0:T(4,128)S(1)} %pad_maximum_fusion.2), channel_id=1, source_target_pairs={{0,8},{2,10},{4,12},{6,14},{8,0},{10,2},{12,4},{14,6},{16,24},{18,... | collective-permute-start | bytes 1544 | tf_op jit(solution)/shard_map/ppermute | solution.py:297
  244.7 9.5 %collective-permute-start.7 = (f32[2,2,16]{2,1,0:T(2,128)S(1)}, f32[2,2,16]{2,1,0:T(2,128)S(1)}, u32[]{:S(2)}, u32[]{:S(2)}) collective-permute-start(f32[2,2,16]{2,1,0:T(2,128)S(1)} %pad_maximum_fusion.3), channel_id=1, source_target_pairs={{0,16},{2,18},{4,20},{6,22},{8,24},{10,26},{12,28},{14,30},{16,0},... | collective-permute-start | bytes 776 | tf_op jit(solution)/shard_map/ppermute | solution.py:297
  262.8 6.3 %collective-permute-start.6 = (f32[4,16,128]{2,1,0:T(8,128)S(1)}, f32[4,16,128]{2,1,0:T(8,128)S(1)}, u32[]{:S(2)}, u32[]{:S(2)}) collective-permute-start(f32[4,16,128]{2,1,0:T(8,128)S(1)} %constant_dynamic-slice_fusion.12), channel_id=1, source_target_pairs={{0,8},{2,10},{4,12},{6,14},{8,0},{10,2},{12,4},{14,6},{16,24},{18,... | collective-permute-start | bytes 98312 | tf_op jit(solution)/shard_map/ppermute | solution.py:296
  271.1 9.5 %collective-permute-start.8 = (f32[2,16,128]{2,1,0:T(8,128)S(1)}, f32[2,16,128]{2,1,0:T(8,128)S(1)}, u32[]{:S(2)}, u32[]{:S(2)}) collective-permute-start(f32[2,16,128]{2,1,0:T(8,128)S(1)} %constant_dynamic-slice_fusion.7), channel_id=1, source_target_pairs={{0,16},{2,18},{4,20},{6,22},{8,24},{10,26},{12,28},{14,30},{16,0},... | collective-permute-start | bytes 49160 | tf_op jit(solution)/shard_map/ppermute | solution.py:296
  280.6 5.3 %collective-permute-start.9 = (f32[2,1,16]{2,1,0:T(1,128)S(1)}, f32[2,1,16]{2,1,0:T(1,128)S(1)}, u32[]{:S(2)}, u32[]{:S(2)}) collective-permute-start(f32[2,1,16]{2,1,0:T(1,128)S(1)} %pad_maximum_fusion.4), channel_id=1, source_target_pairs={{0,32},{2,34},{4,36},{6,38},{8,40},{10,42},{12,44},{14,46},{16,48}... | collective-permute-start | bytes 392 | tf_op jit(solution)/shard_map/ppermute | solution.py:297
  286.0 15.2 %collective-permute-start.10 = (f32[1,16,128]{2,1,0:T(8,128)S(1)}, f32[1,16,128]{2,1,0:T(8,128)S(1)}, u32[]{:S(2)}, u32[]{:S(2)}) collective-permute-start(f32[1,16,128]{2,1,0:T(8,128)S(1)} %constant_dynamic-slice_fusion.1), channel_id=1, source_target_pairs={{0,32},{2,34},{4,36},{6,38},{8,40},{10,42},{12,44},{14,46},{16,48}... | collective-permute-start | bytes 24584 | tf_op jit(solution)/shard_map/ppermute | solution.py:296
  302.6 5.4 %collective-permute-done.10 = f32[1,16,128]{2,1,0:T(8,128)S(1)} collective-permute-done((f32[1,16,128]{2,1,0:T(8,128)S(1)}, f32[1,16,128]{2,1,0:T(8,128)S(1)}, u32[]{:S(2)}, u32[]{:S(2)}) %collective-permute-start.10) | collective-permute-done | bytes 8224 | tf_op jit(solution)/shard_map/ppermute | solution.py:296
  (200 shorter events, 103.3 us)
Async XLA Ops:
  2.6 198.4 %all-to-all-start = ((bf16[32,4,8,256]{3,2,1,0:T(8,128)(2,1)}), bf16[32,4,8,256]{3,2,1,0:T(8,128)(2,1)}, u32[]{:S(2)}, u32[]{:S(2)}) async-start(bf16[32,4,8,256]{3,2,1,0:T(8,128)(2,1)} %bitcast.177), calls=%async_computation | async-start | bytes 1048576 | tf_op jit(solution)/shard_map/all_to_all | solution.py:358
  42.0 63.1 %collective-permute-start.11 = (f16[4,16,8192]{2,1,0:T(8,128)(2,1)S(1)}, f16[4,16,8192]{2,1,0:T(8,128)(2,1)S(1)}, u32[]{:S(2)}, u32[]{:S(2)}) collective-permute-start(f16[4,16,8192]{2,1,0:T(8,128)(2,1)S(1)} %convert_element_type.156), channel_id=1, source_target_pairs={{0,2},{2,0},{4,6},{6,4},{8,10},{10,8},{12,14},{14,12},{16,18},{18,... | collective-permute-start | bytes 3145736 | tf_op jit(solution)/shard_map/ppermute | solution.py:356
  43.4 63.5 %collective-permute-start.12 = (f32[4,8192]{1,0:T(4,128)S(1)}, f32[4,8192]{1,0:T(4,128)S(1)}, u32[]{:S(2)}, u32[]{:S(2)}) collective-permute-start(f32[4,8192]{1,0:T(4,128)S(1)} %copy-done.19), channel_id=1, source_target_pairs={{0,2},{2,0},{4,6},{6,4},{8,10},{10,8},{12,14},{14,12},{16,18},{18,... | collective-permute-start | bytes 393224 | tf_op jit(solution)/shard_map/ppermute | solution.py:357
  108.3 7.7 %collective-permute-start.13 = (f16[136,512]{1,0:T(8,128)(2,1)S(1)}, f16[136,512]{1,0:T(8,128)(2,1)S(1)}, u32[]{:S(2)}, u32[]{:S(2)}) collective-permute-start(f16[136,512]{1,0:T(8,128)(2,1)S(1)} %convert_element_type.158), channel_id=1, source_target_pairs={{0,4},{2,6},{4,8},{6,10},{8,12},{10,14},{12,16},{14,18},{16,20},{1... | collective-permute-start | bytes 417800 | tf_op jit(solution)/shard_map/ppermute | solution.py:253
  110.9 9.3 %collective-permute-start.14 = (f16[136,512]{1,0:T(8,128)(2,1)S(1)}, f16[136,512]{1,0:T(8,128)(2,1)S(1)}, u32[]{:S(2)}, u32[]{:S(2)}) collective-permute-start(f16[136,512]{1,0:T(8,128)(2,1)S(1)} %convert_element_type.160), channel_id=1, source_target_pairs={{0,60},{2,62},{4,0},{6,2},{8,4},{10,6},{12,8},{14,10},{16,12},{18,... | collective-permute-start | bytes 417800 | tf_op jit(solution)/shard_map/ppermute | solution.py:255
  120.9 8.5 %collective-permute-start.15 = (f16[136,512]{1,0:T(8,128)(2,1)S(1)}, f16[136,512]{1,0:T(8,128)(2,1)S(1)}, u32[]{:S(2)}, u32[]{:S(2)}) collective-permute-start(f16[136,512]{1,0:T(8,128)(2,1)S(1)} %convert_element_type.162), channel_id=1, source_target_pairs={{0,4},{2,6},{4,8},{6,10},{8,12},{10,14},{12,16},{14,18},{16,20},{1... | collective-permute-start | bytes 417800 | tf_op jit(solution)/shard_map/ppermute | solution.py:253
  124.9 7.4 %collective-permute-start.16 = (f16[136,512]{1,0:T(8,128)(2,1)S(1)}, f16[136,512]{1,0:T(8,128)(2,1)S(1)}, u32[]{:S(2)}, u32[]{:S(2)}) collective-permute-start(f16[136,512]{1,0:T(8,128)(2,1)S(1)} %convert_element_type.164), channel_id=1, source_target_pairs={{0,60},{2,62},{4,0},{6,2},{8,4},{10,6},{12,8},{14,10},{16,12},{18,... | collective-permute-start | bytes 417800 | tf_op jit(solution)/shard_map/ppermute | solution.py:255
  133.0 7.4 %collective-permute-start.17 = (f16[136,512]{1,0:T(8,128)(2,1)S(1)}, f16[136,512]{1,0:T(8,128)(2,1)S(1)}, u32[]{:S(2)}, u32[]{:S(2)}) collective-permute-start(f16[136,512]{1,0:T(8,128)(2,1)S(1)} %convert_element_type.166), channel_id=1, source_target_pairs={{0,4},{2,6},{4,8},{6,10},{8,12},{10,14},{12,16},{14,18},{16,20},{1... | collective-permute-start | bytes 417800 | tf_op jit(solution)/shard_map/ppermute | solution.py:253
  136.9 6.4 %collective-permute-start.18 = (f16[136,512]{1,0:T(8,128)(2,1)S(1)}, f16[136,512]{1,0:T(8,128)(2,1)S(1)}, u32[]{:S(2)}, u32[]{:S(2)}) collective-permute-start(f16[136,512]{1,0:T(8,128)(2,1)S(1)} %convert_element_type.168), channel_id=1, source_target_pairs={{0,60},{2,62},{4,0},{6,2},{8,4},{10,6},{12,8},{14,10},{16,12},{18,... | collective-permute-start | bytes 417800 | tf_op jit(solution)/shard_map/ppermute | solution.py:255
  144.0 7.4 %collective-permute-start.19 = (f16[136,512]{1,0:T(8,128)(2,1)S(1)}, f16[136,512]{1,0:T(8,128)(2,1)S(1)}, u32[]{:S(2)}, u32[]{:S(2)}) collective-permute-start(f16[136,512]{1,0:T(8,128)(2,1)S(1)} %convert_element_type.170), channel_id=1, source_target_pairs={{0,4},{2,6},{4,8},{6,10},{8,12},{10,14},{12,16},{14,18},{16,20},{1... | collective-permute-start | bytes 417800 | tf_op jit(solution)/shard_map/ppermute | solution.py:253
  148.8 7.5 %collective-permute-start.20 = (f16[136,512]{1,0:T(8,128)(2,1)S(1)}, f16[136,512]{1,0:T(8,128)(2,1)S(1)}, u32[]{:S(2)}, u32[]{:S(2)}) collective-permute-start(f16[136,512]{1,0:T(8,128)(2,1)S(1)} %convert_element_type.172), channel_id=1, source_target_pairs={{0,60},{2,62},{4,0},{6,2},{8,4},{10,6},{12,8},{14,10},{16,12},{18,... | collective-permute-start | bytes 417800 | tf_op jit(solution)/shard_map/ppermute | solution.py:255
  157.1 8.8 %collective-permute-start.21 = (f16[136,512]{1,0:T(8,128)(2,1)S(1)}, f16[136,512]{1,0:T(8,128)(2,1)S(1)}, u32[]{:S(2)}, u32[]{:S(2)}) collective-permute-start(f16[136,512]{1,0:T(8,128)(2,1)S(1)} %convert_element_type.174), channel_id=1, source_target_pairs={{0,4},{2,6},{4,8},{6,10},{8,12},{10,14},{12,16},{14,18},{16,20},{1... | collective-permute-start | bytes 417800 | tf_op jit(solution)/shard_map/ppermute | solution.py:253
  159.9 7.6 %collective-permute-start.22 = (f16[136,512]{1,0:T(8,128)(2,1)S(1)}, f16[136,512]{1,0:T(8,128)(2,1)S(1)}, u32[]{:S(2)}, u32[]{:S(2)}) collective-permute-start(f16[136,512]{1,0:T(8,128)(2,1)S(1)} %convert_element_type.176), channel_id=1, source_target_pairs={{0,60},{2,62},{4,0},{6,2},{8,4},{10,6},{12,8},{14,10},{16,12},{18,... | collective-permute-start | bytes 417800 | tf_op jit(solution)/shard_map/ppermute | solution.py:255
  168.3 8.0 %collective-permute-start.23 = (f16[136,512]{1,0:T(8,128)(2,1)S(1)}, f16[136,512]{1,0:T(8,128)(2,1)S(1)}, u32[]{:S(2)}, u32[]{:S(2)}) collective-permute-start(f16[136,512]{1,0:T(8,128)(2,1)S(1)} %convert_element_type.178), channel_id=1, source_target_pairs={{0,4},{2,6},{4,8},{6,10},{8,12},{10,14},{12,16},{14,18},{16,20},{1... | collective-permute-start | bytes 417800 | tf_op jit(solution)/shard_map/ppermute | solution.py:253
  180.5 7.3 %collective-permute-start.25 = (f16[136,512]{1,0:T(8,128)(2,1)S(1)}, f16[136,512]{1,0:T(8,128)(2,1)S(1)}, u32[]{:S(2)}, u32[]{:S(2)}) collective-permute-start(f16[136,512]{1,0:T(8,128)(2,1)S(1)} %convert_element_type.182), channel_id=1, source_target_pairs={{0,4},{2,6},{4,8},{6,10},{8,12},{10,14},{12,16},{14,18},{16,20},{1... | collective-permute-start | bytes 417800 | tf_op jit(solution)/shard_map/ppermute | solution.py:253
  191.3 7.3 %collective-permute-start.27 = (f16[136,512]{1,0:T(8,128)(2,1)S(1)}, f16[136,512]{1,0:T(8,128)(2,1)S(1)}, u32[]{:S(2)}, u32[]{:S(2)}) collective-permute-start(f16[136,512]{1,0:T(8,128)(2,1)S(1)} %convert_element_type.186), channel_id=1, source_target_pairs={{0,4},{2,6},{4,8},{6,10},{8,12},{10,14},{12,16},{14,18},{16,20},{1... | collective-permute-start | bytes 417800 | tf_op jit(solution)/shard_map/ppermute | solution.py:253
  223.0 8.3 %collective-permute-start.1 = (f32[2,16,16]{2,1,0:T(8,128)}, f32[2,16,16]{2,1,0:T(8,128)}, u32[]{:S(2)}, u32[]{:S(2)}) collective-permute-start(f32[2,16,16]{2,1,0:T(8,128)} %pad_maximum_fusion), channel_id=1, source_target_pairs={{0,2},{2,0},{4,6},{6,4},{8,10},{10,8},{12,14},{14,12},{16,18},{18,... | collective-permute-start | bytes 6152 | tf_op jit(solution)/shard_map/ppermute | solution.py:297
  236.9 7.7 %collective-permute-start.5 = (f32[2,4,16]{2,1,0:T(4,128)S(1)}, f32[2,4,16]{2,1,0:T(4,128)S(1)}, u32[]{:S(2)}, u32[]{:S(2)}) collective-permute-start(f32[2,4,16]{2,1,0:T(4,128)S(1)} %pad_maximum_fusion.2), channel_id=1, source_target_pairs={{0,8},{2,10},{4,12},{6,14},{8,0},{10,2},{12,4},{14,6},{16,24},{18,... | collective-permute-start | bytes 1544 | tf_op jit(solution)/shard_map/ppermute | solution.py:297
  242.0 15.2 %collective-permute-start.2 = (f32[16,16,128]{2,1,0:T(8,128)S(1)}, f32[16,16,128]{2,1,0:T(8,128)S(1)}, u32[]{:S(2)}, u32[]{:S(2)}) collective-permute-start(f32[16,16,128]{2,1,0:T(8,128)S(1)} %constant_dynamic-slice_fusion.22), channel_id=1, source_target_pairs={{0,2},{2,0},{4,6},{6,4},{8,10},{10,8},{12,14},{14,12},{16,18},{18,... | collective-permute-start | bytes 393224 | tf_op jit(solution)/shard_map/ppermute | solution.py:296
  244.7 12.4 %collective-permute-start.7 = (f32[2,2,16]{2,1,0:T(2,128)S(1)}, f32[2,2,16]{2,1,0:T(2,128)S(1)}, u32[]{:S(2)}, u32[]{:S(2)}) collective-permute-start(f32[2,2,16]{2,1,0:T(2,128)S(1)} %pad_maximum_fusion.3), channel_id=1, source_target_pairs={{0,16},{2,18},{4,20},{6,22},{8,24},{10,26},{12,28},{14,30},{16,0},... | collective-permute-start | bytes 776 | tf_op jit(solution)/shard_map/ppermute | solution.py:297
  262.8 8.2 %collective-permute-start.6 = (f32[4,16,128]{2,1,0:T(8,128)S(1)}, f32[4,16,128]{2,1,0:T(8,128)S(1)}, u32[]{:S(2)}, u32[]{:S(2)}) collective-permute-start(f32[4,16,128]{2,1,0:T(8,128)S(1)} %constant_dynamic-slice_fusion.12), channel_id=1, source_target_pairs={{0,8},{2,10},{4,12},{6,14},{8,0},{10,2},{12,4},{14,6},{16,24},{18,... | collective-permute-start | bytes 98312 | tf_op jit(solution)/shard_map/ppermute | solution.py:296
  271.1 14.8 %collective-permute-start.8 = (f32[2,16,128]{2,1,0:T(8,128)S(1)}, f32[2,16,128]{2,1,0:T(8,128)S(1)}, u32[]{:S(2)}, u32[]{:S(2)}) collective-permute-start(f32[2,16,128]{2,1,0:T(8,128)S(1)} %constant_dynamic-slice_fusion.7), channel_id=1, source_target_pairs={{0,16},{2,18},{4,20},{6,22},{8,24},{10,26},{12,28},{14,30},{16,0},... | collective-permute-start | bytes 49160 | tf_op jit(solution)/shard_map/ppermute | solution.py:296
  280.6 21.9 %collective-permute-start.9 = (f32[2,1,16]{2,1,0:T(1,128)S(1)}, f32[2,1,16]{2,1,0:T(1,128)S(1)}, u32[]{:S(2)}, u32[]{:S(2)}) collective-permute-start(f32[2,1,16]{2,1,0:T(1,128)S(1)} %pad_maximum_fusion.4), channel_id=1, source_target_pairs={{0,32},{2,34},{4,36},{6,38},{8,40},{10,42},{12,44},{14,46},{16,48}... | collective-permute-start | bytes 392 | tf_op jit(solution)/shard_map/ppermute | solution.py:297
  286.0 22.1 %collective-permute-start.10 = (f32[1,16,128]{2,1,0:T(8,128)S(1)}, f32[1,16,128]{2,1,0:T(8,128)S(1)}, u32[]{:S(2)}, u32[]{:S(2)}) collective-permute-start(f32[1,16,128]{2,1,0:T(8,128)S(1)} %constant_dynamic-slice_fusion.1), channel_id=1, source_target_pairs={{0,32},{2,34},{4,36},{6,38},{8,40},{10,42},{12,44},{14,46},{16,48}... | collective-permute-start | bytes 24584 | tf_op jit(solution)/shard_map/ppermute | solution.py:296
  (26 other events, 603.8 us)

commit v5 on v2

--- a/solution.py
+++ b/solution.py
@@ -73,7 +73,7 @@
     up_wrapped, down_wrapped = flags[4] == 1, flags[5] == 1
     up_rate, down_rate = rates[:, up_at], rates[:, down_at]
 
-    @pl.loop(0, count)
+    @pl.loop(0, count, unroll=True)
     def _(p):
         here = pl.ds(pl.multiple_of(p * state, state), state)
         there = pl.ds(pl.multiple_of(rows + p * state, state), state)
@@ -120,7 +120,7 @@
     up_wrapped, down_wrapped = flags[4] == 1, flags[5] == 1
     rate = rates[:, at]
 
-    @pl.loop(0, count)
+    @pl.loop(0, count, unroll=True)
     def _(p):
         here = pl.ds(pl.multiple_of(p * state, state), state)
         there = pl.ds(pl.multiple_of(rows + p * state, state), state)
@@ -344,12 +344,13 @@
 
     peer_moved = swapped(moved)
     flat = (block_len, local_prompts, kv_heads * kv_width)
-    picked = jnp.einsum(
+    own_picked = jnp.einsum(
         "rp,ipx->rix",
         own_match.astype(jnp.bfloat16),
         moved.reshape(flat),
         preferred_element_type=jnp.float32,
-    ) + jnp.einsum(
+    )
+    picked = own_picked + jnp.einsum(
         "rp,ipx->rix",
         peer_match.astype(jnp.bfloat16),
         peer_moved.reshape(flat),

time: 266 us -> 265 us (level)
  transfers between devices with their start and end apart: 21 -> 21, of which waited for: 18 -> 18; matrix products, arithmetic and copies ran while one was open for 11% -> 11% of each run, Pallas kernels for 4% -> 3%
where the time goes in v5:
time: 265 us; the launch traced here: 264 us
  waiting for transfers between devices  132 us (50%)
  starting transfers between devices  84 us (32%)
  local copies, waits for them, and re-layouts  18.7 us (7%)
  other arithmetic  12.4 us (5%)
  Pallas kernels  9.14 us (3%)
  matrix products  6.7 us (3%)
    ppermute x1, waiting for transfers between devices, local(): came_state = lax.ppermute(sent_state.astype(jnp.float16), 'seq', pairs)  62.9 us
    all_to_all x1, starting transfers between devices, local(): lax.all_to_all(jnp.swapaxes(prompt_cache, 0, 1), 'seq', split_axis=0, con...  32.7 us
    ppermute x8, starting transfers between devices, hand_over(): sent = lax.ppermute(outs[0].astype(jnp.float16), 'seq', ahead)  28.6 us
    all_to_all x1, waiting for transfers between devices, local(): lax.all_to_all(jnp.concatenate([sums, extra], axis=1).astype(jnp.float16)...  23.7 us
    ppermute x8, waiting for transfers between devices, hand_over(): sent = lax.ppermute(outs[0].astype(jnp.float16), 'seq', ahead)  21.9 us
    ppermute x7, waiting for transfers between devices, hand_over(): down = lax.ppermute(outs[1].astype(jnp.float16), 'seq', behind)  20.5 us
    all_to_all x1, starting transfers between devices, local(): lax.all_to_all(jnp.concatenate([sums, extra], axis=1).astype(jnp.float16)...  15.5 us
    unnamed x67, local copies, waits for them, and re-layouts  7.94 us
  transfers between devices with their start and end apart: 21, of which 18 were waited for; matrix products, arithmetic and copies ran while one was open for 11% of the time, Pallas kernels for 3%

profile of v5, /device:TPU:46, one launch (start us, length us, event | category | flops | bytes accessed | tf_op | source)
XLA Modules:
  0.0 264.3 jit_solution(7898886695355143454)
XLA Ops:
  2.6 32.7 %all-to-all-start = ((bf16[32,4,8,256]{3,2,1,0:T(8,128)(2,1)}), bf16[32,4,8,256]{3,2,1,0:T(8,128)(2,1)}, u32[]{:S(2)}, u32[]{:S(2)}) async-start(bf16[32,4,8,256]{3,2,1,0:T(8,128)(2,1)} %bitcast.98), calls=%async_computation | async-start | bytes 1048576 | tf_op jit(solution)/shard_map/all_to_all | solution.py:330
  42.2 62.9 %collective-permute-done.1 = f16[4,16,8192]{2,1,0:T(8,128)(2,1)S(1)} collective-permute-done((f16[4,16,8192]{2,1,0:T(8,128)(2,1)}, f16[4,16,8192]{2,1,0:T(8,128)(2,1)S(1)}, u32[]{:S(2)}, u32[]{:S(2)}) %collective-permute-start.1) | collective-permute-done | bytes 1048608 | tf_op jit(solution)/shard_map/ppermute | solution.py:328
  112.9 2.6 collective-permute-start.3
  117.4 3.3 %collective-permute-done.3 = f16[136,512]{1,0:T(8,128)(2,1)S(1)} collective-permute-done((f16[136,512]{1,0:T(8,128)(2,1)S(1)}, f16[136,512]{1,0:T(8,128)(2,1)S(1)}, u32[]{:S(2)}, u32[]{:S(2)}) %collective-permute-start.3) | collective-permute-done | bytes 139296 | tf_op jit(solution)/shard_map/ppermute | solution.py:249
  120.6 4.1 %collective-permute-done.4 = f16[136,512]{1,0:T(8,128)(2,1)S(1)} collective-permute-done((f16[136,512]{1,0:T(8,128)(2,1)S(1)}, f16[136,512]{1,0:T(8,128)(2,1)S(1)}, u32[]{:S(2)}, u32[]{:S(2)}) %collective-permute-start.4) | collective-permute-done | bytes 139296 | tf_op jit(solution)/shard_map/ppermute | solution.py:251
  125.5 3.9 %collective-permute-start.5 = (f16[136,512]{1,0:T(8,128)(2,1)S(1)}, f16[136,512]{1,0:T(8,128)(2,1)S(1)}, u32[]{:S(2)}, u32[]{:S(2)}) collective-permute-start(f16[136,512]{1,0:T(8,128)(2,1)S(1)} %convert_element_type.174), channel_id=1, source_target_pairs={{0,4},{2,6},{4,8},{6,10},{8,12},{10,14},{12,16},{14,18},{16,20},{1... | collective-permute-start | bytes 417800 | tf_op jit(solution)/shard_map/ppermute | solution.py:249
  130.0 4.0 %collective-permute-done.5 = f16[136,512]{1,0:T(8,128)(2,1)S(1)} collective-permute-done((f16[136,512]{1,0:T(8,128)(2,1)S(1)}, f16[136,512]{1,0:T(8,128)(2,1)S(1)}, u32[]{:S(2)}, u32[]{:S(2)}) %collective-permute-start.5) | collective-permute-done | bytes 139296 | tf_op jit(solution)/shard_map/ppermute | solution.py:249
  134.0 2.9 %collective-permute-done.6 = f16[136,512]{1,0:T(8,128)(2,1)S(1)} collective-permute-done((f16[136,512]{1,0:T(8,128)(2,1)S(1)}, f16[136,512]{1,0:T(8,128)(2,1)S(1)}, u32[]{:S(2)}, u32[]{:S(2)}) %collective-permute-start.6) | collective-permute-done | bytes 139296 | tf_op jit(solution)/shard_map/ppermute | solution.py:251
  137.6 3.9 %collective-permute-start.7 = (f16[136,512]{1,0:T(8,128)(2,1)S(1)}, f16[136,512]{1,0:T(8,128)(2,1)S(1)}, u32[]{:S(2)}, u32[]{:S(2)}) collective-permute-start(f16[136,512]{1,0:T(8,128)(2,1)S(1)} %convert_element_type.178), channel_id=1, source_target_pairs={{0,4},{2,6},{4,8},{6,10},{8,12},{10,14},{12,16},{14,18},{16,20},{1... | collective-permute-start | bytes 417800 | tf_op jit(solution)/shard_map/ppermute | solution.py:249
  142.1 3.0 %collective-permute-done.7 = f16[136,512]{1,0:T(8,128)(2,1)S(1)} collective-permute-done((f16[136,512]{1,0:T(8,128)(2,1)S(1)}, f16[136,512]{1,0:T(8,128)(2,1)S(1)}, u32[]{:S(2)}, u32[]{:S(2)}) %collective-permute-start.7) | collective-permute-done | bytes 139296 | tf_op jit(solution)/shard_map/ppermute | solution.py:249
  145.1 2.8 %collective-permute-done.8 = f16[136,512]{1,0:T(8,128)(2,1)S(1)} collective-permute-done((f16[136,512]{1,0:T(8,128)(2,1)S(1)}, f16[136,512]{1,0:T(8,128)(2,1)S(1)}, u32[]{:S(2)}, u32[]{:S(2)}) %collective-permute-start.8) | collective-permute-done | bytes 139296 | tf_op jit(solution)/shard_map/ppermute | solution.py:251
  148.7 4.8 %collective-permute-start.9 = (f16[136,512]{1,0:T(8,128)(2,1)S(1)}, f16[136,512]{1,0:T(8,128)(2,1)S(1)}, u32[]{:S(2)}, u32[]{:S(2)}) collective-permute-start(f16[136,512]{1,0:T(8,128)(2,1)S(1)} %convert_element_type.182), channel_id=1, source_target_pairs={{0,4},{2,6},{4,8},{6,10},{8,12},{10,14},{12,16},{14,18},{16,20},{1... | collective-permute-start | bytes 417800 | tf_op jit(solution)/shard_map/ppermute | solution.py:249
  156.1 5.0 %collective-permute-done.10 = f16[136,512]{1,0:T(8,128)(2,1)S(1)} collective-permute-done((f16[136,512]{1,0:T(8,128)(2,1)S(1)}, f16[136,512]{1,0:T(8,128)(2,1)S(1)}, u32[]{:S(2)}, u32[]{:S(2)}) %collective-permute-start.10) | collective-permute-done | bytes 139296 | tf_op jit(solution)/shard_map/ppermute | solution.py:251
  161.8 2.7 %collective-permute-start.11 = (f16[136,512]{1,0:T(8,128)(2,1)S(1)}, f16[136,512]{1,0:T(8,128)(2,1)S(1)}, u32[]{:S(2)}, u32[]{:S(2)}) collective-permute-start(f16[136,512]{1,0:T(8,128)(2,1)S(1)} %convert_element_type.186), channel_id=1, source_target_pairs={{0,4},{2,6},{4,8},{6,10},{8,12},{10,14},{12,16},{14,18},{16,20},{1... | collective-permute-start | bytes 417800 | tf_op jit(solution)/shard_map/ppermute | solution.py:249
  166.4 4.1 %collective-permute-done.11 = f16[136,512]{1,0:T(8,128)(2,1)S(1)} collective-permute-done((f16[136,512]{1,0:T(8,128)(2,1)S(1)}, f16[136,512]{1,0:T(8,128)(2,1)S(1)}, u32[]{:S(2)}, u32[]{:S(2)}) %collective-permute-start.11) | collective-permute-done | bytes 139296 | tf_op jit(solution)/shard_map/ppermute | solution.py:249
  172.9 4.3 %collective-permute-start.13 = (f16[136,512]{1,0:T(8,128)(2,1)S(1)}, f16[136,512]{1,0:T(8,128)(2,1)S(1)}, u32[]{:S(2)}, u32[]{:S(2)}) collective-permute-start(f16[136,512]{1,0:T(8,128)(2,1)S(1)} %convert_element_type.190), channel_id=1, source_target_pairs={{0,4},{2,6},{4,8},{6,10},{8,12},{10,14},{12,16},{14,18},{16,20},{1... | collective-permute-start | bytes 417800 | tf_op jit(solution)/shard_map/ppermute | solution.py:249
  177.6 4.2 %collective-permute-done.13 = f16[136,512]{1,0:T(8,128)(2,1)S(1)} collective-permute-done((f16[136,512]{1,0:T(8,128)(2,1)S(1)}, f16[136,512]{1,0:T(8,128)(2,1)S(1)}, u32[]{:S(2)}, u32[]{:S(2)}) %collective-permute-start.13) | collective-permute-done | bytes 139296 | tf_op jit(solution)/shard_map/ppermute | solution.py:249
  184.1 4.0 %collective-permute-start.15 = (f16[136,512]{1,0:T(8,128)(2,1)S(1)}, f16[136,512]{1,0:T(8,128)(2,1)S(1)}, u32[]{:S(2)}, u32[]{:S(2)}) collective-permute-start(f16[136,512]{1,0:T(8,128)(2,1)S(1)} %convert_element_type.194), channel_id=1, source_target_pairs={{0,4},{2,6},{4,8},{6,10},{8,12},{10,14},{12,16},{14,18},{16,20},{1... | collective-permute-start | bytes 417800 | tf_op jit(solution)/shard_map/ppermute | solution.py:249
  191.4 2.8 %collective-permute-done.16 = f16[136,512]{1,0:T(8,128)(2,1)S(1)} collective-permute-done((f16[136,512]{1,0:T(8,128)(2,1)S(1)}, f16[136,512]{1,0:T(8,128)(2,1)S(1)}, u32[]{:S(2)}, u32[]{:S(2)}) %collective-permute-start.16) | collective-permute-done | bytes 139296 | tf_op jit(solution)/shard_map/ppermute | solution.py:251
  194.8 2.4 collective-permute-start.17
  199.5 2.9 %fusion.30 = f32[8,32,2048]{2,0,1:T(8,128)} fusion(bf16[32,4,2048]{2,1,0:T(4,128)(2,1)} %reshape.278, pred[8,4]{0,1:T(4,128)(4,1)S(1)} %get-tuple-element.55), kind=kOutput, calls=%fused_computation.67 | convolution fusion | flops 4194304 | bytes 2621472 | tf_op jit(solution)/shard_map/rp,ipx->rix/dot_general | solution.py:347
  204.6 2.4 fusion
  212.5 15.5 %all-to-all-start.1 = ((f16[32,17,128]{2,1,0:T(8,128)(2,1)}), f16[32,17,128]{2,1,0:T(8,128)(2,1)S(1)}, u32[]{:S(2)}, u32[]{:S(2)}) async-start(f16[32,17,128]{2,1,0:T(8,128)(2,1)} %copy.61), calls=%async_computation.1 | async-start | bytes 393216 | tf_op jit(solution)/shard_map/all_to_all | solution.py:394
  238.5 23.7 %all-to-all-done.1 = f16[32,17,128]{2,1,0:T(8,128)(2,1)S(1)} async-done(((f16[32,17,128]{2,1,0:T(8,128)(2,1)}), f16[32,17,128]{2,1,0:T(8,128)(2,1)S(1)}, u32[]{:S(2)}, u32[]{:S(2)}) %all-to-all-start.1) | async-done | bytes 139296 | tf_op jit(solution)/shard_map/all_to_all | solution.py:394
  (181 shorter events, 58.3 us)
Async XLA Ops:
  0.6 207.8 %copy-start = (bf16[8,64,128]{2,1,0:T(8,128)(2,1)S(1)}, bf16[8,64,128]{2,1,0:T(8,128)(2,1)}, u32[]{:S(2)}) copy-start(bf16[8,64,128]{2,1,0:T(8,128)(2,1)} %param.25) | copy-start | bytes 393220
  0.6 34.7 %copy-start.8 = (f32[4,1,16384]{2,1,0:T(1,128)S(1)}, f32[4,1,16384]{2,1,0:T(1,128)}, u32[]{:S(2)}) copy-start(f32[4,1,16384]{2,1,0:T(1,128)} %param.19) | copy-start | bytes 786436
  0.7 34.8 %copy-start.25 = (s32[8]{0:T(128)S(1)}, s32[8]{0:T(128)}, u32[]{:S(2)}) copy-start(s32[8]{0:T(128)} %param.20) | copy-start | bytes 100
  2.6 185.9 %all-to-all-start = ((bf16[32,4,8,256]{3,2,1,0:T(8,128)(2,1)}), bf16[32,4,8,256]{3,2,1,0:T(8,128)(2,1)}, u32[]{:S(2)}, u32[]{:S(2)}) async-start(bf16[32,4,8,256]{3,2,1,0:T(8,128)(2,1)} %bitcast.98), calls=%async_computation | async-start | bytes 1048576 | tf_op jit(solution)/shard_map/all_to_all | solution.py:330
  40.0 65.1 %collective-permute-start.1 = (f16[4,16,8192]{2,1,0:T(8,128)(2,1)}, f16[4,16,8192]{2,1,0:T(8,128)(2,1)S(1)}, u32[]{:S(2)}, u32[]{:S(2)}) collective-permute-start(f16[4,16,8192]{2,1,0:T(8,128)(2,1)} %convert_element_type.168), channel_id=1, source_target_pairs={{0,2},{2,0},{4,6},{6,4},{8,10},{10,8},{12,14},{14,12},{16,18},{18,... | collective-permute-start | bytes 3145736 | tf_op jit(solution)/shard_map/ppermute | solution.py:328
  41.4 65.6 %collective-permute-start.2 = (f32[4,8192]{1,0:T(4,128)S(1)}, f32[4,8192]{1,0:T(4,128)S(1)}, u32[]{:S(2)}, u32[]{:S(2)}) collective-permute-start(f32[4,8192]{1,0:T(4,128)S(1)} %get-tuple-element.24), channel_id=1, source_target_pairs={{0,2},{2,0},{4,6},{6,4},{8,10},{10,8},{12,14},{14,12},{16,18},{18,... | collective-permute-start | bytes 393224 | tf_op jit(solution)/shard_map/ppermute | solution.py:329
  112.9 7.7 %collective-permute-start.3 = (f16[136,512]{1,0:T(8,128)(2,1)S(1)}, f16[136,512]{1,0:T(8,128)(2,1)S(1)}, u32[]{:S(2)}, u32[]{:S(2)}) collective-permute-start(f16[136,512]{1,0:T(8,128)(2,1)S(1)} %convert_element_type.170), channel_id=1, source_target_pairs={{0,4},{2,6},{4,8},{6,10},{8,12},{10,14},{12,16},{14,18},{16,20},{1... | collective-permute-start | bytes 417800 | tf_op jit(solution)/shard_map/ppermute | solution.py:249
  115.5 9.3 %collective-permute-start.4 = (f16[136,512]{1,0:T(8,128)(2,1)S(1)}, f16[136,512]{1,0:T(8,128)(2,1)S(1)}, u32[]{:S(2)}, u32[]{:S(2)}) collective-permute-start(f16[136,512]{1,0:T(8,128)(2,1)S(1)} %convert_element_type.172), channel_id=1, source_target_pairs={{0,60},{2,62},{4,0},{6,2},{8,4},{10,6},{12,8},{14,10},{16,12},{18,... | collective-permute-start | bytes 417800 | tf_op jit(solution)/shard_map/ppermute | solution.py:251
  125.5 8.5 %collective-permute-start.5 = (f16[136,512]{1,0:T(8,128)(2,1)S(1)}, f16[136,512]{1,0:T(8,128)(2,1)S(1)}, u32[]{:S(2)}, u32[]{:S(2)}) collective-permute-start(f16[136,512]{1,0:T(8,128)(2,1)S(1)} %convert_element_type.174), channel_id=1, source_target_pairs={{0,4},{2,6},{4,8},{6,10},{8,12},{10,14},{12,16},{14,18},{16,20},{1... | collective-permute-start | bytes 417800 | tf_op jit(solution)/shard_map/ppermute | solution.py:249
  129.5 7.4 %collective-permute-start.6 = (f16[136,512]{1,0:T(8,128)(2,1)S(1)}, f16[136,512]{1,0:T(8,128)(2,1)S(1)}, u32[]{:S(2)}, u32[]{:S(2)}) collective-permute-start(f16[136,512]{1,0:T(8,128)(2,1)S(1)} %convert_element_type.176), channel_id=1, source_target_pairs={{0,60},{2,62},{4,0},{6,2},{8,4},{10,6},{12,8},{14,10},{16,12},{18,... | collective-permute-start | bytes 417800 | tf_op jit(solution)/shard_map/ppermute | solution.py:251
  137.6 7.5 %collective-permute-start.7 = (f16[136,512]{1,0:T(8,128)(2,1)S(1)}, f16[136,512]{1,0:T(8,128)(2,1)S(1)}, u32[]{:S(2)}, u32[]{:S(2)}) collective-permute-start(f16[136,512]{1,0:T(8,128)(2,1)S(1)} %convert_element_type.178), channel_id=1, source_target_pairs={{0,4},{2,6},{4,8},{6,10},{8,12},{10,14},{12,16},{14,18},{16,20},{1... | collective-permute-start | bytes 417800 | tf_op jit(solution)/shard_map/ppermute | solution.py:249
  141.5 6.4 %collective-permute-start.8 = (f16[136,512]{1,0:T(8,128)(2,1)S(1)}, f16[136,512]{1,0:T(8,128)(2,1)S(1)}, u32[]{:S(2)}, u32[]{:S(2)}) collective-permute-start(f16[136,512]{1,0:T(8,128)(2,1)S(1)} %convert_element_type.180), channel_id=1, source_target_pairs={{0,60},{2,62},{4,0},{6,2},{8,4},{10,6},{12,8},{14,10},{16,12},{18,... | collective-permute-start | bytes 417800 | tf_op jit(solution)/shard_map/ppermute | solution.py:251
  148.7 7.4 %collective-permute-start.9 = (f16[136,512]{1,0:T(8,128)(2,1)S(1)}, f16[136,512]{1,0:T(8,128)(2,1)S(1)}, u32[]{:S(2)}, u32[]{:S(2)}) collective-permute-start(f16[136,512]{1,0:T(8,128)(2,1)S(1)} %convert_element_type.182), channel_id=1, source_target_pairs={{0,4},{2,6},{4,8},{6,10},{8,12},{10,14},{12,16},{14,18},{16,20},{1... | collective-permute-start | bytes 417800 | tf_op jit(solution)/shard_map/ppermute | solution.py:249
  153.5 7.6 %collective-permute-start.10 = (f16[136,512]{1,0:T(8,128)(2,1)S(1)}, f16[136,512]{1,0:T(8,128)(2,1)S(1)}, u32[]{:S(2)}, u32[]{:S(2)}) collective-permute-start(f16[136,512]{1,0:T(8,128)(2,1)S(1)} %convert_element_type.184), channel_id=1, source_target_pairs={{0,60},{2,62},{4,0},{6,2},{8,4},{10,6},{12,8},{14,10},{16,12},{18,... | collective-permute-start | bytes 417800 | tf_op jit(solution)/shard_map/ppermute | solution.py:251
  161.8 8.8 %collective-permute-start.11 = (f16[136,512]{1,0:T(8,128)(2,1)S(1)}, f16[136,512]{1,0:T(8,128)(2,1)S(1)}, u32[]{:S(2)}, u32[]{:S(2)}) collective-permute-start(f16[136,512]{1,0:T(8,128)(2,1)S(1)} %convert_element_type.186), channel_id=1, source_target_pairs={{0,4},{2,6},{4,8},{6,10},{8,12},{10,14},{12,16},{14,18},{16,20},{1... | collective-permute-start | bytes 417800 | tf_op jit(solution)/shard_map/ppermute | solution.py:249
  164.6 7.6 %collective-permute-start.12 = (f16[136,512]{1,0:T(8,128)(2,1)S(1)}, f16[136,512]{1,0:T(8,128)(2,1)S(1)}, u32[]{:S(2)}, u32[]{:S(2)}) collective-permute-start(f16[136,512]{1,0:T(8,128)(2,1)S(1)} %convert_element_type.188), channel_id=1, source_target_pairs={{0,60},{2,62},{4,0},{6,2},{8,4},{10,6},{12,8},{14,10},{16,12},{18,... | collective-permute-start | bytes 417800 | tf_op jit(solution)/shard_map/ppermute | solution.py:251
  172.9 8.8 %collective-permute-start.13 = (f16[136,512]{1,0:T(8,128)(2,1)S(1)}, f16[136,512]{1,0:T(8,128)(2,1)S(1)}, u32[]{:S(2)}, u32[]{:S(2)}) collective-permute-start(f16[136,512]{1,0:T(8,128)(2,1)S(1)} %convert_element_type.190), channel_id=1, source_target_pairs={{0,4},{2,6},{4,8},{6,10},{8,12},{10,14},{12,16},{14,18},{16,20},{1... | collective-permute-start | bytes 417800 | tf_op jit(solution)/shard_map/ppermute | solution.py:249
  177.2 6.1 %collective-permute-start.14 = (f16[136,512]{1,0:T(8,128)(2,1)S(1)}, f16[136,512]{1,0:T(8,128)(2,1)S(1)}, u32[]{:S(2)}, u32[]{:S(2)}) collective-permute-start(f16[136,512]{1,0:T(8,128)(2,1)S(1)} %convert_element_type.192), channel_id=1, source_target_pairs={{0,60},{2,62},{4,0},{6,2},{8,4},{10,6},{12,8},{14,10},{16,12},{18,... | collective-permute-start | bytes 417800 | tf_op jit(solution)/shard_map/ppermute | solution.py:251
  184.1 7.3 %collective-permute-start.15 = (f16[136,512]{1,0:T(8,128)(2,1)S(1)}, f16[136,512]{1,0:T(8,128)(2,1)S(1)}, u32[]{:S(2)}, u32[]{:S(2)}) collective-permute-start(f16[136,512]{1,0:T(8,128)(2,1)S(1)} %convert_element_type.194), channel_id=1, source_target_pairs={{0,4},{2,6},{4,8},{6,10},{8,12},{10,14},{12,16},{14,18},{16,20},{1... | collective-permute-start | bytes 417800 | tf_op jit(solution)/shard_map/ppermute | solution.py:249
  188.1 6.1 %collective-permute-start.16 = (f16[136,512]{1,0:T(8,128)(2,1)S(1)}, f16[136,512]{1,0:T(8,128)(2,1)S(1)}, u32[]{:S(2)}, u32[]{:S(2)}) collective-permute-start(f16[136,512]{1,0:T(8,128)(2,1)S(1)} %convert_element_type.196), channel_id=1, source_target_pairs={{0,60},{2,62},{4,0},{6,2},{8,4},{10,6},{12,8},{14,10},{16,12},{18,... | collective-permute-start | bytes 417800 | tf_op jit(solution)/shard_map/ppermute | solution.py:251
  188.5 13.9 %collective-permute-start = (bf16[32,4,8,256]{3,2,1,0:T(8,128)(2,1)}, bf16[32,4,8,256]{3,2,1,0:T(8,128)(2,1)}, u32[]{:S(2)}, u32[]{:S(2)}) collective-permute-start(bf16[32,4,8,256]{3,2,1,0:T(8,128)(2,1)} %all-to-all-done), channel_id=1, source_target_pairs={{0,1},{1,0},{2,3},{3,2},{4,5},{5,4},{6,7},{7,6},{8,9},{9,8},{10,11... | collective-permute-start | bytes 1572872 | tf_op jit(solution)/shard_map/ppermute | solution.py:282
  194.8 37.2 %collective-permute-start.17 = (f16[136,512]{1,0:T(8,128)(2,1)S(1)}, f16[136,512]{1,0:T(8,128)(2,1)}, u32[]{:S(2)}, u32[]{:S(2)}) collective-permute-start(f16[136,512]{1,0:T(8,128)(2,1)S(1)} %convert_element_type.198), channel_id=1, source_target_pairs={{0,4},{2,6},{4,8},{6,10},{8,12},{10,14},{12,16},{14,18},{16,20},{1... | collective-permute-start | bytes 417800 | tf_op jit(solution)/shard_map/ppermute | solution.py:249
  212.5 49.8 %all-to-all-start.1 = ((f16[32,17,128]{2,1,0:T(8,128)(2,1)}), f16[32,17,128]{2,1,0:T(8,128)(2,1)S(1)}, u32[]{:S(2)}, u32[]{:S(2)}) async-start(f16[32,17,128]{2,1,0:T(8,128)(2,1)} %copy.61), calls=%async_computation.1 | async-start | bytes 393216 | tf_op jit(solution)/shard_map/all_to_all | solution.py:394
  233.8 1.5 collective-permute-start.18
  (29 other events, 98.9 us)
